TPU v7x, 128 devices: a whole 4x4x4 slice. The times are simulated.
128 devices in a mesh: gx: 4 (over x), gy: 4 (over z_hi, core), gz: 8 (over y, z_lo).
Axes of the slice: x: 4, y: 4, z: 4 (z_hi: 2, z_lo: 2; z = z_hi * 2 + z_lo), core: 2. Of those that a mesh axis runs over, the one named last changes fastest.
Arguments:
- amplitudes: bfloat16 [2, 65536, 2048], P(None, ('gx', 'gy', 'gz')), may hold values from -6 to 6
- pauli_x: int32 [200], replicated, may hold values from 0 to 2047, as said below
- pauli_z: int32 [200], replicated, may hold values from 0 to 2047
- pauli_phase: int32 [200], replicated, may hold values from 0 to 3
Outputs:
- density_real: float32 [2048, 2048], P(('gx', 'gy', 'gz'))
- density_imag: float32 [2048, 2048], P(('gx', 'gy', 'gz'))
- expectations: float32 [2, 200], replicated
Inputs may be any that keep to these rules, and one draw needn't show every extreme that they name: Bit q of the mask acts on kept qubit q (the bit of weight 2^q of the last index); pauli_x and pauli_z of a term are never both zero.
All inputs are finite; a program needn't handle non-finite values.
Results may differ from a plain program's by a relative error of at most 0.0003.
Values sent between devices are 32-bit elements; how exact they have to be, the bound alone decides.
No kernel may reach another device: no remote copies, remote signals or barrier semaphores. Data moves between devices by JAX's collectives and lax.ppermute only.
A program may use at most 192 MiB of HBM per device.

v0:
```python
import functools

import jax
import jax.numpy as jnp
from jax import lax
from jax.sharding import Mesh
from jax.sharding import PartitionSpec as P

QUBITS = 11
GY = ("gy_0", "gy_1")
GZ = ("gz_0", "gz_1")
GX_GY_GZ = ("gx", "gy_0", "gy_1", "gz_0", "gz_1")


def in_blocks(array, dim, peers):
    before, after = (array.shape[:dim], array.shape[dim + 1 :])
    return jnp.moveaxis(array.reshape(*before, peers, -1, *after), dim, 0)


def sent_and_summed(array, axis, dim):
    parts = in_blocks(array, dim, lax.axis_size(axis))
    arrived = lax.all_to_all(parts, axis, split_axis=0, concat_axis=0, tiled=True)
    return arrived.sum(axis=0)


def over_axes(array, axes):
    return functools.reduce(lax.psum, axes, array)


def parity_sign(values, masks):
    anded = jnp.bitwise_and(values, masks)
    counted = jnp.zeros_like(anded)
    for bit_index in range(QUBITS):
        counted = counted + jnp.bitwise_and(jnp.right_shift(anded, bit_index), 1)
    return (1 - 2 * jnp.bitwise_and(counted, 1)).astype(jnp.float32)


def phase_parts(pauli_phase):
    phase_real = jnp.where(pauli_phase == 0, 1.0, jnp.where(pauli_phase == 2, -1.0, 0.0)).astype(
        jnp.float32
    )
    phase_imag = jnp.where(pauli_phase == 1, 1.0, jnp.where(pauli_phase == 3, -1.0, 0.0)).astype(
        jnp.float32
    )
    return (phase_real, phase_imag)


def on_device(amplitudes, pauli_x, pauli_z, pauli_phase):
    real_part = amplitudes[0]
    imag_part = amplitudes[1]
    order = real_part.shape[1]
    stacked = jnp.concatenate([real_part, imag_part], 0)
    crossed = jnp.concatenate([imag_part, jnp.negative(real_part)], 0)
    dims = (((0,), (0,)), ((), ()))
    devices = lax.axis_size("gx") * lax.axis_size(GY) * lax.axis_size(GZ)
    own_count = order // devices
    real_rows = lax.dot_general(stacked, stacked, dims, preferred_element_type=jnp.float32)
    imag_rows = lax.dot_general(crossed, stacked, dims, preferred_element_type=jnp.float32)
    by_gx = lax.psum_scatter(
        jnp.concatenate([real_rows, imag_rows], 1), "gx", scatter_dimension=0, tiled=True
    )
    by_gy = lax.psum_scatter(by_gx, GY, scatter_dimension=0, tiled=True)
    summed = sent_and_summed(by_gy, GZ, 0)
    total_cols = amplitudes.shape[1] * devices
    density = summed / total_cols
    density_real = density[:, :order]
    density_imag = density[:, order:]
    first_row = lax.axis_index(GX_GY_GZ) * own_count
    owned_rows = (first_row + jnp.arange(own_count, dtype=jnp.int32))[:, None]
    partner = jnp.bitwise_xor(owned_rows, pauli_x[None, :])
    picked_real = jnp.take_along_axis(density_real, partner, axis=1)
    picked_imag = jnp.take_along_axis(density_imag, partner, axis=1)
    signs = parity_sign(owned_rows, pauli_z[None, :])
    phase_real, phase_imag = phase_parts(pauli_phase)
    sum_real = jnp.sum(signs * picked_real, axis=0)
    sum_imag = jnp.sum(signs * picked_imag, axis=0)
    local_real = phase_real * sum_real - phase_imag * sum_imag
    local_imag = phase_real * sum_imag + phase_imag * sum_real
    expectations = over_axes(jnp.stack([local_real, local_imag], 0), GX_GY_GZ)
    return (density_real, density_imag, expectations)


def solution(mesh):
    finer = Mesh(
        mesh.devices.reshape(mesh.shape["gx"], 2, 2, 4, 2), ("gx", "gy_0", "gy_1", "gz_0", "gz_1")
    )
    in_specs = (P(None, GX_GY_GZ, None), P(), P(), P())
    out_specs = (P(GX_GY_GZ, None), P(GX_GY_GZ, None), P())
    return jax.shard_map(
        on_device, mesh=finer, in_specs=in_specs, out_specs=out_specs, check_vma=False
    )
```

profile of v0, /device:TPU:8, one launch (start us, length us, event | category | flops | bytes accessed | tf_op | source)
XLA Modules:
  0.0 552.8 jit_solution(16060468333758578852)
XLA Ops:
  7.2 0.0 reduce-scatter.3.cloned.1.call-start
  7.2 0.0 copy-start.2
  7.2 1.9 fusion.37
  9.1 0.9 copy-done.2
  10.0 2.5 slice_bitcast_fusion.1
  12.5 12.8 %fusion.4 = f32[2048,2048]{0,1:T(8,128)S(1)} fusion(bf16[512,2048]{1,0:T(8,128)(2,1)} %get-tuple-element.7, bf16[512,2048]{1,0:T(8,128)(2,1)} %get-tuple-element.6), kind=kOutput, calls=%fused_computation.8 | convolution fusion | flops 8598323200 | bytes 20971520 | tf_op jit(solution)/shard_map/dot_general | solution.py:57
  25.3 14.8 %fusion = f32[2048,2048]{0,1:T(8,128)} fusion(bf16[512,2048]{1,0:T(8,128)(2,1)S(1)} %fusion.37, bf16[512,2048]{1,0:T(8,128)(2,1)} %get-tuple-element.7, bf16[512,2048]{1,0:T(8,128)(2,1)} %get-tuple-element.6), kind=kOutput, calls=%fused_computation.4 | convolution fusion | flops 8606711808 | bytes 23068672 | tf_op jit(solution)/shard_map/dot_general | solution.py:58
  40.0 18.9 %pad_maximum_fusion = f32[2048,4096]{0,1:T(8,128)} fusion(f32[2048,2048]{0,1:T(8,128)} %fusion, f32[2048,2048]{0,1:T(8,128)S(1)} %fusion.4), kind=kLoop, calls=%fused_computation.2 | loop fusion | flops 8388608 | bytes 67108864 | tf_op jit(solution)/shard_map/concatenate | solution.py:60
  58.9 0.0 reduce-scatter.3.cloned.1.call-update
  58.9 0.0 reduce-scatter.5.cloned.1.call-start
  59.0 285.1 %reduce-scatter.3.cloned.1.call-done = f32[512,4096]{0,1:T(8,128)} async-done(((f32[2048,4096]{0,1:T(8,128)}), f32[512,4096]{0,1:T(8,128)}) %reduce-scatter.3.cloned.1.call-update) | async-done | bytes 8388624 | tf_op jit(solution)/shard_map/reduce_scatter | solution.py:59
  344.1 0.0 reduce-scatter.5.cloned.1.call-update
  344.1 80.8 %reduce-scatter.5.cloned.1.call-done = f32[128,4096]{0,1:T(8,128)} async-done(((f32[512,4096]{0,1:T(8,128)}), f32[128,4096]{0,1:T(8,128)}) %reduce-scatter.5.cloned.1.call-update) | async-done | bytes 2097168 | tf_op jit(solution)/shard_map/reduce_scatter | solution.py:62
  424.9 2.9 copy.8
  427.8 0.0 copy-start.3
  427.8 5.0 all-to-all-start
  432.8 0.0 copy-done.3
  432.8 0.1 bitcast_or_fusion
  432.9 0.1 reshape.48
  433.0 28.0 %all-to-all-done = f32[8,16,4096]{2,1,0:T(8,128)S(1)} async-done(((f32[8,16,4096]{2,1,0:T(8,128)}), f32[8,16,4096]{2,1,0:T(8,128)S(1)}, u32[]{:S(2)}, u32[]{:S(2)}) %all-to-all-start) | async-done | bytes 2097184 | tf_op jit(solution)/shard_map/all_to_all | solution.py:22
  461.0 0.1 reduce_sum.27
  461.2 0.0 copy-start
  461.2 0.0 copy-start.1
  461.2 24.6 %gather_fusion.1 = f32[3200]{0:T(1024)S(1)} fusion(f32[16,2048]{1,0:T(8,128)S(1)} %get-tuple-element.8, s32[3200]{0:T(1024)S(1)} %reshape.48), kind=kCustom, calls=%fused_computation.1.clone | custom fusion | bytes 51200 | tf_op jit(solution)/shard_map/jit(take_along_axis)/gather | solution.py:72
  485.8 0.0 copy-done
  485.8 0.1 reshape.56
  485.9 0.0 copy-done.1
  485.9 0.0 copy-start.4
  485.9 0.0 copy-start.5
  485.9 24.6 %gather_fusion = f32[3200]{0:T(1024)S(1)} fusion(f32[16,2048]{1,0:T(8,128)S(1)} %get-tuple-element.9, s32[3200]{0:T(1024)S(1)} %reshape.48), kind=kCustom, calls=%fused_computation.clone | custom fusion | bytes 51200 | tf_op jit(solution)/shard_map/jit(take_along_axis)/gather | solution.py:71
  510.5 0.1 reshape.51
  510.6 0.0 copy-done.4
  510.6 0.1 fusion.30
  510.7 0.0 copy-done.5
  510.7 10.4 %psum.35 = f32[2,200]{1,0:T(2,128)S(1)} all-reduce(f32[2,200]{1,0:T(2,128)S(1)} %pad_maximum_fusion.4), channel_id=1, replica_groups=mesh['gx'=4,'gy_0'=2,'gy_1'=2,'gz_0'=4,'gz_1'=2] {'gx'}, use_global_device_ids=true, to_apply=%region_5.7 | all-reduce | flops 400 | bytes 3200 | tf_op jit(solution)/shard_map/psum | solution.py:27
  521.2 6.4 %psum.36 = f32[2,200]{1,0:T(2,128)S(1)} all-reduce(f32[2,200]{1,0:T(2,128)S(1)} %psum.35), channel_id=1, replica_groups=mesh['gx'=4,'gy_0'=2,'gy_1'=2,'gz_0'=4,'gz_1'=2] {'gy_0'}, use_global_device_ids=true, to_apply=%region_6.8 | all-reduce | flops 400 | bytes 3200 | tf_op jit(solution)/shard_map/psum | solution.py:27
  527.6 2.4 psum.37
  530.0 10.4 %psum.38 = f32[2,200]{1,0:T(2,128)S(1)} all-reduce(f32[2,200]{1,0:T(2,128)S(1)} %psum.37), channel_id=1, replica_groups=mesh['gx'=4,'gy_0'=2,'gy_1'=2,'gz_0'=4,'gz_1'=2] {'gz_0'}, use_global_device_ids=true, to_apply=%region_8.10 | all-reduce | flops 400 | bytes 3200 | tf_op jit(solution)/shard_map/psum | solution.py:27
  540.5 5.5 psum.39
  (5 shorter events, 0.1 us)
Async XLA Ops:
  7.2 336.9 %reduce-scatter.3.cloned.1.call-start = ((), (), s32[]{:S(2)}) async-start(), calls=%async_computation.3 | async-start | bytes 41943040 | tf_op jit(solution)/shard_map/reduce_scatter | solution.py:59
  7.2 2.8 copy-start.2
  58.9 366.0 %reduce-scatter.5.cloned.1.call-start = ((), (), s32[]{:S(2)}) async-start(), calls=%async_computation.4 | async-start | bytes 10485760 | tf_op jit(solution)/shard_map/reduce_scatter | solution.py:62
  427.8 5.0 copy-start.3
  427.8 33.2 %all-to-all-start = ((f32[8,16,4096]{2,1,0:T(8,128)}), f32[8,16,4096]{2,1,0:T(8,128)S(1)}, u32[]{:S(2)}, u32[]{:S(2)}) async-start(f32[8,16,4096]{2,1,0:T(8,128)} %bitcast.14), calls=%async_computation.2 | async-start | bytes 4194304 | tf_op jit(solution)/shard_map/all_to_all | solution.py:22
  461.2 24.6 %copy-start = (f32[16,2048]{1,0:T(8,128)}, f32[16,2048]{1,0:T(8,128)S(1)}, u32[]{:S(2)}) copy-start(f32[16,2048]{1,0:T(8,128)S(1)} %get-tuple-element.8) | copy-start | bytes 393220
  461.2 24.7 %copy-start.1 = (f32[16,2048]{1,0:T(8,128)}, f32[16,2048]{1,0:T(8,128)S(1)}, u32[]{:S(2)}) copy-start(f32[16,2048]{1,0:T(8,128)S(1)} %get-tuple-element.9) | copy-start | bytes 393220
  485.9 24.7 %copy-start.4 = (s32[200]{0:T(256)S(1)}, s32[200]{0:T(256)}, u32[]{:S(2)}) copy-start(s32[200]{0:T(256)} %param.8) | copy-start | bytes 2404
  485.9 24.8 %copy-start.5 = (s32[200]{0:T(256)S(1)}, s32[200]{0:T(256)}, u32[]{:S(2)}) copy-start(s32[200]{0:T(256)} %param.9) | copy-start | bytes 2404
Sparse Core Ops, SparseCore 0:
  59.0 285.0 reduce-scatter.2
  346.8 78.0 reduce-scatter.4
where the time goes:
time: 553 us
  waiting for transfers between devices  394 us (71%)
  local copies, waits for them, and re-layouts  55.7 us (10%)
  blocking collectives  35.2 us (6%)
  matrix products  27.5 us (5%)
  other arithmetic  21.1 us (4%)
  between operations  14.2 us (3%)
    reduce_scatter x1, waiting for transfers between devices, on_device(): lax.psum_scatter(jnp.concatenate([real_rows, imag_rows], 1), 'gx', scatte...  285 us
    reduce_scatter x1, waiting for transfers between devices, on_device(): by_gy = lax.psum_scatter(by_gx, GY, scatter_dimension=0, tiled=True)  80.8 us
    psum x5, blocking collectives, over_axes(): return functools.reduce(lax.psum, axes, array)  35.2 us
    all_to_all x1, waiting for transfers between devices, sent_and_summed(): lax.all_to_all(parts, axis, split_axis=0, concat_axis=0, tiled=True)  28 us
    gather x3, local copies, waits for them, and re-layouts, on_device(): picked_real = jnp.take_along_axis(density_real, partner, axis=1)  24.7 us
    gather x2, local copies, waits for them, and re-layouts, on_device(): picked_imag = jnp.take_along_axis(density_imag, partner, axis=1)  24.7 us
    concatenate x1, other arithmetic, on_device(): jnp.concatenate([real_rows, imag_rows], 1)  18.9 us
    dot_general x1, matrix products, on_device(): lax.dot_general(crossed, stacked, dims, preferred_element_type=jnp.float32)  14.8 us
  transfers between devices with their start and end apart: 3, of which 3 were waited for; matrix products, arithmetic and copies ran while one was open for 0% of the time, Pallas kernels for 0%

commit v1 on v0

v1 whole, which is shorter than its diff:
```python
import functools

import jax
import jax.numpy as jnp
from jax import lax
from jax.experimental import pallas as pl
from jax.experimental.pallas import tpu as pltpu
from jax.sharding import Mesh
from jax.sharding import PartitionSpec as P

AX = ("gx", "gy_0", "gy_1", "gz_0", "gz_1")
CORE = "gy_1"
SAME_CORE = ("gx", "gy_0", "gz_0", "gz_1")
CHUNK = 512


def device_index(x, y, z, core):
    return x * 32 + (z >> 1) * 16 + core * 8 + y * 2 + (z & 1)


def ring_perm(turn, step):
    pairs = []
    for x in range(4):
        for y in range(4):
            for z in range(4):
                for core in range(2):
                    to = [x, y, z]
                    axis = (turn + core) % 3
                    to[axis] = (to[axis] + step) % 4
                    pairs.append((device_index(x, y, z, core), device_index(*to, core)))
    return pairs


def round_ring(array, turn, step):
    return lax.ppermute(array, AX, ring_perm(turn, step))


def swapped(array):
    return lax.ppermute(array, CORE, [(0, 1), (1, 0)])


def prepare_kernel(pos_ref, a_ref, lt_ref, own_ref, other_ref):
    core = pos_ref[3]
    for block in range(16):
        cols = slice(block * 128, (block + 1) * 128)
        re = a_ref[0, :, cols].T
        im = a_ref[1, :, cols].T
        lt_ref[cols, 0:512] = re
        lt_ref[cols, 512:1024] = im
        lt_ref[cols, 1024:1536] = -re
    for block in range(8):
        cols = slice(block * 128, (block + 1) * 128)
        for ref, which in ((own_ref, core), (other_ref, core ^ 1)):
            from_cols = pl.ds(pl.multiple_of(block * 256 + which * 128, 128), 128)
            ref[:, cols] = a_ref[:, :, from_cols].reshape(1024, 128)


def prepare(pos, amps):
    return pl.pallas_call(
        prepare_kernel,
        out_shape=[
            jax.ShapeDtypeStruct((2048, 1536), jnp.bfloat16),
            jax.ShapeDtypeStruct((1024, 1024), jnp.bfloat16),
            jax.ShapeDtypeStruct((1024, 1024), jnp.bfloat16),
        ],
        grid_spec=pltpu.PrefetchScalarGridSpec(
            num_scalar_prefetch=1,
            grid=(1,),
            in_specs=[pl.BlockSpec((2, 512, 2048), lambda i, p: (0, 0, 0))],
            out_specs=[
                pl.BlockSpec((2048, 1536), lambda i, p: (0, 0)),
                pl.BlockSpec((1024, 1024), lambda i, p: (0, 0)),
                pl.BlockSpec((1024, 1024), lambda i, p: (0, 0)),
            ],
        ),
        compiler_params=pltpu.CompilerParams(vmem_limit_bytes=20 * 2**20),
        cost_estimate=pl.CostEstimate(flops=2 * 10**9, bytes_accessed=14 * 2**20, transcendentals=0),
        name="prepare",
    )(pos, amps)


CHUNKS = (((2, 0), (2, 1)), ((1, 1), (3, 0)), ((1, 0), (3, 1)), ((0, 0), (0, 1)))


def chunk_kernel(pos_ref, lt_ref, w_ref, *refs, halves, own, waits):
    refs = refs[waits:]
    recv_ref = refs[0] if own else None
    *outs, rows_ref, ids_ref = refs[1:] if own else refs
    whose = pos_ref[3] if own else pos_ref[3] ^ 1
    lane = lax.broadcasted_iota(jnp.int32, (16, 128), 0)
    at = 0
    for k1, half in halves:
        for k2 in (2 * half, 2 * half + 1):
            for k3 in range(4):
                ahead = [(k1, k2, k3), (k3, k1, k2)]
                x, y, z = [
                    (pos_ref[n] + jnp.where(whose == 0, ahead[0][n], ahead[1][n])) & 3 for n in range(3)
                ]
                base = x * 512 + (z >> 1) * 256 + y * 32 + (z & 1) * 16
                for co in range(2):
                    row = pl.multiple_of(base + co * 128, 16)
                    rows_ref[at : at + 16, :] = lt_ref[pl.ds(row, 16), :]
                    ids_ref[at : at + 16, :] = lane + row
                    at += 16
    for tile in range(4):
        cols = slice(tile * 256, (tile + 1) * 256)
        real = jnp.dot(rows_ref[:, 0:1024], w_ref[:, cols], preferred_element_type=jnp.float32)
        imag = jnp.dot(rows_ref[:, 512:1536], w_ref[:, cols], preferred_element_type=jnp.float32)
        for part in range(2):
            here = slice(part * 128, (part + 1) * 128)
            to = slice(tile * 256 + part * 128, tile * 256 + (part + 1) * 128)
            col = lax.broadcasted_iota(jnp.int32, (CHUNK, 128), 1) + ((tile * 2 + part) * 256 + whose * 128)
            value = jnp.where(ids_ref[...] >= col, real[:, here], imag[:, here])
            if own:
                value = value + recv_ref[:, to]
                outs[0][:, to] = value[: CHUNK // 2]
                outs[1][:, to] = value[CHUNK // 2 :]
            else:
                outs[0][:, to] = value


def chunk_part(pos, lt, w, halves, recv=None, waits=()):
    own = recv is not None
    full = pl.BlockSpec((CHUNK, 1024), lambda i, p: (0, 0))
    half = pl.BlockSpec((CHUNK // 2, 1024), lambda i, p: (0, 0))
    args = (pos, lt, w, *waits) + ((recv,) if own else ())
    in_specs = [
        pl.BlockSpec((2048, 1536), lambda i, p: (0, 0)),
        pl.BlockSpec((1024, 1024), lambda i, p: (0, 0)),
        *[pl.BlockSpec(memory_space=pl.ANY) for _ in waits],
    ]
    if own:
        in_specs.append(full)
        out_shape = [jax.ShapeDtypeStruct((CHUNK // 2, 1024), jnp.float32)] * 2
    else:
        out_shape = jax.ShapeDtypeStruct((CHUNK, 1024), jnp.float32)
    return pl.pallas_call(
        functools.partial(chunk_kernel, halves=halves, own=own, waits=len(waits)),
        out_shape=out_shape,
        grid_spec=pltpu.PrefetchScalarGridSpec(
            num_scalar_prefetch=1,
            grid=(1,),
            in_specs=in_specs,
            out_specs=[half] * 2 if own else full,
            scratch_shapes=[pltpu.VMEM((CHUNK, 1536), jnp.bfloat16), pltpu.VMEM((CHUNK, 128), jnp.int32)],
        ),
        compiler_params=pltpu.CompilerParams(vmem_limit_bytes=20 * 2**20),
        cost_estimate=pl.CostEstimate(
            flops=4 * CHUNK * 1024 * 1024, bytes_accessed=2**20 * 8, transcendentals=0
        ),
        name="own" if own else "other",
    )(*args)


def parity_sign(values, masks):
    anded = jnp.bitwise_and(values, masks)
    for shift in (8, 4, 2, 1):
        anded = jnp.bitwise_xor(anded, jnp.right_shift(anded, shift))
    return (1 - 2 * jnp.bitwise_and(anded, 1)).astype(jnp.float32)


def phase_parts(pauli_phase):
    real = jnp.where(pauli_phase == 0, 1.0, jnp.where(pauli_phase == 2, -1.0, 0.0))
    imag = jnp.where(pauli_phase == 1, 1.0, jnp.where(pauli_phase == 3, -1.0, 0.0))
    return real.astype(jnp.float32), imag.astype(jnp.float32)


def pauli_kernel(at_ref, w_ref, x_ref, z_ref, out_ref):
    own = lax.broadcasted_iota(jnp.int32, (32, 128), 0)
    row = at_ref[0] + jnp.where(own >= 16, own + 112, own)
    for half in range(2):
        cols = slice(half * 128, (half + 1) * 128)
        x, z = x_ref[:, cols], z_ref[:, cols]
        col = jnp.bitwise_xor(row, x)
        lane = jnp.bitwise_and(col, 127)
        block = jnp.right_shift(col, 7)
        picked = jnp.zeros((32, 128), jnp.float32)
        for b in range(8):
            got = jnp.take_along_axis(w_ref[:, b * 128 : (b + 1) * 128], lane, axis=1)
            picked = jnp.where(block == 2 * b + at_ref[1], got, picked)
        found = jnp.where(col <= row, 1.0, -1.0)
        twice = jnp.where(x == 0, 1.0, 2.0)
        here = jnp.where(found == parity_sign(x, z), parity_sign(row, z) * picked, 0.0)
        out_ref[:, cols] = twice * jnp.sum(here, axis=0, keepdims=True)


def pauli_parts(at, w_part, x, z):
    return pl.pallas_call(
        pauli_kernel,
        out_shape=jax.ShapeDtypeStruct((1, 256), jnp.float32),
        grid_spec=pltpu.PrefetchScalarGridSpec(
            num_scalar_prefetch=1,
            grid=(1,),
            in_specs=[
                pl.BlockSpec((32, 1024), lambda i, p: (0, 0)),
                pl.BlockSpec((1, 256), lambda i, p: (0, 0)),
                pl.BlockSpec((1, 256), lambda i, p: (0, 0)),
            ],
            out_specs=pl.BlockSpec((1, 256), lambda i, p: (0, 0)),
        ),
        compiler_params=pltpu.CompilerParams(vmem_limit_bytes=4 * 2**20),
        name="pauli",
    )(at, w_part, x, z)


def on_device(amplitudes, pauli_x, pauli_z, pauli_phase):
    total_cols = amplitudes.shape[1] * 128
    core = lax.axis_index(CORE)
    z_at = lax.axis_index(("gy_0", "gz_1"))
    pos = jnp.stack([lax.axis_index("gx"), lax.axis_index("gz_0"), z_at, core]).astype(jnp.int32)
    lt, w_own, w_other = prepare(pos, amplitudes)
    part = functools.partial(chunk_part, pos, lt)
    send1 = part(w_other, CHUNKS[0])
    recv1 = swapped(send1)
    send2 = part(w_other, CHUNKS[1], waits=(send1,))
    recv2 = swapped(send2)
    far0, far1 = part(w_own, CHUNKS[0], recv1, waits=(send2,))
    via_left = round_ring(far0, 0, 1)
    via_right = round_ring(far1, 0, -1)
    send3 = part(w_other, CHUNKS[2], waits=(far0,))
    recv3 = swapped(send3)
    right1, left0 = part(w_own, CHUNKS[1], recv2, waits=(send3,))
    from_left1 = round_ring(right1, 0, 1)
    from_right0 = round_ring(left0, 0, -1)
    send4 = part(w_other, CHUNKS[3], waits=(right1,))
    recv4 = swapped(send4)
    right0, left1 = part(w_own, CHUNKS[2], recv3, waits=(send4,))
    from_left0 = round_ring(right0 + via_left, 0, 1)
    from_right1 = round_ring(left1 + via_right, 0, -1)
    mine0, mine1 = part(w_own, CHUNKS[3], recv4, waits=(right0,))
    rows = []
    for mine, left, right in ((mine0, from_left0, from_right0), (mine1, from_left1, from_right1)):
        rows += [mine[k : k + 128] + left[k : k + 128] + right[k : k + 128] for k in (0, 128)]
    arrived = {k: round_ring(rows[k], 1, k) for k in (2, 1, 3)}
    rows = [
        sum((arrived[m][k : k + 32] for m in (1, 2, 3)), rows[0][k : k + 32]) for k in (0, 32, 64, 96)
    ]
    arrived = {k: round_ring(rows[k], 2, k) for k in (2, 1, 3)}
    both = (rows[0] + arrived[1] + arrived[2] + arrived[3]) * (1.0 / total_cols)
    first = lax.axis_index(AX) * 16
    first_rows = (first - core * 128).astype(jnp.int32)
    parts = pauli_parts(jnp.stack([first_rows, core.astype(jnp.int32)]), both, pauli_x[None], pauli_z[None])
    blocks = both.reshape(32, 64, 16).transpose(1, 2, 0).reshape(64, 512)
    message = jnp.concatenate([blocks, jnp.broadcast_to(parts, (64, 256))], 1).reshape(64, 6, 128)
    keep = lax.dynamic_slice_in_dim(both, core * 16, 16, 0)
    got = swapped(lax.dynamic_slice_in_dim(both, (1 - core) * 16, 16, 0))
    arrived = lax.all_to_all(message, SAME_CORE, split_axis=0, concat_axis=0, tiled=True)
    even_cols = jnp.where(core == 0, keep, got).reshape(16, 8, 128)
    odd_cols = jnp.where(core == 0, got, keep).reshape(16, 8, 128)
    w_rows = jnp.stack([even_cols, odd_cols], 2).reshape(16, 2048)
    sums = arrived[:, 4:].sum(0).reshape(256)[:200]
    sums = sums + swapped(sums)
    w_cols = arrived[:, :4].reshape(8, 8, 16, 2, 16).transpose(2, 0, 3, 1, 4).reshape(16, 2048)
    row = first + jnp.arange(16, dtype=jnp.int32)[:, None]
    col = jnp.arange(2048, dtype=jnp.int32)[None]
    density_real = jnp.where(col <= row, w_rows, w_cols)
    density_imag = jnp.where(col > row, w_rows, jnp.where(col < row, -w_cols, 0.0))
    even = parity_sign(pauli_x, pauli_z) > 0
    sum_real = jnp.where(even, sums, 0.0)
    sum_imag = jnp.where(even, 0.0, sums)
    phase_real, phase_imag = phase_parts(pauli_phase)
    expectations = jnp.stack(
        [phase_real * sum_real - phase_imag * sum_imag, phase_real * sum_imag + phase_imag * sum_real], 0
    )
    return density_real, density_imag, expectations


def solution(mesh):
    finer = Mesh(mesh.devices.reshape(mesh.shape["gx"], 2, 2, 4, 2), AX)
    in_specs = (P(None, AX, None), P(), P(), P())
    out_specs = (P(AX, None), P(AX, None), P())
    return jax.shard_map(on_device, mesh=finer, in_specs=in_specs, out_specs=out_specs, check_vma=False)
```

time: 553 us -> 128 us (0.23)
  waiting for transfers between devices: 394 us -> 48 us
  local copies, waits for them, and re-layouts: 55.7 us -> 6.49 us
  blocking collectives: 35.2 us -> 0 us
  starting transfers between devices: 5.11 us -> 39.2 us
  matrix products: 27.5 us -> 0 us
  Pallas kernels: 0 us -> 26.9 us
  other arithmetic: 21.1 us -> 3.67 us
  between operations: 14.2 us -> 0.9 us
    reduce_scatter x2 -> x0, waiting for transfers between devices: 366 us -> none  [the longest x1 285 us: on_device(): lax.psum_scatter(jnp.concatenate([real_rows, imag_rows], 1), 'gx', scatte...]
    gather x5 -> x0, local copies, waits for them, and re-layouts: 49.4 us -> none  [the longest x3 24.7 us: on_device(): picked_real = jnp.take_along_axis(density_real, partner, axis=1)]
    ppermute x0 -> x18, waiting for transfers between devices: none -> 38.7 us  [the longest x12 37.6 us: round_ring(): return lax.ppermute(array, AX, ring_perm(turn, step))]
    psum x5 -> x0, blocking collectives: 35.2 us -> none  [over_axes(): return functools.reduce(lax.psum, axes, array)]
    dot_general x2 -> x0, matrix products: 27.5 us -> none  [the longest x1 14.8 us: on_device(): lax.dot_general(crossed, stacked, dims, preferred_element_type=jnp.float32)]
    pallas_call x0 -> x10, Pallas kernels: none -> 26.9 us  [the longest x8 23.3 us: chunk_part(): pl.pallas_call(functools.partial(chunk_kernel, halves=halves, own=own, wa...]
    ppermute x0 -> x18, starting transfers between devices: none -> 21.2 us  [the longest x12 19.4 us: round_ring(): return lax.ppermute(array, AX, ring_perm(turn, step))]
    concatenate x1, other arithmetic: 18.9 us -> 0.17 us  [on_device(): jnp.concatenate([blocks, jnp.broadcast_to(parts, (64, 256))], 1)]
  transfers between devices with their start and end apart: 3 -> 19, of which waited for: 3 -> 12; matrix products, arithmetic and copies ran while one was open for 0% -> 3% of each run, Pallas kernels for 0% -> 17%
where the time goes in v1:
time: 128 us; the launch traced here: 125 us
  waiting for transfers between devices  48 us (38%)
  starting transfers between devices  39.2 us (31%)
  Pallas kernels  26.9 us (21%)
  local copies, waits for them, and re-layouts  6.49 us (5%)
  other arithmetic  3.67 us (3%)
    ppermute x12, waiting for transfers between devices, round_ring(): return lax.ppermute(array, AX, ring_perm(turn, step))  37.6 us
    pallas_call x8, Pallas kernels, chunk_part(): pl.pallas_call(functools.partial(chunk_kernel, halves=halves, own=own, wa...  23.3 us
    ppermute x12, starting transfers between devices, round_ring(): return lax.ppermute(array, AX, ring_perm(turn, step))  19.4 us
    all_to_all x1, starting transfers between devices, on_device(): lax.all_to_all(message, SAME_CORE, split_axis=0, concat_axis=0, tiled=True)  18 us
    all_to_all x1, waiting for transfers between devices, on_device(): lax.all_to_all(message, SAME_CORE, split_axis=0, concat_axis=0, tiled=True)  9.37 us
    pallas_call x1, Pallas kernels, prepare(): pl.pallas_call(prepare_kernel, out_shape=[jax.ShapeDtypeStruct((2048, 153...  2.8 us
  transfers between devices with their start and end apart: 19, of which 12 were waited for; matrix products, arithmetic and copies ran while one was open for 3% of the time, Pallas kernels for 17%

profile of v1, /device:TPU:8, one launch (start us, length us, event | category | flops | bytes accessed | tf_op | source)
XLA Modules:
  0.0 125.2 jit_solution(7843581341529342391)
XLA Ops:
  0.7 2.2 %copy-done.2 = bf16[2,512,2048]{2,1,0:T(8,128)(2,1)S(1)} copy-done((bf16[2,512,2048]{2,1,0:T(8,128)(2,1)S(1)}, bf16[2,512,2048]{2,1,0:T(8,128)(2,1)}, u32[]{:S(2)}) %copy-start.2) | copy-done | bytes 4194328
  2.9 2.8 %prepare.1 = (bf16[2048,1536]{1,0:T(8,128)(2,1)S(1)}, bf16[1024,1024]{1,0:T(8,128)(2,1)S(1)}, bf16[1024,1024]{1,0:T(8,128)(2,1)S(1)}) custom-call(s32[4]{0:T(128)S(1)} %pad_add_fusion.pos_ref, bf16[2,512,2048]{2,1,0:T(8,128)(2,1)S(1)} %copy-done.2), custom_call_target="tpu_custom_call" | custom-call | flops 2000000000 | bytes 14680064 | tf_op jit(solution)/shard_map/prepare/pallas_call | solution.py:59
  5.7 2.9 %other.4.refs_0_ = f32[512,1024]{1,0:T(8,128)S(1)} custom-call(s32[4]{0:T(128)S(1)} %pad_add_fusion.pos_ref, bf16[2048,1536]{1,0:T(8,128)(2,1)S(1)} %get-tuple-element.14.lt_ref, bf16[1024,1024]{1,0:T(8,128)(2,1)S(1)} %get-tuple-element.16.w_ref), custom_call_target="tpu_custom_call" | custom-call | flops 2147483648 | bytes 8388608 | tf_op jit(solution)/shard_map/other/pallas_call | solution.py:137
  8.7 2.9 %other.5.refs_0_ = f32[512,1024]{1,0:T(8,128)S(1)} custom-call(s32[4]{0:T(128)S(1)} %pad_add_fusion.pos_ref, bf16[2048,1536]{1,0:T(8,128)(2,1)S(1)} %get-tuple-element.14.lt_ref, bf16[1024,1024]{1,0:T(8,128)(2,1)S(1)} %get-tuple-element.16.w_ref, f32[512,1024]{1,0:T(8,128)S(1)} %other.4.refs_0_), custom_call_target="tpu_custom_call" | custom-call | flops 2147483648 | bytes 8388608 | tf_op jit(solution)/shard_map/other/pallas_call | solution.py:137
  11.6 0.6 collective-permute-start.1
  12.2 0.7 collective-permute-done.refs_1_
  12.9 2.9 %own.4 = (f32[256,1024]{1,0:T(8,128)S(1)}, f32[256,1024]{1,0:T(8,128)S(1)}) custom-call(s32[4]{0:T(128)S(1)} %pad_add_fusion.pos_ref, bf16[2048,1536]{1,0:T(8,128)(2,1)S(1)} %get-tuple-element.14.lt_ref, bf16[1024,1024]{1,0:T(8,128)(2,1)S(1)} %get-tuple-element.15.w_ref, f32[512,1024]{1,0:T(8,128)S(1)} %other.5.refs_0_, ...), custom_call_target="tpu_custom_call" | custom-call | flops 2147483648 | bytes 8388608 | tf_op jit(solution)/shard_map/own/pallas_call | solution.py:137
  15.8 2.9 %other.6.refs_0_ = f32[512,1024]{1,0:T(8,128)S(1)} custom-call(s32[4]{0:T(128)S(1)} %pad_add_fusion.pos_ref, bf16[2048,1536]{1,0:T(8,128)(2,1)S(1)} %get-tuple-element.14.lt_ref, bf16[1024,1024]{1,0:T(8,128)(2,1)S(1)} %get-tuple-element.16.w_ref, f32[256,1024]{1,0:T(8,128)S(1)} %get-tuple-element.17.refs_0_), custom_call_target="tpu_custom_call" | custom-call | flops 2147483648 | bytes 8388608 | tf_op jit(solution)/shard_map/other/pallas_call | solution.py:137
  18.7 0.4 collective-permute-start.2
  19.1 2.9 %own.5 = (f32[256,1024]{1,0:T(8,128)S(1)}, f32[256,1024]{1,0:T(8,128)S(1)}) custom-call(s32[4]{0:T(128)S(1)} %pad_add_fusion.pos_ref, bf16[2048,1536]{1,0:T(8,128)(2,1)S(1)} %get-tuple-element.14.lt_ref, bf16[1024,1024]{1,0:T(8,128)(2,1)S(1)} %get-tuple-element.15.w_ref, f32[512,1024]{1,0:T(8,128)S(1)} %other.6.refs_0_, ...), custom_call_target="tpu_custom_call" | custom-call | flops 2147483648 | bytes 8388608 | tf_op jit(solution)/shard_map/own/pallas_call | solution.py:137
  22.0 2.9 %other.7.refs_0_ = f32[512,1024]{1,0:T(8,128)S(1)} custom-call(s32[4]{0:T(128)S(1)} %pad_add_fusion.pos_ref, bf16[2048,1536]{1,0:T(8,128)(2,1)S(1)} %get-tuple-element.14.lt_ref, bf16[1024,1024]{1,0:T(8,128)(2,1)S(1)} %get-tuple-element.16.w_ref, f32[256,1024]{1,0:T(8,128)S(1)} %get-tuple-element.18.refs_0_), custom_call_target="tpu_custom_call" | custom-call | flops 2147483648 | bytes 8388608 | tf_op jit(solution)/shard_map/other/pallas_call | solution.py:137
  25.0 0.5 collective-permute-start.3
  25.4 2.8 %collective-permute-start.9 = (f32[256,1024]{1,0:T(8,128)S(1)}, f32[256,1024]{1,0:T(8,128)S(1)}, u32[]{:S(2)}, u32[]{:S(2)}) collective-permute-start(f32[256,1024]{1,0:T(8,128)S(1)} %get-tuple-element.24), channel_id=1, source_target_pairs={{0,96},{8,14},{1,97},{9,15},{16,112},{24,30},{17,113},{25,31},{2,9... | collective-permute-start | bytes 3145736 | tf_op jit(solution)/shard_map/ppermute | solution.py:35
  28.2 0.8 collective-permute-start.8
  28.9 2.9 %own.6 = (f32[256,1024]{1,0:T(8,128)S(1)}, f32[256,1024]{1,0:T(8,128)S(1)}) custom-call(s32[4]{0:T(128)S(1)} %pad_add_fusion.pos_ref, bf16[2048,1536]{1,0:T(8,128)(2,1)S(1)} %get-tuple-element.14.lt_ref, bf16[1024,1024]{1,0:T(8,128)(2,1)S(1)} %get-tuple-element.15.w_ref, f32[512,1024]{1,0:T(8,128)S(1)} %other.7.refs_0_, ...), custom_call_target="tpu_custom_call" | custom-call | flops 2147483648 | bytes 8388608 | tf_op jit(solution)/shard_map/own/pallas_call | solution.py:137
  31.9 8.6 %collective-permute-done.9 = f32[256,1024]{1,0:T(8,128)S(1)} collective-permute-done((f32[256,1024]{1,0:T(8,128)S(1)}, f32[256,1024]{1,0:T(8,128)S(1)}, u32[]{:S(2)}, u32[]{:S(2)}) %collective-permute-start.9) | collective-permute-done | bytes 1048608 | tf_op jit(solution)/shard_map/ppermute | solution.py:35
  40.7 3.8 %collective-permute-start.10 = (f32[256,1024]{1,0:T(8,128)S(1)}, f32[256,1024]{1,0:T(8,128)S(1)}, u32[]{:S(2)}, u32[]{:S(2)}) collective-permute-start(f32[256,1024]{1,0:T(8,128)S(1)} %add.127), channel_id=1, source_target_pairs={{0,96},{8,14},{1,97},{9,15},{16,112},{24,30},{17,113},{25,31},{2,9... | collective-permute-start | bytes 3145736 | tf_op jit(solution)/shard_map/ppermute | solution.py:35
  44.5 0.2 add.120
  44.7 2.0 %collective-permute-start.5 = (f32[256,1024]{1,0:T(8,128)S(1)}, f32[256,1024]{1,0:T(8,128)S(1)}, u32[]{:S(2)}, u32[]{:S(2)}) collective-permute-start(f32[256,1024]{1,0:T(8,128)S(1)} %add.120), channel_id=1, source_target_pairs={{0,32},{8,10},{1,33},{9,11},{16,48},{24,26},{17,49},{25,27},{2,34}... | collective-permute-start | bytes 3145736 | tf_op jit(solution)/shard_map/ppermute | solution.py:35
  46.7 2.9 %own.7 = (f32[256,1024]{1,0:T(8,128)S(1)}, f32[256,1024]{1,0:T(8,128)S(1)}) custom-call(s32[4]{0:T(128)S(1)} %pad_add_fusion.pos_ref, bf16[2048,1536]{1,0:T(8,128)(2,1)S(1)} %get-tuple-element.14.lt_ref, bf16[1024,1024]{1,0:T(8,128)(2,1)S(1)} %get-tuple-element.15.w_ref, f32[256,1024]{1,0:T(8,128)S(1)} %get-tuple-element.19.refs_0_, ...), custom_call_target="tpu_custom_call" | custom-call | flops 2147483648 | bytes 8388608 | tf_op jit(solution)/shard_map/own/pallas_call | solution.py:137
  49.6 5.8 %collective-permute-done.8 = f32[256,1024]{1,0:T(8,128)S(1)} collective-permute-done((f32[256,1024]{1,0:T(8,128)S(1)}, f32[256,1024]{1,0:T(8,128)S(1)}, u32[]{:S(2)}, u32[]{:S(2)}) %collective-permute-start.8) | collective-permute-done | bytes 1048608 | tf_op jit(solution)/shard_map/ppermute | solution.py:35
  55.4 1.3 %collective-permute-done.10 = f32[256,1024]{1,0:T(8,128)S(1)} collective-permute-done((f32[256,1024]{1,0:T(8,128)S(1)}, f32[256,1024]{1,0:T(8,128)S(1)}, u32[]{:S(2)}, u32[]{:S(2)}) %collective-permute-start.10) | collective-permute-done | bytes 1048608 | tf_op jit(solution)/shard_map/ppermute | solution.py:35
  56.7 0.3 slice_add_fusion.2
  57.0 0.5 collective-permute-start.12
  57.5 2.6 %collective-permute-start.11 = (f32[128,1024]{1,0:T(8,128)S(1)}, f32[128,1024]{1,0:T(8,128)S(1)}, u32[]{:S(2)}, u32[]{:S(2)}) collective-permute-start(f32[128,1024]{1,0:T(8,128)S(1)} %get-tuple-element.27), channel_id=1, source_target_pairs={{0,4},{8,24},{1,5},{9,25},{16,20},{24,8},{17,21},{25,9},{2,6},{10,... | collective-permute-start | bytes 1572872 | tf_op jit(solution)/shard_map/ppermute | solution.py:35
  60.1 7.9 %collective-permute-done.6 = f32[256,1024]{1,0:T(8,128)S(1)} collective-permute-done((f32[256,1024]{1,0:T(8,128)S(1)}, f32[256,1024]{1,0:T(8,128)S(1)}, u32[]{:S(2)}, u32[]{:S(2)}) %collective-permute-start.6) | collective-permute-done | bytes 1048608 | tf_op jit(solution)/shard_map/ppermute | solution.py:35
  68.0 1.1 slice_add_fusion.6
  69.1 1.6 %collective-permute-start.7 = (f32[128,1024]{1,0:T(8,128)}, f32[128,1024]{1,0:T(8,128)S(1)}, u32[]{:S(2)}, u32[]{:S(2)}) collective-permute-start(f32[128,1024]{1,0:T(8,128)} %get-tuple-element.26), channel_id=1, source_target_pairs={{0,2},{8,9},{1,3},{9,24},{16,18},{24,25},{17,19},{25,8},{2,4},{10,... | collective-permute-start | bytes 1572872 | tf_op jit(solution)/shard_map/ppermute | solution.py:35
  70.6 7.2 %collective-permute-done.11 = f32[128,1024]{1,0:T(8,128)S(1)} collective-permute-done((f32[128,1024]{1,0:T(8,128)S(1)}, f32[128,1024]{1,0:T(8,128)S(1)}, u32[]{:S(2)}, u32[]{:S(2)}) %collective-permute-start.11) | collective-permute-done | bytes 524320 | tf_op jit(solution)/shard_map/ppermute | solution.py:35
  77.8 0.7 collective-permute-done.7
  78.5 4.1 %collective-permute-start.15 = (f32[32,1024]{1,0:T(8,128)S(1)}, f32[32,1024]{1,0:T(8,128)S(1)}, u32[]{:S(2)}, u32[]{:S(2)}) collective-permute-start(f32[32,1024]{1,0:T(8,128)S(1)} %get-tuple-element.30), channel_id=1, source_target_pairs={{0,17},{8,104},{1,0},{9,105},{16,1},{24,120},{17,16},{25,121},{2,1... | collective-permute-start | bytes 393224 | tf_op jit(solution)/shard_map/ppermute | solution.py:35
  82.7 1.3 %collective-permute-start.13 = (f32[32,1024]{1,0:T(8,128)S(1)}, f32[32,1024]{1,0:T(8,128)S(1)}, u32[]{:S(2)}, u32[]{:S(2)}) collective-permute-start(f32[32,1024]{1,0:T(8,128)S(1)} %get-tuple-element.29), channel_id=1, source_target_pairs={{0,1},{8,40},{1,16},{9,41},{16,17},{24,56},{17,0},{25,57},{2,3},{1... | collective-permute-start | bytes 393224 | tf_op jit(solution)/shard_map/ppermute | solution.py:35
  84.0 2.6 %collective-permute-done.15 = f32[32,1024]{1,0:T(8,128)S(1)} collective-permute-done((f32[32,1024]{1,0:T(8,128)S(1)}, f32[32,1024]{1,0:T(8,128)S(1)}, u32[]{:S(2)}, u32[]{:S(2)}) %collective-permute-start.15) | collective-permute-done | bytes 131104 | tf_op jit(solution)/shard_map/ppermute | solution.py:35
  86.6 2.6 %collective-permute-done.14 = f32[32,1024]{1,0:T(8,128)S(1)} collective-permute-done((f32[32,1024]{1,0:T(8,128)S(1)}, f32[32,1024]{1,0:T(8,128)S(1)}, u32[]{:S(2)}, u32[]{:S(2)}) %collective-permute-start.14) | collective-permute-done | bytes 131104 | tf_op jit(solution)/shard_map/ppermute | solution.py:35
  89.2 1.0 collective-permute-done.13
  90.3 0.2 copy.13
  90.5 0.2 collective-permute-start.16
  90.7 0.3 copy.14
  91.0 0.8 pauli.1
  92.0 0.9 copy.17
  92.8 18.0 %all-to-all-start = ((f32[64,6,128]{2,1,0:T(8,128)}), f32[64,6,128]{2,1,0:T(8,128)S(1)}, u32[]{:S(2)}, u32[]{:S(2)}) async-start(f32[64,6,128]{2,1,0:T(8,128)} %copy.17), calls=%async_computation | async-start | bytes 524288 | tf_op jit(solution)/shard_map/all_to_all | solution.py:247
  111.2 9.4 %all-to-all-done = f32[64,6,128]{2,1,0:T(8,128)S(1)} async-done(((f32[64,6,128]{2,1,0:T(8,128)}), f32[64,6,128]{2,1,0:T(8,128)S(1)}, u32[]{:S(2)}, u32[]{:S(2)}) %all-to-all-start) | async-done | bytes 196640 | tf_op jit(solution)/shard_map/all_to_all | solution.py:247
  120.6 1.4 %reshape.36 = f32[8,8,16,2,16]{4,3,2,1,0:T(2,128)S(1)} reshape(f32[64,4,128]{2,1,0:T(4,128)S(1)} %slice.148) | data formatting | bytes 262144 | tf_op jit(solution)/shard_map/reshape | solution.py:253
  122.0 0.6 copy.16
  122.6 0.6 reshape.37
  123.4 0.8 select_select_fusion
  124.2 0.3 collective-permute-done.17
  124.6 0.6 pad_maximum_fusion.2
  (37 shorter events, 1.3 us)
Async XLA Ops:
  0.7 2.2 %copy-start.2 = (bf16[2,512,2048]{2,1,0:T(8,128)(2,1)S(1)}, bf16[2,512,2048]{2,1,0:T(8,128)(2,1)}, u32[]{:S(2)}) copy-start(bf16[2,512,2048]{2,1,0:T(8,128)(2,1)} %a_ref.1) | copy-start | bytes 12582916
  8.6 4.2 %collective-permute-start = (f32[512,1024]{1,0:T(8,128)S(1)}, f32[512,1024]{1,0:T(8,128)S(1)}, u32[]{:S(2)}, u32[]{:S(2)}) collective-permute-start(f32[512,1024]{1,0:T(8,128)S(1)} %other.4.refs_0_), channel_id=1, source_target_pairs={{0,8},{8,0},{1,9},{9,1},{2,10},{10,2},{3,11},{11,3},{4,12},{12,4},... | collective-permute-start | bytes 6291464 | tf_op jit(solution)/shard_map/ppermute | solution.py:39
  11.6 7.5 %collective-permute-start.1 = (f32[512,1024]{1,0:T(8,128)S(1)}, f32[512,1024]{1,0:T(8,128)S(1)}, u32[]{:S(2)}, u32[]{:S(2)}) collective-permute-start(f32[512,1024]{1,0:T(8,128)S(1)} %other.5.refs_0_), channel_id=1, source_target_pairs={{0,8},{8,0},{1,9},{9,1},{2,10},{10,2},{3,11},{11,3},{4,12},{12,4},... | collective-permute-start | bytes 6291464 | tf_op jit(solution)/shard_map/ppermute | solution.py:39
  18.7 10.2 %collective-permute-start.2 = (f32[512,1024]{1,0:T(8,128)S(1)}, f32[512,1024]{1,0:T(8,128)S(1)}, u32[]{:S(2)}, u32[]{:S(2)}) collective-permute-start(f32[512,1024]{1,0:T(8,128)S(1)} %other.6.refs_0_), channel_id=1, source_target_pairs={{0,8},{8,0},{1,9},{9,1},{2,10},{10,2},{3,11},{11,3},{4,12},{12,4},... | collective-permute-start | bytes 6291464 | tf_op jit(solution)/shard_map/ppermute | solution.py:39
  25.0 21.8 %collective-permute-start.3 = (f32[512,1024]{1,0:T(8,128)S(1)}, f32[512,1024]{1,0:T(8,128)S(1)}, u32[]{:S(2)}, u32[]{:S(2)}) collective-permute-start(f32[512,1024]{1,0:T(8,128)S(1)} %other.7.refs_0_), channel_id=1, source_target_pairs={{0,8},{8,0},{1,9},{9,1},{2,10},{10,2},{3,11},{11,3},{4,12},{12,4},... | collective-permute-start | bytes 6291464 | tf_op jit(solution)/shard_map/ppermute | solution.py:39
  25.4 15.1 %collective-permute-start.9 = (f32[256,1024]{1,0:T(8,128)S(1)}, f32[256,1024]{1,0:T(8,128)S(1)}, u32[]{:S(2)}, u32[]{:S(2)}) collective-permute-start(f32[256,1024]{1,0:T(8,128)S(1)} %get-tuple-element.24), channel_id=1, source_target_pairs={{0,96},{8,14},{1,97},{9,15},{16,112},{24,30},{17,113},{25,31},{2,9... | collective-permute-start | bytes 3145736 | tf_op jit(solution)/shard_map/ppermute | solution.py:35
  28.2 16.3 %collective-permute-start.4 = (f32[256,1024]{1,0:T(8,128)S(1)}, f32[256,1024]{1,0:T(8,128)S(1)}, u32[]{:S(2)}, u32[]{:S(2)}) collective-permute-start(f32[256,1024]{1,0:T(8,128)S(1)} %get-tuple-element.17.refs_0_), channel_id=1, source_target_pairs={{0,32},{8,10},{1,33},{9,11},{16,48},{24,26},{17,49},{25,27},{2,34}... | collective-permute-start | bytes 3145736 | tf_op jit(solution)/shard_map/ppermute | solution.py:35
  28.2 27.2 %collective-permute-start.8 = (f32[256,1024]{1,0:T(8,128)S(1)}, f32[256,1024]{1,0:T(8,128)S(1)}, u32[]{:S(2)}, u32[]{:S(2)}) collective-permute-start(f32[256,1024]{1,0:T(8,128)S(1)} %get-tuple-element.18.refs_0_), channel_id=1, source_target_pairs={{0,32},{8,10},{1,33},{9,11},{16,48},{24,26},{17,49},{25,27},{2,34}... | collective-permute-start | bytes 3145736 | tf_op jit(solution)/shard_map/ppermute | solution.py:35
  40.7 16.1 %collective-permute-start.10 = (f32[256,1024]{1,0:T(8,128)S(1)}, f32[256,1024]{1,0:T(8,128)S(1)}, u32[]{:S(2)}, u32[]{:S(2)}) collective-permute-start(f32[256,1024]{1,0:T(8,128)S(1)} %add.127), channel_id=1, source_target_pairs={{0,96},{8,14},{1,97},{9,15},{16,112},{24,30},{17,113},{25,31},{2,9... | collective-permute-start | bytes 3145736 | tf_op jit(solution)/shard_map/ppermute | solution.py:35
  44.4 23.6 %collective-permute-start.6 = (f32[256,1024]{1,0:T(8,128)S(1)}, f32[256,1024]{1,0:T(8,128)S(1)}, u32[]{:S(2)}, u32[]{:S(2)}) collective-permute-start(f32[256,1024]{1,0:T(8,128)S(1)} %get-tuple-element.21), channel_id=1, source_target_pairs={{0,96},{8,14},{1,97},{9,15},{16,112},{24,30},{17,113},{25,31},{2,9... | collective-permute-start | bytes 3145736 | tf_op jit(solution)/shard_map/ppermute | solution.py:35
  44.7 23.3 %collective-permute-start.5 = (f32[256,1024]{1,0:T(8,128)S(1)}, f32[256,1024]{1,0:T(8,128)S(1)}, u32[]{:S(2)}, u32[]{:S(2)}) collective-permute-start(f32[256,1024]{1,0:T(8,128)S(1)} %add.120), channel_id=1, source_target_pairs={{0,32},{8,10},{1,33},{9,11},{16,48},{24,26},{17,49},{25,27},{2,34}... | collective-permute-start | bytes 3145736 | tf_op jit(solution)/shard_map/ppermute | solution.py:35
  57.0 13.6 %collective-permute-start.12 = (f32[128,1024]{1,0:T(8,128)S(1)}, f32[128,1024]{1,0:T(8,128)S(1)}, u32[]{:S(2)}, u32[]{:S(2)}) collective-permute-start(f32[128,1024]{1,0:T(8,128)S(1)} %get-tuple-element.28), channel_id=1, source_target_pairs={{0,6},{8,25},{1,7},{9,8},{16,22},{24,9},{17,23},{25,24},{2,0},{10,... | collective-permute-start | bytes 1572872 | tf_op jit(solution)/shard_map/ppermute | solution.py:35
  57.5 20.3 %collective-permute-start.11 = (f32[128,1024]{1,0:T(8,128)S(1)}, f32[128,1024]{1,0:T(8,128)S(1)}, u32[]{:S(2)}, u32[]{:S(2)}) collective-permute-start(f32[128,1024]{1,0:T(8,128)S(1)} %get-tuple-element.27), channel_id=1, source_target_pairs={{0,4},{8,24},{1,5},{9,25},{16,20},{24,8},{17,21},{25,9},{2,6},{10,... | collective-permute-start | bytes 1572872 | tf_op jit(solution)/shard_map/ppermute | solution.py:35
  69.1 9.4 %collective-permute-start.7 = (f32[128,1024]{1,0:T(8,128)}, f32[128,1024]{1,0:T(8,128)S(1)}, u32[]{:S(2)}, u32[]{:S(2)}) collective-permute-start(f32[128,1024]{1,0:T(8,128)} %get-tuple-element.26), channel_id=1, source_target_pairs={{0,2},{8,9},{1,3},{9,24},{16,18},{24,25},{17,19},{25,8},{2,4},{10,... | collective-permute-start | bytes 1572872 | tf_op jit(solution)/shard_map/ppermute | solution.py:35
  78.5 12.5 %copy-start = (s32[200]{0:T(256)S(1)}, s32[200]{0:T(256)}, u32[]{:S(2)}) copy-start(s32[200]{0:T(256)} %param.5) | copy-start | bytes 2404
  78.5 12.5 %copy-start.1 = (s32[200]{0:T(256)S(1)}, s32[200]{0:T(256)}, u32[]{:S(2)}) copy-start(s32[200]{0:T(256)} %param.6) | copy-start | bytes 2404
  78.5 8.0 %collective-permute-start.15 = (f32[32,1024]{1,0:T(8,128)S(1)}, f32[32,1024]{1,0:T(8,128)S(1)}, u32[]{:S(2)}, u32[]{:S(2)}) collective-permute-start(f32[32,1024]{1,0:T(8,128)S(1)} %get-tuple-element.30), channel_id=1, source_target_pairs={{0,17},{8,104},{1,0},{9,105},{16,1},{24,120},{17,16},{25,121},{2,1... | collective-permute-start | bytes 393224 | tf_op jit(solution)/shard_map/ppermute | solution.py:35
  82.7 6.6 %collective-permute-start.14 = (f32[32,1024]{1,0:T(8,128)S(1)}, f32[32,1024]{1,0:T(8,128)S(1)}, u32[]{:S(2)}, u32[]{:S(2)}) collective-permute-start(f32[32,1024]{1,0:T(8,128)S(1)} %get-tuple-element.31), channel_id=1, source_target_pairs={{0,16},{8,72},{1,17},{9,73},{16,0},{24,88},{17,1},{25,89},{2,18},{... | collective-permute-start | bytes 393224 | tf_op jit(solution)/shard_map/ppermute | solution.py:35
  82.7 7.6 %collective-permute-start.13 = (f32[32,1024]{1,0:T(8,128)S(1)}, f32[32,1024]{1,0:T(8,128)S(1)}, u32[]{:S(2)}, u32[]{:S(2)}) collective-permute-start(f32[32,1024]{1,0:T(8,128)S(1)} %get-tuple-element.29), channel_id=1, source_target_pairs={{0,1},{8,40},{1,16},{9,41},{16,17},{24,56},{17,0},{25,57},{2,3},{1... | collective-permute-start | bytes 393224 | tf_op jit(solution)/shard_map/ppermute | solution.py:35
  90.5 20.3 %collective-permute-start.16 = (f32[16,1024]{1,0:T(8,128)S(1)}, f32[16,1024]{1,0:T(8,128)S(1)}, u32[]{:S(2)}, u32[]{:S(2)}) collective-permute-start(f32[16,1024]{1,0:T(8,128)S(1)} %constant_dynamic-slice_fusion), channel_id=1, source_target_pairs={{0,8},{8,0},{1,9},{9,1},{2,10},{10,2},{3,11},{11,3},{4,12},{12,4},... | collective-permute-start | bytes 196616 | tf_op jit(solution)/shard_map/ppermute | solution.py:39
  92.8 27.7 %all-to-all-start = ((f32[64,6,128]{2,1,0:T(8,128)}), f32[64,6,128]{2,1,0:T(8,128)S(1)}, u32[]{:S(2)}, u32[]{:S(2)}) async-start(f32[64,6,128]{2,1,0:T(8,128)} %copy.17), calls=%async_computation | async-start | bytes 524288 | tf_op jit(solution)/shard_map/all_to_all | solution.py:247
  122.0 2.6 %copy-start.3 = (s32[200]{0:T(256)S(1)}, s32[200]{0:T(256)}, u32[]{:S(2)}) copy-start(s32[200]{0:T(256)} %param.7) | copy-start | bytes 2404
  123.3 1.2 collective-permute-start.17

commit v2 on v1

--- a/solution.py
+++ b/solution.py
@@ -82,10 +82,10 @@
 CHUNKS = (((2, 0), (2, 1)), ((1, 1), (3, 0)), ((1, 0), (3, 1)), ((0, 0), (0, 1)))
 
 
-def chunk_kernel(pos_ref, lt_ref, w_ref, *refs, halves, own, waits):
+def chunk_kernel(pos_ref, lt_ref, w_ref, *refs, halves, own, adds, waits):
     refs = refs[waits:]
-    recv_ref = refs[0] if own else None
-    *outs, rows_ref, ids_ref = refs[1:] if own else refs
+    recv_ref = refs[0] if adds else None
+    *outs, rows_ref, ids_ref = refs[1:] if adds else refs
     whose = pos_ref[3] if own else pos_ref[3] ^ 1
     lane = lax.broadcasted_iota(jnp.int32, (16, 128), 0)
     at = 0
@@ -111,31 +111,33 @@
             to = slice(tile * 256 + part * 128, tile * 256 + (part + 1) * 128)
             col = lax.broadcasted_iota(jnp.int32, (CHUNK, 128), 1) + ((tile * 2 + part) * 256 + whose * 128)
             value = jnp.where(ids_ref[...] >= col, real[:, here], imag[:, here])
+            if adds:
+                value = value + recv_ref[:, to]
             if own:
-                value = value + recv_ref[:, to]
                 outs[0][:, to] = value[: CHUNK // 2]
                 outs[1][:, to] = value[CHUNK // 2 :]
             else:
                 outs[0][:, to] = value
 
 
-def chunk_part(pos, lt, w, halves, recv=None, waits=()):
-    own = recv is not None
+def chunk_part(pos, lt, w, halves, own, recv=None, waits=()):
+    adds = recv is not None
     full = pl.BlockSpec((CHUNK, 1024), lambda i, p: (0, 0))
     half = pl.BlockSpec((CHUNK // 2, 1024), lambda i, p: (0, 0))
-    args = (pos, lt, w, *waits) + ((recv,) if own else ())
+    args = (pos, lt, w, *waits) + ((recv,) if adds else ())
     in_specs = [
         pl.BlockSpec((2048, 1536), lambda i, p: (0, 0)),
         pl.BlockSpec((1024, 1024), lambda i, p: (0, 0)),
         *[pl.BlockSpec(memory_space=pl.ANY) for _ in waits],
     ]
+    if adds:
+        in_specs.append(full)
     if own:
-        in_specs.append(full)
         out_shape = [jax.ShapeDtypeStruct((CHUNK // 2, 1024), jnp.float32)] * 2
     else:
         out_shape = jax.ShapeDtypeStruct((CHUNK, 1024), jnp.float32)
     return pl.pallas_call(
-        functools.partial(chunk_kernel, halves=halves, own=own, waits=len(waits)),
+        functools.partial(chunk_kernel, halves=halves, own=own, adds=adds, waits=len(waits)),
         out_shape=out_shape,
         grid_spec=pltpu.PrefetchScalarGridSpec(
             num_scalar_prefetch=1,
@@ -144,7 +146,7 @@
             out_specs=[half] * 2 if own else full,
             scratch_shapes=[pltpu.VMEM((CHUNK, 1536), jnp.bfloat16), pltpu.VMEM((CHUNK, 128), jnp.int32)],
         ),
-        compiler_params=pltpu.CompilerParams(vmem_limit_bytes=20 * 2**20),
+        compiler_params=pltpu.CompilerParams(vmem_limit_bytes=12 * 2**20),
         cost_estimate=pl.CostEstimate(
             flops=4 * CHUNK * 1024 * 1024, bytes_accessed=2**20 * 8, transcendentals=0
         ),
@@ -203,58 +205,111 @@
     )(at, w_part, x, z)
 
 
+def swap_blocks(value):
+    row = lax.broadcasted_iota(jnp.int32, (8, 128), 0)
+    group = jnp.right_shift(lax.broadcasted_iota(jnp.int32, (8, 128), 1), 4)
+    for step in (4, 2, 1):
+        up = pltpu.roll(pltpu.roll(value, 8 - step, 0), 16 * step, 1)
+        down = up if step == 4 else pltpu.roll(pltpu.roll(value, step, 0), 128 - 16 * step, 1)
+        low_row = jnp.bitwise_and(row, step) == 0
+        low_group = jnp.bitwise_and(group, step) == 0
+        value = jnp.where(low_row, jnp.where(low_group, value, up), jnp.where(low_group, down, value))
+    return value
+
+
+def densities_kernel(place_ref, keep_ref, got_ref, col_ref, real_ref, imag_ref):
+    first, core = place_ref[0], place_ref[1]
+    row = lax.broadcasted_iota(jnp.int32, (8, 128), 0)
+    lane = lax.broadcasted_iota(jnp.int32, (8, 128), 1)
+    for t in range(8):
+        for high in range(2):
+            here = slice(high * 8, (high + 1) * 8)
+            kept = keep_ref[here, t * 128 : (t + 1) * 128]
+            got = got_ref[here, t * 128 : (t + 1) * 128]
+            for co in range(2):
+                across = swap_blocks(
+                    col_ref[t * 8 : (t + 1) * 8, (co * 2 + high) * 128 : (co * 2 + high + 1) * 128]
+                )
+                mine = jnp.where(core == co, kept, got)
+                i = row + (first + high * 8)
+                j = lane + (t * 256 + co * 128)
+                cols = slice(t * 256 + co * 128, t * 256 + (co + 1) * 128)
+                real_ref[here, cols] = jnp.where(j <= i, mine, across)
+                imag_ref[here, cols] = jnp.where(j > i, mine, jnp.where(j < i, -across, 0.0))
+
+
+def densities(place, keep, got, arrived):
+    rows = pl.BlockSpec((16, 1024), lambda i, p: (0, 0))
+    out = pl.BlockSpec((16, 2048), lambda i, p: (0, 0))
+    return pl.pallas_call(
+        densities_kernel,
+        out_shape=[jax.ShapeDtypeStruct((16, 2048), jnp.float32)] * 2,
+        grid_spec=pltpu.PrefetchScalarGridSpec(
+            num_scalar_prefetch=1,
+            grid=(1,),
+            in_specs=[rows, rows, pl.BlockSpec((64, 768), lambda i, p: (0, 0))],
+            out_specs=[out, out],
+        ),
+        compiler_params=pltpu.CompilerParams(vmem_limit_bytes=4 * 2**20),
+        name="densities",
+    )(place, keep, got, arrived)
+
+
 def on_device(amplitudes, pauli_x, pauli_z, pauli_phase):
     total_cols = amplitudes.shape[1] * 128
     core = lax.axis_index(CORE)
     z_at = lax.axis_index(("gy_0", "gz_1"))
     pos = jnp.stack([lax.axis_index("gx"), lax.axis_index("gz_0"), z_at, core]).astype(jnp.int32)
     lt, w_own, w_other = prepare(pos, amplitudes)
-    part = functools.partial(chunk_part, pos, lt)
-    send1 = part(w_other, CHUNKS[0])
+    send = functools.partial(chunk_part, pos, lt, w_other, own=False)
+    make = functools.partial(chunk_part, pos, lt, w_own, own=True)
+    send1 = send(CHUNKS[0])
     recv1 = swapped(send1)
-    send2 = part(w_other, CHUNKS[1], waits=(send1,))
-    recv2 = swapped(send2)
-    far0, far1 = part(w_own, CHUNKS[0], recv1, waits=(send2,))
+    far0, far1 = make(CHUNKS[0], waits=(send1,))
+    far0, far1 = far0 + recv1[: CHUNK // 2], far1 + recv1[CHUNK // 2 :]
     via_left = round_ring(far0, 0, 1)
     via_right = round_ring(far1, 0, -1)
-    send3 = part(w_other, CHUNKS[2], waits=(far0,))
+    send2 = send(CHUNKS[1], waits=(far0,))
+    recv2 = swapped(send2)
+    send3 = send(CHUNKS[2], waits=(send2,))
     recv3 = swapped(send3)
-    right1, left0 = part(w_own, CHUNKS[1], recv2, waits=(send3,))
+    right1, left0 = make(CHUNKS[1], recv=recv2, waits=(send3,))
     from_left1 = round_ring(right1, 0, 1)
     from_right0 = round_ring(left0, 0, -1)
-    send4 = part(w_other, CHUNKS[3], waits=(right1,))
+    send4 = send(CHUNKS[3], waits=(right1,))
     recv4 = swapped(send4)
-    right0, left1 = part(w_own, CHUNKS[2], recv3, waits=(send4,))
+    right0, left1 = make(CHUNKS[2], recv=recv3, waits=(send4,))
     from_left0 = round_ring(right0 + via_left, 0, 1)
     from_right1 = round_ring(left1 + via_right, 0, -1)
-    mine0, mine1 = part(w_own, CHUNKS[3], recv4, waits=(right0,))
+    mine0, mine1 = make(CHUNKS[3], recv=recv4, waits=(right0,))
+    from_left0, from_left1, from_right0, from_right1 = lax.optimization_barrier(
+        (from_left0, from_left1, from_right0, from_right1)
+    )
     rows = []
     for mine, left, right in ((mine0, from_left0, from_right0), (mine1, from_left1, from_right1)):
         rows += [mine[k : k + 128] + left[k : k + 128] + right[k : k + 128] for k in (0, 128)]
-    arrived = {k: round_ring(rows[k], 1, k) for k in (2, 1, 3)}
+    arrived = {}
+    for k in (2, 1, 3):
+        arrived[k] = round_ring(rows[k], 1, k)
     rows = [
         sum((arrived[m][k : k + 32] for m in (1, 2, 3)), rows[0][k : k + 32]) for k in (0, 32, 64, 96)
     ]
-    arrived = {k: round_ring(rows[k], 2, k) for k in (2, 1, 3)}
+    arrived = {}
+    for k in (2, 1, 3):
+        arrived[k] = round_ring(rows[k], 2, k)
     both = (rows[0] + arrived[1] + arrived[2] + arrived[3]) * (1.0 / total_cols)
     first = lax.axis_index(AX) * 16
     first_rows = (first - core * 128).astype(jnp.int32)
     parts = pauli_parts(jnp.stack([first_rows, core.astype(jnp.int32)]), both, pauli_x[None], pauli_z[None])
-    blocks = both.reshape(32, 64, 16).transpose(1, 2, 0).reshape(64, 512)
-    message = jnp.concatenate([blocks, jnp.broadcast_to(parts, (64, 256))], 1).reshape(64, 6, 128)
+    blocks = both.reshape(2, 16, 64, 16).transpose(2, 0, 3, 1).reshape(64, 512)
+    message = jnp.concatenate([blocks, jnp.broadcast_to(parts, (64, 256))], 1)
     keep = lax.dynamic_slice_in_dim(both, core * 16, 16, 0)
     got = swapped(lax.dynamic_slice_in_dim(both, (1 - core) * 16, 16, 0))
     arrived = lax.all_to_all(message, SAME_CORE, split_axis=0, concat_axis=0, tiled=True)
-    even_cols = jnp.where(core == 0, keep, got).reshape(16, 8, 128)
-    odd_cols = jnp.where(core == 0, got, keep).reshape(16, 8, 128)
-    w_rows = jnp.stack([even_cols, odd_cols], 2).reshape(16, 2048)
-    sums = arrived[:, 4:].sum(0).reshape(256)[:200]
+    sums = arrived[:, 512:].sum(0)[:200]
     sums = sums + swapped(sums)
-    w_cols = arrived[:, :4].reshape(8, 8, 16, 2, 16).transpose(2, 0, 3, 1, 4).reshape(16, 2048)
-    row = first + jnp.arange(16, dtype=jnp.int32)[:, None]
-    col = jnp.arange(2048, dtype=jnp.int32)[None]
-    density_real = jnp.where(col <= row, w_rows, w_cols)
-    density_imag = jnp.where(col > row, w_rows, jnp.where(col < row, -w_cols, 0.0))
+    place = jnp.stack([first.astype(jnp.int32), core.astype(jnp.int32)])
+    density_real, density_imag = densities(place, keep, got, arrived)
     even = parity_sign(pauli_x, pauli_z) > 0
     sum_real = jnp.where(even, sums, 0.0)
     sum_imag = jnp.where(even, 0.0, sums)

time: 128 us -> 121 us (0.945)
  the two profiles are of different devices: /device:TPU:8 before, /device:TPU:1 now
where the time goes in v2:
time: 121 us; the launch traced here: 120 us
  waiting for transfers between devices  48.4 us (40%)
  starting transfers between devices  36.3 us (30%)
  Pallas kernels  28.4 us (23%)
  local copies, waits for them, and re-layouts  3.76 us (3%)
  other arithmetic  2.56 us (2%)
    ppermute x12, waiting for transfers between devices, round_ring(): return lax.ppermute(array, AX, ring_perm(turn, step))  44 us
    pallas_call x8, Pallas kernels, chunk_part(): pl.pallas_call(functools.partial(chunk_kernel, halves=halves, own=own, ad...  23.3 us
    ppermute x12, starting transfers between devices, round_ring(): return lax.ppermute(array, AX, ring_perm(turn, step))  15.5 us
    ppermute x6, starting transfers between devices, swapped(): return lax.ppermute(array, CORE, [(0, 1), (1, 0)])  14.9 us
    all_to_all x1, starting transfers between devices, on_device(): lax.all_to_all(message, SAME_CORE, split_axis=0, concat_axis=0, tiled=True)  5.88 us
    all_to_all x1, waiting for transfers between devices, on_device(): lax.all_to_all(message, SAME_CORE, split_axis=0, concat_axis=0, tiled=True)  3.51 us
    pallas_call x1, Pallas kernels, prepare(): pl.pallas_call(prepare_kernel, out_shape=[jax.ShapeDtypeStruct((2048, 153...  2.8 us
  transfers between devices with their start and end apart: 19, of which 10 were waited for; matrix products, arithmetic and copies ran while one was open for 1% of the time, Pallas kernels for 13%

profile of v2, /device:TPU:1, one launch (start us, length us, event | category | flops | bytes accessed | tf_op | source)
XLA Modules:
  0.0 120.3 jit_solution(2674883239576276175)
XLA Ops:
  0.7 2.2 %copy-done.2 = bf16[2,512,2048]{2,1,0:T(8,128)(2,1)S(1)} copy-done((bf16[2,512,2048]{2,1,0:T(8,128)(2,1)S(1)}, bf16[2,512,2048]{2,1,0:T(8,128)(2,1)}, u32[]{:S(2)}) %copy-start.2) | copy-done | bytes 4194328
  2.9 2.8 %prepare.1 = (bf16[2048,1536]{1,0:T(8,128)(2,1)S(1)}, bf16[1024,1024]{1,0:T(8,128)(2,1)S(1)}, bf16[1024,1024]{1,0:T(8,128)(2,1)S(1)}) custom-call(s32[4]{0:T(128)S(1)} %pad_add_fusion.1.pos_ref, bf16[2,512,2048]{2,1,0:T(8,128)(2,1)S(1)} %copy-done.2), custom_call_target="tpu_custom_call" | custom-call | flops 2000000000 | bytes 14680064 | tf_op jit(solution)/shard_map/prepare/pallas_call | solution.py:59
  5.7 2.9 %other.4.refs_0_ = f32[512,1024]{1,0:T(8,128)S(1)} custom-call(s32[4]{0:T(128)S(1)} %pad_add_fusion.1.pos_ref, bf16[2048,1536]{1,0:T(8,128)(2,1)S(1)} %get-tuple-element.20.lt_ref, bf16[1024,1024]{1,0:T(8,128)(2,1)S(1)} %get-tuple-element.22.w_ref), custom_call_target="tpu_custom_call" | custom-call | flops 2147483648 | bytes 8388608 | tf_op jit(solution)/shard_map/other/pallas_call | solution.py:139
  8.6 1.5 %collective-permute-start = (f32[512,1024]{1,0:T(8,128)S(1)}, f32[512,1024]{1,0:T(8,128)S(1)}, u32[]{:S(2)}, u32[]{:S(2)}) collective-permute-start(f32[512,1024]{1,0:T(8,128)S(1)} %other.4.refs_0_), channel_id=1, source_target_pairs={{0,8},{8,0},{1,9},{9,1},{2,10},{10,2},{3,11},{11,3},{4,12},{12,4},... | collective-permute-start | bytes 6291464 | tf_op jit(solution)/shard_map/ppermute | solution.py:39
  10.1 2.9 %own.4 = (f32[256,1024]{1,0:T(8,128)S(1)}, f32[256,1024]{1,0:T(8,128)S(1)}) custom-call(s32[4]{0:T(128)S(1)} %pad_add_fusion.1.pos_ref, bf16[2048,1536]{1,0:T(8,128)(2,1)S(1)} %get-tuple-element.20.lt_ref, bf16[1024,1024]{1,0:T(8,128)(2,1)S(1)} %get-tuple-element.21.w_ref, f32[512,1024]{1,0:T(8,128)S(1)} %other.4.refs_0_), custom_call_target="tpu_custom_call" | custom-call | flops 2147483648 | bytes 8388608 | tf_op jit(solution)/shard_map/own/pallas_call | solution.py:139
  13.0 0.9 collective-permute-done
  13.9 0.4 slice_add_fusion
  14.3 2.9 %other.5.refs_0_ = f32[512,1024]{1,0:T(8,128)S(1)} custom-call(s32[4]{0:T(128)S(1)} %pad_add_fusion.1.pos_ref, bf16[2048,1536]{1,0:T(8,128)(2,1)S(1)} %get-tuple-element.20.lt_ref, bf16[1024,1024]{1,0:T(8,128)(2,1)S(1)} %get-tuple-element.22.w_ref, f32[256,1024]{1,0:T(8,128)S(1)} %get-tuple-element.45.refs_0_), custom_call_target="tpu_custom_call" | custom-call | flops 2147483648 | bytes 8388608 | tf_op jit(solution)/shard_map/other/pallas_call | solution.py:139
  17.2 0.5 collective-permute-start.1
  17.7 2.9 %other.6.refs_0_ = f32[512,1024]{1,0:T(8,128)S(1)} custom-call(s32[4]{0:T(128)S(1)} %pad_add_fusion.1.pos_ref, bf16[2048,1536]{1,0:T(8,128)(2,1)S(1)} %get-tuple-element.20.lt_ref, bf16[1024,1024]{1,0:T(8,128)(2,1)S(1)} %get-tuple-element.22.w_ref, f32[512,1024]{1,0:T(8,128)S(1)} %other.5.refs_0_), custom_call_target="tpu_custom_call" | custom-call | flops 2147483648 | bytes 8388608 | tf_op jit(solution)/shard_map/other/pallas_call | solution.py:139
  20.6 0.2 collective-permute-start.2
  20.8 1.4 %collective-permute-start.4 = (f32[256,1024]{1,0:T(8,128)S(1)}, f32[256,1024]{1,0:T(8,128)S(1)}, u32[]{:S(2)}, u32[]{:S(2)}) collective-permute-start(f32[256,1024]{1,0:T(8,128)S(1)} %get-tuple-element.45.refs_0_), channel_id=1, source_target_pairs={{0,32},{8,10},{1,33},{9,11},{16,48},{24,26},{17,49},{25,27},{2,34}... | collective-permute-start | bytes 3145736 | tf_op jit(solution)/shard_map/ppermute | solution.py:35
  22.2 1.6 %collective-permute-start.8 = (f32[256,1024]{1,0:T(8,128)S(1)}, f32[256,1024]{1,0:T(8,128)S(1)}, u32[]{:S(2)}, u32[]{:S(2)}) collective-permute-start(f32[256,1024]{1,0:T(8,128)S(1)} %get-tuple-element.44), channel_id=1, source_target_pairs={{0,96},{8,14},{1,97},{9,15},{16,112},{24,30},{17,113},{25,31},{2,9... | collective-permute-start | bytes 3145736 | tf_op jit(solution)/shard_map/ppermute | solution.py:35
  23.9 2.9 %own.5 = (f32[256,1024]{1,0:T(8,128)S(1)}, f32[256,1024]{1,0:T(8,128)S(1)}) custom-call(s32[4]{0:T(128)S(1)} %pad_add_fusion.1.pos_ref, bf16[2048,1536]{1,0:T(8,128)(2,1)S(1)} %get-tuple-element.20.lt_ref, bf16[1024,1024]{1,0:T(8,128)(2,1)S(1)} %get-tuple-element.21.w_ref, f32[512,1024]{1,0:T(8,128)S(1)} %other.6.refs_0_, ...), custom_call_target="tpu_custom_call" | custom-call | flops 2147483648 | bytes 8388608 | tf_op jit(solution)/shard_map/own/pallas_call | solution.py:139
  26.8 2.9 %other.7.refs_0_ = f32[512,1024]{1,0:T(8,128)S(1)} custom-call(s32[4]{0:T(128)S(1)} %pad_add_fusion.1.pos_ref, bf16[2048,1536]{1,0:T(8,128)(2,1)S(1)} %get-tuple-element.20.lt_ref, bf16[1024,1024]{1,0:T(8,128)(2,1)S(1)} %get-tuple-element.22.w_ref, f32[256,1024]{1,0:T(8,128)S(1)} %get-tuple-element.24.refs_0_), custom_call_target="tpu_custom_call" | custom-call | flops 2147483648 | bytes 8388608 | tf_op jit(solution)/shard_map/other/pallas_call | solution.py:139
  29.7 0.6 collective-permute-start.3
  30.4 1.4 %collective-permute-start.6 = (f32[256,1024]{1,0:T(8,128)S(1)}, f32[256,1024]{1,0:T(8,128)S(1)}, u32[]{:S(2)}, u32[]{:S(2)}) collective-permute-start(f32[256,1024]{1,0:T(8,128)S(1)} %get-tuple-element.24.refs_0_), channel_id=1, source_target_pairs={{0,32},{8,10},{1,33},{9,11},{16,48},{24,26},{17,49},{25,27},{2,34}... | collective-permute-start | bytes 3145736 | tf_op jit(solution)/shard_map/ppermute | solution.py:35
  31.8 2.9 %own.6 = (f32[256,1024]{1,0:T(8,128)S(1)}, f32[256,1024]{1,0:T(8,128)S(1)}) custom-call(s32[4]{0:T(128)S(1)} %pad_add_fusion.1.pos_ref, bf16[2048,1536]{1,0:T(8,128)(2,1)S(1)} %get-tuple-element.20.lt_ref, bf16[1024,1024]{1,0:T(8,128)(2,1)S(1)} %get-tuple-element.21.w_ref, f32[512,1024]{1,0:T(8,128)S(1)} %other.7.refs_0_, ...), custom_call_target="tpu_custom_call" | custom-call | flops 2147483648 | bytes 8388608 | tf_op jit(solution)/shard_map/own/pallas_call | solution.py:139
  34.7 1.4 %collective-permute-done.4 = f32[256,1024]{1,0:T(8,128)S(1)} collective-permute-done((f32[256,1024]{1,0:T(8,128)S(1)}, f32[256,1024]{1,0:T(8,128)S(1)}, u32[]{:S(2)}, u32[]{:S(2)}) %collective-permute-start.4) | collective-permute-done | bytes 1048608 | tf_op jit(solution)/shard_map/ppermute | solution.py:35
  36.1 0.2 add.114
  36.4 2.7 %collective-permute-start.7 = (f32[256,1024]{1,0:T(8,128)S(1)}, f32[256,1024]{1,0:T(8,128)S(1)}, u32[]{:S(2)}, u32[]{:S(2)}) collective-permute-start(f32[256,1024]{1,0:T(8,128)S(1)} %get-tuple-element.27), channel_id=1, source_target_pairs={{0,96},{8,14},{1,97},{9,15},{16,112},{24,30},{17,113},{25,31},{2,9... | collective-permute-start | bytes 3145736 | tf_op jit(solution)/shard_map/ppermute | solution.py:35
  39.2 0.3 collective-permute-start.9
  39.5 19.1 %collective-permute-done.5 = f32[256,1024]{1,0:T(8,128)S(1)} collective-permute-done((f32[256,1024]{1,0:T(8,128)S(1)}, f32[256,1024]{1,0:T(8,128)S(1)}, u32[]{:S(2)}, u32[]{:S(2)}) %collective-permute-start.5) | collective-permute-done | bytes 1048608 | tf_op jit(solution)/shard_map/ppermute | solution.py:35
  58.6 3.4 %collective-permute-done.9 = f32[256,1024]{1,0:T(8,128)S(1)} collective-permute-done((f32[256,1024]{1,0:T(8,128)S(1)}, f32[256,1024]{1,0:T(8,128)S(1)}, u32[]{:S(2)}, u32[]{:S(2)}) %collective-permute-start.9) | collective-permute-done | bytes 1048608 | tf_op jit(solution)/shard_map/ppermute | solution.py:35
  62.0 2.9 %own.7 = (f32[256,1024]{1,0:T(8,128)S(1)}, f32[256,1024]{1,0:T(8,128)S(1)}) custom-call(s32[4]{0:T(128)S(1)} %pad_add_fusion.1.pos_ref, bf16[2048,1536]{1,0:T(8,128)(2,1)S(1)} %get-tuple-element.20.lt_ref, bf16[1024,1024]{1,0:T(8,128)(2,1)S(1)} %get-tuple-element.21.w_ref, f32[256,1024]{1,0:T(8,128)S(1)} %get-tuple-element.25.refs_0_, ...), custom_call_target="tpu_custom_call" | custom-call | flops 2147483648 | bytes 8388608 | tf_op jit(solution)/shard_map/own/pallas_call | solution.py:139
  65.0 0.3 slice_add_fusion.3
  65.3 3.8 %collective-permute-start.12 = (f32[128,1024]{1,0:T(8,128)S(1)}, f32[128,1024]{1,0:T(8,128)S(1)}, u32[]{:S(2)}, u32[]{:S(2)}) collective-permute-start(f32[128,1024]{1,0:T(8,128)S(1)} %get-tuple-element.40), channel_id=1, source_target_pairs={{0,6},{8,25},{1,7},{9,8},{16,22},{24,9},{17,23},{25,24},{2,0},{10,... | collective-permute-start | bytes 1572872 | tf_op jit(solution)/shard_map/ppermute | solution.py:35
  69.1 0.3 slice_add_fusion.5
  69.5 0.8 collective-permute-start.10
  70.2 10.7 %collective-permute-done.12 = f32[128,1024]{1,0:T(8,128)S(1)} collective-permute-done((f32[128,1024]{1,0:T(8,128)S(1)}, f32[128,1024]{1,0:T(8,128)S(1)}, u32[]{:S(2)}, u32[]{:S(2)}) %collective-permute-start.12) | collective-permute-done | bytes 524320 | tf_op jit(solution)/shard_map/ppermute | solution.py:35
  80.9 3.7 %collective-permute-done.10 = f32[128,1024]{1,0:T(8,128)S(1)} collective-permute-done((f32[128,1024]{1,0:T(8,128)S(1)}, f32[128,1024]{1,0:T(8,128)S(1)}, u32[]{:S(2)}, u32[]{:S(2)}) %collective-permute-start.10) | collective-permute-done | bytes 524320 | tf_op jit(solution)/shard_map/ppermute | solution.py:35
  84.7 2.5 %collective-permute-start.15 = (f32[32,1024]{1,0:T(8,128)S(1)}, f32[32,1024]{1,0:T(8,128)S(1)}, u32[]{:S(2)}, u32[]{:S(2)}) collective-permute-start(f32[32,1024]{1,0:T(8,128)S(1)} %get-tuple-element.42), channel_id=1, source_target_pairs={{0,17},{8,104},{1,0},{9,105},{16,1},{24,120},{17,16},{25,121},{2,1... | collective-permute-start | bytes 393224 | tf_op jit(solution)/shard_map/ppermute | solution.py:35
  87.2 0.2 collective-permute-start.14
  87.5 0.6 collective-permute-start.13
  88.2 2.4 %collective-permute-done.15 = f32[32,1024]{1,0:T(8,128)S(1)} collective-permute-done((f32[32,1024]{1,0:T(8,128)S(1)}, f32[32,1024]{1,0:T(8,128)S(1)}, u32[]{:S(2)}, u32[]{:S(2)}) %collective-permute-start.15) | collective-permute-done | bytes 131104 | tf_op jit(solution)/shard_map/ppermute | solution.py:35
  90.6 2.1 %collective-permute-done.14 = f32[32,1024]{1,0:T(8,128)S(1)} collective-permute-done((f32[32,1024]{1,0:T(8,128)S(1)}, f32[32,1024]{1,0:T(8,128)S(1)}, u32[]{:S(2)}, u32[]{:S(2)}) %collective-permute-start.14) | collective-permute-done | bytes 131104 | tf_op jit(solution)/shard_map/ppermute | solution.py:35
  92.7 1.2 %collective-permute-done.13 = f32[32,1024]{1,0:T(8,128)S(1)} collective-permute-done((f32[32,1024]{1,0:T(8,128)S(1)}, f32[32,1024]{1,0:T(8,128)S(1)}, u32[]{:S(2)}, u32[]{:S(2)}) %collective-permute-start.13) | collective-permute-done | bytes 131104 | tf_op jit(solution)/shard_map/ppermute | solution.py:35
  94.0 0.4 reshape.14
  94.3 0.3 copy.10
  94.7 0.8 pauli.1
  95.5 0.2 maximum_bitcast_fusion
  95.7 0.8 copy.11
  96.5 5.9 %all-to-all-start = ((f32[64,1,768]{2,1,0:T(1,128)}), f32[64,1,768]{2,1,0:T(1,128)S(1)}, u32[]{:S(2)}, u32[]{:S(2)}) async-start(f32[64,1,768]{2,1,0:T(1,128)} %copy.11), calls=%async_computation | async-start | bytes 393216 | tf_op jit(solution)/shard_map/all_to_all | solution.py:308
  102.4 5.5 %collective-permute-start.16 = (f32[16,1024]{1,0:T(8,128)S(1)}, f32[16,1024]{1,0:T(8,128)S(1)}, u32[]{:S(2)}, u32[]{:S(2)}) collective-permute-start(f32[16,1024]{1,0:T(8,128)S(1)} %get-tuple-element.46), channel_id=1, source_target_pairs={{0,8},{8,0},{1,9},{9,1},{2,10},{10,2},{3,11},{11,3},{4,12},{12,4},... | collective-permute-start | bytes 196616 | tf_op jit(solution)/shard_map/ppermute | solution.py:39
  107.9 3.5 %all-to-all-done = f32[64,1,768]{2,1,0:T(1,128)S(1)} async-done(((f32[64,1,768]{2,1,0:T(1,128)}), f32[64,1,768]{2,1,0:T(1,128)S(1)}, u32[]{:S(2)}, u32[]{:S(2)}) %all-to-all-start) | async-done | bytes 196640 | tf_op jit(solution)/shard_map/all_to_all | solution.py:308
  111.5 6.6 %collective-permute-start.17 = (f32[200]{0:T(256)S(1)}, f32[200]{0:T(256)S(1)}, u32[]{:S(2)}, u32[]{:S(2)}) collective-permute-start(f32[200]{0:T(256)S(1)} %bitcast.26), channel_id=1, source_target_pairs={{0,8},{8,0},{1,9},{9,1},{2,10},{10,2},{3,11},{11,3},{4,12},{12,4},... | collective-permute-start | bytes 2408 | tf_op jit(solution)/shard_map/ppermute | solution.py:39
  118.2 1.5 %densities.1 = (f32[16,2048]{1,0:T(8,128)}, f32[16,2048]{1,0:T(8,128)}) custom-call(s32[2]{0:T(128)S(1)} %pad_add_fusion.place_ref, f32[16,1024]{1,0:T(8,128)S(1)} %get-tuple-element.47.keep_ref, f32[16,1024]{1,0:T(8,128)S(1)} %collective-permute-done.16.got_ref, f32[64,768]{1,0:T(8,128)S(1)} %bitcast.20), custom_call_target="tpu_custom_call" | custom-call | tf_op jit(solution)/shard_map/densities/pallas_call | solution.py:244
  119.7 0.6 pad_maximum_fusion
  (29 shorter events, 0.8 us)
Async XLA Ops:
  0.7 2.2 %copy-start.2 = (bf16[2,512,2048]{2,1,0:T(8,128)(2,1)S(1)}, bf16[2,512,2048]{2,1,0:T(8,128)(2,1)}, u32[]{:S(2)}) copy-start(bf16[2,512,2048]{2,1,0:T(8,128)(2,1)} %a_ref.1) | copy-start | bytes 12582916
  8.6 5.2 %collective-permute-start = (f32[512,1024]{1,0:T(8,128)S(1)}, f32[512,1024]{1,0:T(8,128)S(1)}, u32[]{:S(2)}, u32[]{:S(2)}) collective-permute-start(f32[512,1024]{1,0:T(8,128)S(1)} %other.4.refs_0_), channel_id=1, source_target_pairs={{0,8},{8,0},{1,9},{9,1},{2,10},{10,2},{3,11},{11,3},{4,12},{12,4},... | collective-permute-start | bytes 6291464 | tf_op jit(solution)/shard_map/ppermute | solution.py:39
  17.2 6.6 %collective-permute-start.1 = (f32[512,1024]{1,0:T(8,128)S(1)}, f32[512,1024]{1,0:T(8,128)S(1)}, u32[]{:S(2)}, u32[]{:S(2)}) collective-permute-start(f32[512,1024]{1,0:T(8,128)S(1)} %other.5.refs_0_), channel_id=1, source_target_pairs={{0,8},{8,0},{1,9},{9,1},{2,10},{10,2},{3,11},{11,3},{4,12},{12,4},... | collective-permute-start | bytes 6291464 | tf_op jit(solution)/shard_map/ppermute | solution.py:39
  20.6 11.2 %collective-permute-start.2 = (f32[512,1024]{1,0:T(8,128)S(1)}, f32[512,1024]{1,0:T(8,128)S(1)}, u32[]{:S(2)}, u32[]{:S(2)}) collective-permute-start(f32[512,1024]{1,0:T(8,128)S(1)} %other.6.refs_0_), channel_id=1, source_target_pairs={{0,8},{8,0},{1,9},{9,1},{2,10},{10,2},{3,11},{11,3},{4,12},{12,4},... | collective-permute-start | bytes 6291464 | tf_op jit(solution)/shard_map/ppermute | solution.py:39
  20.8 15.3 %collective-permute-start.4 = (f32[256,1024]{1,0:T(8,128)S(1)}, f32[256,1024]{1,0:T(8,128)S(1)}, u32[]{:S(2)}, u32[]{:S(2)}) collective-permute-start(f32[256,1024]{1,0:T(8,128)S(1)} %get-tuple-element.45.refs_0_), channel_id=1, source_target_pairs={{0,32},{8,10},{1,33},{9,11},{16,48},{24,26},{17,49},{25,27},{2,34}... | collective-permute-start | bytes 3145736 | tf_op jit(solution)/shard_map/ppermute | solution.py:35
  22.2 16.8 %collective-permute-start.8 = (f32[256,1024]{1,0:T(8,128)S(1)}, f32[256,1024]{1,0:T(8,128)S(1)}, u32[]{:S(2)}, u32[]{:S(2)}) collective-permute-start(f32[256,1024]{1,0:T(8,128)S(1)} %get-tuple-element.44), channel_id=1, source_target_pairs={{0,96},{8,14},{1,97},{9,15},{16,112},{24,30},{17,113},{25,31},{2,9... | collective-permute-start | bytes 3145736 | tf_op jit(solution)/shard_map/ppermute | solution.py:35
  29.7 32.3 %collective-permute-start.3 = (f32[512,1024]{1,0:T(8,128)S(1)}, f32[512,1024]{1,0:T(8,128)S(1)}, u32[]{:S(2)}, u32[]{:S(2)}) collective-permute-start(f32[512,1024]{1,0:T(8,128)S(1)} %other.7.refs_0_), channel_id=1, source_target_pairs={{0,8},{8,0},{1,9},{9,1},{2,10},{10,2},{3,11},{11,3},{4,12},{12,4},... | collective-permute-start | bytes 6291464 | tf_op jit(solution)/shard_map/ppermute | solution.py:39
  30.4 28.3 %collective-permute-start.6 = (f32[256,1024]{1,0:T(8,128)S(1)}, f32[256,1024]{1,0:T(8,128)S(1)}, u32[]{:S(2)}, u32[]{:S(2)}) collective-permute-start(f32[256,1024]{1,0:T(8,128)S(1)} %get-tuple-element.24.refs_0_), channel_id=1, source_target_pairs={{0,32},{8,10},{1,33},{9,11},{16,48},{24,26},{17,49},{25,27},{2,34}... | collective-permute-start | bytes 3145736 | tf_op jit(solution)/shard_map/ppermute | solution.py:35
  36.3 22.3 %collective-permute-start.5 = (f32[256,1024]{1,0:T(8,128)S(1)}, f32[256,1024]{1,0:T(8,128)S(1)}, u32[]{:S(2)}, u32[]{:S(2)}) collective-permute-start(f32[256,1024]{1,0:T(8,128)S(1)} %add.114), channel_id=1, source_target_pairs={{0,32},{8,10},{1,33},{9,11},{16,48},{24,26},{17,49},{25,27},{2,34}... | collective-permute-start | bytes 3145736 | tf_op jit(solution)/shard_map/ppermute | solution.py:35
  36.4 22.2 %collective-permute-start.7 = (f32[256,1024]{1,0:T(8,128)S(1)}, f32[256,1024]{1,0:T(8,128)S(1)}, u32[]{:S(2)}, u32[]{:S(2)}) collective-permute-start(f32[256,1024]{1,0:T(8,128)S(1)} %get-tuple-element.27), channel_id=1, source_target_pairs={{0,96},{8,14},{1,97},{9,15},{16,112},{24,30},{17,113},{25,31},{2,9... | collective-permute-start | bytes 3145736 | tf_op jit(solution)/shard_map/ppermute | solution.py:35
  39.2 22.8 %collective-permute-start.9 = (f32[256,1024]{1,0:T(8,128)S(1)}, f32[256,1024]{1,0:T(8,128)S(1)}, u32[]{:S(2)}, u32[]{:S(2)}) collective-permute-start(f32[256,1024]{1,0:T(8,128)S(1)} %add.116), channel_id=1, source_target_pairs={{0,96},{8,14},{1,97},{9,15},{16,112},{24,30},{17,113},{25,31},{2,9... | collective-permute-start | bytes 3145736 | tf_op jit(solution)/shard_map/ppermute | solution.py:35
  65.3 15.6 %collective-permute-start.12 = (f32[128,1024]{1,0:T(8,128)S(1)}, f32[128,1024]{1,0:T(8,128)S(1)}, u32[]{:S(2)}, u32[]{:S(2)}) collective-permute-start(f32[128,1024]{1,0:T(8,128)S(1)} %get-tuple-element.40), channel_id=1, source_target_pairs={{0,6},{8,25},{1,7},{9,8},{16,22},{24,9},{17,23},{25,24},{2,0},{10,... | collective-permute-start | bytes 1572872 | tf_op jit(solution)/shard_map/ppermute | solution.py:35
  69.1 11.7 %collective-permute-start.11 = (f32[128,1024]{1,0:T(8,128)S(1)}, f32[128,1024]{1,0:T(8,128)S(1)}, u32[]{:S(2)}, u32[]{:S(2)}) collective-permute-start(f32[128,1024]{1,0:T(8,128)S(1)} %get-tuple-element.39), channel_id=1, source_target_pairs={{0,4},{8,24},{1,5},{9,25},{16,20},{24,8},{17,21},{25,9},{2,6},{10,... | collective-permute-start | bytes 1572872 | tf_op jit(solution)/shard_map/ppermute | solution.py:35
  69.5 15.1 %collective-permute-start.10 = (f32[128,1024]{1,0:T(8,128)S(1)}, f32[128,1024]{1,0:T(8,128)S(1)}, u32[]{:S(2)}, u32[]{:S(2)}) collective-permute-start(f32[128,1024]{1,0:T(8,128)S(1)} %get-tuple-element.38), channel_id=1, source_target_pairs={{0,2},{8,9},{1,3},{9,24},{16,18},{24,25},{17,19},{25,8},{2,4},{10,... | collective-permute-start | bytes 1572872 | tf_op jit(solution)/shard_map/ppermute | solution.py:35
  84.7 10.0 %copy-start = (s32[200]{0:T(256)S(1)}, s32[200]{0:T(256)}, u32[]{:S(2)}) copy-start(s32[200]{0:T(256)} %param.5) | copy-start | bytes 2404
  84.7 10.0 %copy-start.1 = (s32[200]{0:T(256)S(1)}, s32[200]{0:T(256)}, u32[]{:S(2)}) copy-start(s32[200]{0:T(256)} %param.6) | copy-start | bytes 2404
  84.7 5.9 %collective-permute-start.15 = (f32[32,1024]{1,0:T(8,128)S(1)}, f32[32,1024]{1,0:T(8,128)S(1)}, u32[]{:S(2)}, u32[]{:S(2)}) collective-permute-start(f32[32,1024]{1,0:T(8,128)S(1)} %get-tuple-element.42), channel_id=1, source_target_pairs={{0,17},{8,104},{1,0},{9,105},{16,1},{24,120},{17,16},{25,121},{2,1... | collective-permute-start | bytes 393224 | tf_op jit(solution)/shard_map/ppermute | solution.py:35
  87.2 5.4 %collective-permute-start.14 = (f32[32,1024]{1,0:T(8,128)S(1)}, f32[32,1024]{1,0:T(8,128)S(1)}, u32[]{:S(2)}, u32[]{:S(2)}) collective-permute-start(f32[32,1024]{1,0:T(8,128)S(1)} %get-tuple-element.43), channel_id=1, source_target_pairs={{0,16},{8,72},{1,17},{9,73},{16,0},{24,88},{17,1},{25,89},{2,18},{... | collective-permute-start | bytes 393224 | tf_op jit(solution)/shard_map/ppermute | solution.py:35
  87.5 6.4 %collective-permute-start.13 = (f32[32,1024]{1,0:T(8,128)S(1)}, f32[32,1024]{1,0:T(8,128)S(1)}, u32[]{:S(2)}, u32[]{:S(2)}) collective-permute-start(f32[32,1024]{1,0:T(8,128)S(1)} %get-tuple-element.41), channel_id=1, source_target_pairs={{0,1},{8,40},{1,16},{9,41},{16,17},{24,56},{17,0},{25,57},{2,3},{1... | collective-permute-start | bytes 393224 | tf_op jit(solution)/shard_map/ppermute | solution.py:35
  94.3 25.4 %copy-start.3 = (s32[200]{0:T(256)S(1)}, s32[200]{0:T(256)}, u32[]{:S(2)}) copy-start(s32[200]{0:T(256)} %param.7) | copy-start | bytes 2404
  96.5 14.9 %all-to-all-start = ((f32[64,1,768]{2,1,0:T(1,128)}), f32[64,1,768]{2,1,0:T(1,128)S(1)}, u32[]{:S(2)}, u32[]{:S(2)}) async-start(f32[64,1,768]{2,1,0:T(1,128)} %copy.11), calls=%async_computation | async-start | bytes 393216 | tf_op jit(solution)/shard_map/all_to_all | solution.py:308
  102.4 15.8 %collective-permute-start.16 = (f32[16,1024]{1,0:T(8,128)S(1)}, f32[16,1024]{1,0:T(8,128)S(1)}, u32[]{:S(2)}, u32[]{:S(2)}) collective-permute-start(f32[16,1024]{1,0:T(8,128)S(1)} %get-tuple-element.46), channel_id=1, source_target_pairs={{0,8},{8,0},{1,9},{9,1},{2,10},{10,2},{3,11},{11,3},{4,12},{12,4},... | collective-permute-start | bytes 196616 | tf_op jit(solution)/shard_map/ppermute | solution.py:39
  111.5 8.2 %collective-permute-start.17 = (f32[200]{0:T(256)S(1)}, f32[200]{0:T(256)S(1)}, u32[]{:S(2)}, u32[]{:S(2)}) collective-permute-start(f32[200]{0:T(256)S(1)} %bitcast.26), channel_id=1, source_target_pairs={{0,8},{8,0},{1,9},{9,1},{2,10},{10,2},{3,11},{11,3},{4,12},{12,4},... | collective-permute-start | bytes 2408 | tf_op jit(solution)/shard_map/ppermute | solution.py:39

commit v3 on v2

--- a/solution.py
+++ b/solution.py
@@ -82,10 +82,8 @@
 CHUNKS = (((2, 0), (2, 1)), ((1, 1), (3, 0)), ((1, 0), (3, 1)), ((0, 0), (0, 1)))
 
 
-def chunk_kernel(pos_ref, lt_ref, w_ref, *refs, halves, own, adds, waits):
-    refs = refs[waits:]
-    recv_ref = refs[0] if adds else None
-    *outs, rows_ref, ids_ref = refs[1:] if adds else refs
+def chunk_kernel(pos_ref, lt_ref, w_ref, *refs, halves, own, waits):
+    *outs, rows_ref, ids_ref = refs[waits:]
     whose = pos_ref[3] if own else pos_ref[3] ^ 1
     lane = lax.broadcasted_iota(jnp.int32, (16, 128), 0)
     at = 0
@@ -111,8 +109,6 @@
             to = slice(tile * 256 + part * 128, tile * 256 + (part + 1) * 128)
             col = lax.broadcasted_iota(jnp.int32, (CHUNK, 128), 1) + ((tile * 2 + part) * 256 + whose * 128)
             value = jnp.where(ids_ref[...] >= col, real[:, here], imag[:, here])
-            if adds:
-                value = value + recv_ref[:, to]
             if own:
                 outs[0][:, to] = value[: CHUNK // 2]
                 outs[1][:, to] = value[CHUNK // 2 :]
@@ -120,24 +116,21 @@
                 outs[0][:, to] = value
 
 
-def chunk_part(pos, lt, w, halves, own, recv=None, waits=()):
-    adds = recv is not None
+def chunk_part(pos, lt, w, halves, own, waits=()):
     full = pl.BlockSpec((CHUNK, 1024), lambda i, p: (0, 0))
     half = pl.BlockSpec((CHUNK // 2, 1024), lambda i, p: (0, 0))
-    args = (pos, lt, w, *waits) + ((recv,) if adds else ())
+    args = (pos, lt, w, *waits)
     in_specs = [
         pl.BlockSpec((2048, 1536), lambda i, p: (0, 0)),
         pl.BlockSpec((1024, 1024), lambda i, p: (0, 0)),
         *[pl.BlockSpec(memory_space=pl.ANY) for _ in waits],
     ]
-    if adds:
-        in_specs.append(full)
     if own:
         out_shape = [jax.ShapeDtypeStruct((CHUNK // 2, 1024), jnp.float32)] * 2
     else:
         out_shape = jax.ShapeDtypeStruct((CHUNK, 1024), jnp.float32)
     return pl.pallas_call(
-        functools.partial(chunk_kernel, halves=halves, own=own, adds=adds, waits=len(waits)),
+        functools.partial(chunk_kernel, halves=halves, own=own, waits=len(waits)),
         out_shape=out_shape,
         grid_spec=pltpu.PrefetchScalarGridSpec(
             num_scalar_prefetch=1,
@@ -265,35 +258,46 @@
     make = functools.partial(chunk_part, pos, lt, w_own, own=True)
     send1 = send(CHUNKS[0])
     recv1 = swapped(send1)
-    far0, far1 = make(CHUNKS[0], waits=(send1,))
-    far0, far1 = far0 + recv1[: CHUNK // 2], far1 + recv1[CHUNK // 2 :]
+    far = make(CHUNKS[0], waits=(send1,))
+    far0, far1 = far[0] + recv1[:256], far[1] + recv1[256:]
     via_left = round_ring(far0, 0, 1)
     via_right = round_ring(far1, 0, -1)
     send2 = send(CHUNKS[1], waits=(far0,))
     recv2 = swapped(send2)
-    send3 = send(CHUNKS[2], waits=(send2,))
-    recv3 = swapped(send3)
-    right1, left0 = make(CHUNKS[1], recv=recv2, waits=(send3,))
+    near = make(CHUNKS[1], waits=(send2,))
+    right1, left0 = near[0] + recv2[:256], near[1] + recv2[256:]
     from_left1 = round_ring(right1, 0, 1)
     from_right0 = round_ring(left0, 0, -1)
-    send4 = send(CHUNKS[3], waits=(right1,))
+    send3 = send(CHUNKS[2], waits=(near[0],))
+    recv3 = swapped(send3)
+    near = make(CHUNKS[2], waits=(send3,))
+    from_left0 = round_ring(near[0] + recv3[:256] + via_left, 0, 1)
+    from_right1 = round_ring(near[1] + recv3[256:] + via_right, 0, -1)
+    send4 = send(CHUNKS[3], waits=(near[0],))
     recv4 = swapped(send4)
-    right0, left1 = make(CHUNKS[2], recv=recv3, waits=(send4,))
-    from_left0 = round_ring(right0 + via_left, 0, 1)
-    from_right1 = round_ring(left1 + via_right, 0, -1)
-    mine0, mine1 = make(CHUNKS[3], recv=recv4, waits=(right0,))
-    from_left0, from_left1, from_right0, from_right1 = lax.optimization_barrier(
-        (from_left0, from_left1, from_right0, from_right1)
+    mine = make(CHUNKS[3], waits=(send4,))
+    came = lax.optimization_barrier(((from_left0, from_right0), (from_left1, from_right1)))
+
+    def first_sum(came, half, at):
+        left, right = came[half]
+        here = slice(at, at + 64)
+        return (mine[half][here] + recv4[half * 256 + at : half * 256 + at + 64]) + (left[here] + right[here])
+
+    places = ((1, 0), (1, 64), (0, 192), (1, 128))
+    (far0, far1, right1, left0), came = lax.optimization_barrier(
+        (tuple(first_sum(came, *p) for p in places), came)
     )
-    rows = []
-    for mine, left, right in ((mine0, from_left0, from_right0), (mine1, from_left1, from_right1)):
-        rows += [mine[k : k + 128] + left[k : k + 128] + right[k : k + 128] for k in (0, 128)]
-    arrived = {}
-    for k in (2, 1, 3):
-        arrived[k] = round_ring(rows[k], 1, k)
-    rows = [
-        sum((arrived[m][k : k + 32] for m in (1, 2, 3)), rows[0][k : k + 32]) for k in (0, 32, 64, 96)
-    ]
+    via_left = round_ring(far0, 1, 1)
+    via_right = round_ring(far1, 1, -1)
+    from_left1 = round_ring(right1, 1, 1)
+    from_right0 = round_ring(left0, 1, -1)
+    places = ((0, 128), (1, 192), (0, 0), (0, 64))
+    right0, left1, low, high = lax.optimization_barrier(tuple(first_sum(came, *p) for p in places))
+    from_left0 = round_ring(right0 + via_left, 1, 1)
+    from_right1 = round_ring(left1 + via_right, 1, -1)
+    low = low + from_left0 + from_right0
+    high = high + from_left1 + from_right1
+    rows = [low[:32], low[32:], high[:32], high[32:]]
     arrived = {}
     for k in (2, 1, 3):
         arrived[k] = round_ring(rows[k], 2, k)

time: 121 us -> 120 us (level)
  waiting for transfers between devices: 48.4 us -> 42.4 us
  starting transfers between devices: 36.3 us -> 40.5 us
  other arithmetic: 2.56 us -> 3.85 us
    ppermute x12 -> x15, waiting for transfers between devices: 44 us -> 38.8 us  [round_ring(): return lax.ppermute(array, AX, ring_perm(turn, step))]
    ppermute x12 -> x15, starting transfers between devices: 15.5 us -> 19.4 us  [round_ring(): return lax.ppermute(array, AX, ring_perm(turn, step))]
    add x6 -> x9, other arithmetic: 1.48 us -> 2.79 us  [the longest x2 0.88 us: first_sum(): mine[half][here] + recv4[half * 256 + at:half * 256 + at + 64] + (left[he...]
  transfers between devices with their start and end apart: 19 -> 22, of which waited for: 10 -> 12; matrix products, arithmetic and copies ran while one was open for 1% -> 2% of each run, Pallas kernels for 13% -> 11%
where the time goes in v3:
time: 120 us
  waiting for transfers between devices  42.4 us (35%)
  starting transfers between devices  40.5 us (34%)
  Pallas kernels  28.6 us (24%)
  other arithmetic  3.85 us (3%)
  local copies, waits for them, and re-layouts  3.79 us (3%)
    ppermute x15, waiting for transfers between devices, round_ring(): return lax.ppermute(array, AX, ring_perm(turn, step))  38.8 us
    pallas_call x8, Pallas kernels, chunk_part(): pl.pallas_call(functools.partial(chunk_kernel, halves=halves, own=own, wa...  23.5 us
    ppermute x15, starting transfers between devices, round_ring(): return lax.ppermute(array, AX, ring_perm(turn, step))  19.4 us
    ppermute x6, starting transfers between devices, swapped(): return lax.ppermute(array, CORE, [(0, 1), (1, 0)])  16 us
    all_to_all x1, starting transfers between devices, on_device(): lax.all_to_all(message, SAME_CORE, split_axis=0, concat_axis=0, tiled=True)  5.13 us
    all_to_all x1, waiting for transfers between devices, on_device(): lax.all_to_all(message, SAME_CORE, split_axis=0, concat_axis=0, tiled=True)  2.82 us
    pallas_call x1, Pallas kernels, prepare(): pl.pallas_call(prepare_kernel, out_shape=[jax.ShapeDtypeStruct((2048, 153...  2.81 us
  transfers between devices with their start and end apart: 22, of which 12 were waited for; matrix products, arithmetic and copies ran while one was open for 2% of the time, Pallas kernels for 11%

profile of v3, /device:TPU:1, one launch (start us, length us, event | category | flops | bytes accessed | tf_op | source)
XLA Modules:
  0.0 120.1 jit_solution(13212390297834983339)
XLA Ops:
  0.7 2.2 %copy-done.2 = bf16[2,512,2048]{2,1,0:T(8,128)(2,1)S(1)} copy-done((bf16[2,512,2048]{2,1,0:T(8,128)(2,1)S(1)}, bf16[2,512,2048]{2,1,0:T(8,128)(2,1)}, u32[]{:S(2)}) %copy-start.2) | copy-done | bytes 4194328
  2.9 2.8 %prepare.1 = (bf16[2048,1536]{1,0:T(8,128)(2,1)S(1)}, bf16[1024,1024]{1,0:T(8,128)(2,1)S(1)}, bf16[1024,1024]{1,0:T(8,128)(2,1)S(1)}) custom-call(s32[4]{0:T(128)S(1)} %pad_add_fusion.1.pos_ref, bf16[2,512,2048]{2,1,0:T(8,128)(2,1)S(1)} %copy-done.2), custom_call_target="tpu_custom_call" | custom-call | flops 2000000000 | bytes 14680064 | tf_op jit(solution)/shard_map/prepare/pallas_call | solution.py:59
  5.7 2.9 %other.4.refs_0_ = f32[512,1024]{1,0:T(8,128)S(1)} custom-call(s32[4]{0:T(128)S(1)} %pad_add_fusion.1.pos_ref, bf16[2048,1536]{1,0:T(8,128)(2,1)S(1)} %get-tuple-element.32.lt_ref, bf16[1024,1024]{1,0:T(8,128)(2,1)S(1)} %get-tuple-element.34.w_ref), custom_call_target="tpu_custom_call" | custom-call | flops 2147483648 | bytes 8388608 | tf_op jit(solution)/shard_map/other/pallas_call | solution.py:132
  8.7 1.5 %collective-permute-start = (f32[512,1024]{1,0:T(8,128)S(1)}, f32[512,1024]{1,0:T(8,128)S(1)}, u32[]{:S(2)}, u32[]{:S(2)}) collective-permute-start(f32[512,1024]{1,0:T(8,128)S(1)} %other.4.refs_0_), channel_id=1, source_target_pairs={{0,8},{8,0},{1,9},{9,1},{2,10},{10,2},{3,11},{11,3},{4,12},{12,4},... | collective-permute-start | bytes 6291464 | tf_op jit(solution)/shard_map/ppermute | solution.py:39
  10.1 2.9 %own.4 = (f32[256,1024]{1,0:T(8,128)S(1)}, f32[256,1024]{1,0:T(8,128)S(1)}) custom-call(s32[4]{0:T(128)S(1)} %pad_add_fusion.1.pos_ref, bf16[2048,1536]{1,0:T(8,128)(2,1)S(1)} %get-tuple-element.32.lt_ref, bf16[1024,1024]{1,0:T(8,128)(2,1)S(1)} %get-tuple-element.33.w_ref, f32[512,1024]{1,0:T(8,128)S(1)} %other.4.refs_0_), custom_call_target="tpu_custom_call" | custom-call | flops 2147483648 | bytes 8388608 | tf_op jit(solution)/shard_map/own/pallas_call | solution.py:132
  13.1 0.8 collective-permute-done
  13.9 0.4 slice_add_fusion
  14.3 2.9 %other.5.refs_0_ = f32[512,1024]{1,0:T(8,128)S(1)} custom-call(s32[4]{0:T(128)S(1)} %pad_add_fusion.1.pos_ref, bf16[2048,1536]{1,0:T(8,128)(2,1)S(1)} %get-tuple-element.32.lt_ref, bf16[1024,1024]{1,0:T(8,128)(2,1)S(1)} %get-tuple-element.34.w_ref, f32[256,1024]{1,0:T(8,128)S(1)} %get-tuple-element.72.refs_0_), custom_call_target="tpu_custom_call" | custom-call | flops 2147483648 | bytes 8388608 | tf_op jit(solution)/shard_map/other/pallas_call | solution.py:132
  17.3 2.9 %own.5 = (f32[256,1024]{1,0:T(8,128)S(1)}, f32[256,1024]{1,0:T(8,128)S(1)}) custom-call(s32[4]{0:T(128)S(1)} %pad_add_fusion.1.pos_ref, bf16[2048,1536]{1,0:T(8,128)(2,1)S(1)} %get-tuple-element.32.lt_ref, bf16[1024,1024]{1,0:T(8,128)(2,1)S(1)} %get-tuple-element.33.w_ref, f32[512,1024]{1,0:T(8,128)S(1)} %other.5.refs_0_), custom_call_target="tpu_custom_call" | custom-call | flops 2147483648 | bytes 8388608 | tf_op jit(solution)/shard_map/own/pallas_call | solution.py:132
  20.2 2.9 %other.6.refs_0_ = f32[512,1024]{1,0:T(8,128)S(1)} custom-call(s32[4]{0:T(128)S(1)} %pad_add_fusion.1.pos_ref, bf16[2048,1536]{1,0:T(8,128)(2,1)S(1)} %get-tuple-element.32.lt_ref, bf16[1024,1024]{1,0:T(8,128)(2,1)S(1)} %get-tuple-element.34.w_ref, f32[256,1024]{1,0:T(8,128)S(1)} %get-tuple-element.36.refs_0_), custom_call_target="tpu_custom_call" | custom-call | flops 2147483648 | bytes 8388608 | tf_op jit(solution)/shard_map/other/pallas_call | solution.py:132
  23.2 0.5 collective-permute-start.2
  23.8 2.8 %collective-permute-start.8 = (f32[256,1024]{1,0:T(8,128)S(1)}, f32[256,1024]{1,0:T(8,128)S(1)}, u32[]{:S(2)}, u32[]{:S(2)}) collective-permute-start(f32[256,1024]{1,0:T(8,128)S(1)} %get-tuple-element.71), channel_id=1, source_target_pairs={{0,96},{8,14},{1,97},{9,15},{16,112},{24,30},{17,113},{25,31},{2,9... | collective-permute-start | bytes 3145736 | tf_op jit(solution)/shard_map/ppermute | solution.py:35
  26.6 2.9 %own.6 = (f32[256,1024]{1,0:T(8,128)S(1)}, f32[256,1024]{1,0:T(8,128)S(1)}) custom-call(s32[4]{0:T(128)S(1)} %pad_add_fusion.1.pos_ref, bf16[2048,1536]{1,0:T(8,128)(2,1)S(1)} %get-tuple-element.32.lt_ref, bf16[1024,1024]{1,0:T(8,128)(2,1)S(1)} %get-tuple-element.33.w_ref, f32[512,1024]{1,0:T(8,128)S(1)} %other.6.refs_0_), custom_call_target="tpu_custom_call" | custom-call | flops 2147483648 | bytes 8388608 | tf_op jit(solution)/shard_map/own/pallas_call | solution.py:132
  29.5 2.9 %other.7.refs_0_ = f32[512,1024]{1,0:T(8,128)S(1)} custom-call(s32[4]{0:T(128)S(1)} %pad_add_fusion.1.pos_ref, bf16[2048,1536]{1,0:T(8,128)(2,1)S(1)} %get-tuple-element.32.lt_ref, bf16[1024,1024]{1,0:T(8,128)(2,1)S(1)} %get-tuple-element.34.w_ref, f32[256,1024]{1,0:T(8,128)S(1)} %get-tuple-element.37.refs_0_), custom_call_target="tpu_custom_call" | custom-call | flops 2147483648 | bytes 8388608 | tf_op jit(solution)/shard_map/other/pallas_call | solution.py:132
  32.5 0.5 collective-permute-start.1
  33.0 5.4 %collective-permute-done.8 = f32[256,1024]{1,0:T(8,128)S(1)} collective-permute-done((f32[256,1024]{1,0:T(8,128)S(1)}, f32[256,1024]{1,0:T(8,128)S(1)}, u32[]{:S(2)}, u32[]{:S(2)}) %collective-permute-start.8) | collective-permute-done | bytes 1048608 | tf_op jit(solution)/shard_map/ppermute | solution.py:35
  38.3 3.4 %collective-permute-done.3 = f32[256,1024]{1,0:T(8,128)S(1)} collective-permute-done((f32[256,1024]{1,0:T(8,128)S(1)}, f32[256,1024]{1,0:T(8,128)S(1)}, u32[]{:S(2)}, u32[]{:S(2)}) %collective-permute-start.3) | collective-permute-done | bytes 1048608 | tf_op jit(solution)/shard_map/ppermute | solution.py:35
  41.8 0.9 fusion
  42.7 1.5 %collective-permute-start.4 = (f32[256,1024]{1,0:T(8,128)S(1)}, f32[256,1024]{1,0:T(8,128)S(1)}, u32[]{:S(2)}, u32[]{:S(2)}) collective-permute-start(f32[256,1024]{1,0:T(8,128)S(1)} %get-tuple-element.70), channel_id=1, source_target_pairs={{0,32},{8,10},{1,33},{9,11},{16,48},{24,26},{17,49},{25,27},{2,34}... | collective-permute-start | bytes 3145736 | tf_op jit(solution)/shard_map/ppermute | solution.py:35
  44.2 0.5 slice_add_fusion.2
  44.7 2.7 %collective-permute-start.6 = (f32[256,1024]{1,0:T(8,128)S(1)}, f32[256,1024]{1,0:T(8,128)S(1)}, u32[]{:S(2)}, u32[]{:S(2)}) collective-permute-start(f32[256,1024]{1,0:T(8,128)S(1)} %get-tuple-element.74), channel_id=1, source_target_pairs={{0,96},{8,14},{1,97},{9,15},{16,112},{24,30},{17,113},{25,31},{2,9... | collective-permute-start | bytes 3145736 | tf_op jit(solution)/shard_map/ppermute | solution.py:35
  47.4 2.9 %own.7 = (f32[256,1024]{1,0:T(8,128)S(1)}, f32[256,1024]{1,0:T(8,128)S(1)}) custom-call(s32[4]{0:T(128)S(1)} %pad_add_fusion.1.pos_ref, bf16[2048,1536]{1,0:T(8,128)(2,1)S(1)} %get-tuple-element.32.lt_ref, bf16[1024,1024]{1,0:T(8,128)(2,1)S(1)} %get-tuple-element.33.w_ref, f32[512,1024]{1,0:T(8,128)S(1)} %other.7.refs_0_), custom_call_target="tpu_custom_call" | custom-call | flops 2147483648 | bytes 8388608 | tf_op jit(solution)/shard_map/own/pallas_call | solution.py:132
  50.3 6.3 %collective-permute-done.9 = f32[256,1024]{1,0:T(8,128)S(1)} collective-permute-done((f32[256,1024]{1,0:T(8,128)S(1)}, f32[256,1024]{1,0:T(8,128)S(1)}, u32[]{:S(2)}, u32[]{:S(2)}) %collective-permute-start.9) | collective-permute-done | bytes 1048608 | tf_op jit(solution)/shard_map/ppermute | solution.py:35
  56.6 1.3 %collective-permute-done.4 = f32[256,1024]{1,0:T(8,128)S(1)} collective-permute-done((f32[256,1024]{1,0:T(8,128)S(1)}, f32[256,1024]{1,0:T(8,128)S(1)}, u32[]{:S(2)}, u32[]{:S(2)}) %collective-permute-start.4) | collective-permute-done | bytes 1048608 | tf_op jit(solution)/shard_map/ppermute | solution.py:35
  57.9 11.2 %collective-permute-done.7 = f32[256,1024]{1,0:T(8,128)S(1)} collective-permute-done((f32[256,1024]{1,0:T(8,128)S(1)}, f32[256,1024]{1,0:T(8,128)S(1)}, u32[]{:S(2)}, u32[]{:S(2)}) %collective-permute-start.7) | collective-permute-done | bytes 1048608 | tf_op jit(solution)/shard_map/ppermute | solution.py:35
  69.2 0.4 fusion.5
  69.6 1.7 %collective-permute-start.10 = (f32[64,1024]{1,0:T(8,128)S(1)}, f32[64,1024]{1,0:T(8,128)S(1)}, u32[]{:S(2)}, u32[]{:S(2)}) collective-permute-start(f32[64,1024]{1,0:T(8,128)S(1)} %get-tuple-element.53), channel_id=1, source_target_pairs={{0,2},{8,9},{1,3},{9,24},{16,18},{24,25},{17,19},{25,8},{2,4},{10,... | collective-permute-start | bytes 786440 | tf_op jit(solution)/shard_map/ppermute | solution.py:35
  71.3 2.2 %collective-permute-start.15 = (f32[64,1024]{1,0:T(8,128)S(1)}, f32[64,1024]{1,0:T(8,128)S(1)}, u32[]{:S(2)}, u32[]{:S(2)}) collective-permute-start(f32[64,1024]{1,0:T(8,128)S(1)} %get-tuple-element.58), channel_id=1, source_target_pairs={{0,6},{8,25},{1,7},{9,8},{16,22},{24,9},{17,23},{25,24},{2,0},{10,... | collective-permute-start | bytes 786440 | tf_op jit(solution)/shard_map/ppermute | solution.py:35
  73.5 0.4 fusion.2
  74.0 1.5 %collective-permute-start.12 = (f32[64,1024]{1,0:T(8,128)S(1)}, f32[64,1024]{1,0:T(8,128)S(1)}, u32[]{:S(2)}, u32[]{:S(2)}) collective-permute-start(f32[64,1024]{1,0:T(8,128)S(1)} %get-tuple-element.54), channel_id=1, source_target_pairs={{0,6},{8,25},{1,7},{9,8},{16,22},{24,9},{17,23},{25,24},{2,0},{10,... | collective-permute-start | bytes 786440 | tf_op jit(solution)/shard_map/ppermute | solution.py:35
  75.4 2.1 %collective-permute-done.10 = f32[64,1024]{1,0:T(8,128)S(1)} collective-permute-done((f32[64,1024]{1,0:T(8,128)S(1)}, f32[64,1024]{1,0:T(8,128)S(1)}, u32[]{:S(2)}, u32[]{:S(2)}) %collective-permute-start.10) | collective-permute-done | bytes 262176 | tf_op jit(solution)/shard_map/ppermute | solution.py:35
  77.6 0.7 collective-permute-start.14
  78.3 2.1 %collective-permute-start.16 = (f32[64,1024]{1,0:T(8,128)S(1)}, f32[64,1024]{1,0:T(8,128)S(1)}, u32[]{:S(2)}, u32[]{:S(2)}) collective-permute-start(f32[64,1024]{1,0:T(8,128)S(1)} %add.192), channel_id=1, source_target_pairs={{0,6},{8,25},{1,7},{9,8},{16,22},{24,9},{17,23},{25,24},{2,0},{10,... | collective-permute-start | bytes 786440 | tf_op jit(solution)/shard_map/ppermute | solution.py:35
  80.5 3.9 %collective-permute-done.11 = f32[64,1024]{1,0:T(8,128)S(1)} collective-permute-done((f32[64,1024]{1,0:T(8,128)S(1)}, f32[64,1024]{1,0:T(8,128)S(1)}, u32[]{:S(2)}, u32[]{:S(2)}) %collective-permute-start.11) | collective-permute-done | bytes 262176 | tf_op jit(solution)/shard_map/ppermute | solution.py:35
  84.4 0.7 collective-permute-start.13
  85.1 2.0 %collective-permute-done.14 = f32[64,1024]{1,0:T(8,128)S(1)} collective-permute-done((f32[64,1024]{1,0:T(8,128)S(1)}, f32[64,1024]{1,0:T(8,128)S(1)}, u32[]{:S(2)}, u32[]{:S(2)}) %collective-permute-start.14) | collective-permute-done | bytes 262176 | tf_op jit(solution)/shard_map/ppermute | solution.py:35
  87.3 2.3 %collective-permute-start.17 = (f32[32,1024]{1,0:T(8,128)S(1)}, f32[32,1024]{1,0:T(8,128)S(1)}, u32[]{:S(2)}, u32[]{:S(2)}) collective-permute-start(f32[32,1024]{1,0:T(8,128)S(1)} %get-tuple-element.75), channel_id=1, source_target_pairs={{0,16},{8,72},{1,17},{9,73},{16,0},{24,88},{17,1},{25,89},{2,18},{... | collective-permute-start | bytes 393224 | tf_op jit(solution)/shard_map/ppermute | solution.py:35
  89.6 1.0 collective-permute-start.18
  90.7 2.2 %collective-permute-done.17 = f32[32,1024]{1,0:T(8,128)S(1)} collective-permute-done((f32[32,1024]{1,0:T(8,128)S(1)}, f32[32,1024]{1,0:T(8,128)S(1)}, u32[]{:S(2)}, u32[]{:S(2)}) %collective-permute-start.17) | collective-permute-done | bytes 131104 | tf_op jit(solution)/shard_map/ppermute | solution.py:35
  92.9 0.9 collective-permute-done.18
  94.6 0.8 pauli.1
  95.6 0.8 copy.11
  96.4 5.1 %all-to-all-start = ((f32[64,1,768]{2,1,0:T(1,128)}), f32[64,1,768]{2,1,0:T(1,128)S(1)}, u32[]{:S(2)}, u32[]{:S(2)}) async-start(f32[64,1,768]{2,1,0:T(1,128)} %copy.11), calls=%async_computation | async-start | bytes 393216 | tf_op jit(solution)/shard_map/all_to_all | solution.py:312
  101.5 6.2 %collective-permute-start.19 = (f32[16,1024]{1,0:T(8,128)S(1)}, f32[16,1024]{1,0:T(8,128)S(1)}, u32[]{:S(2)}, u32[]{:S(2)}) collective-permute-start(f32[16,1024]{1,0:T(8,128)S(1)} %get-tuple-element.77), channel_id=1, source_target_pairs={{0,8},{8,0},{1,9},{9,1},{2,10},{10,2},{3,11},{11,3},{4,12},{12,4},... | collective-permute-start | bytes 196616 | tf_op jit(solution)/shard_map/ppermute | solution.py:39
  107.7 2.8 %all-to-all-done = f32[64,1,768]{2,1,0:T(1,128)S(1)} async-done(((f32[64,1,768]{2,1,0:T(1,128)}), f32[64,1,768]{2,1,0:T(1,128)S(1)}, u32[]{:S(2)}, u32[]{:S(2)}) %all-to-all-start) | async-done | bytes 196640 | tf_op jit(solution)/shard_map/all_to_all | solution.py:312
  110.6 7.3 %collective-permute-start.20 = (f32[200]{0:T(256)S(1)}, f32[200]{0:T(256)S(1)}, u32[]{:S(2)}, u32[]{:S(2)}) collective-permute-start(f32[200]{0:T(256)S(1)} %bitcast.26), channel_id=1, source_target_pairs={{0,8},{8,0},{1,9},{9,1},{2,10},{10,2},{3,11},{11,3},{4,12},{12,4},... | collective-permute-start | bytes 2408 | tf_op jit(solution)/shard_map/ppermute | solution.py:39
  118.0 1.5 %densities.1 = (f32[16,2048]{1,0:T(8,128)}, f32[16,2048]{1,0:T(8,128)}) custom-call(s32[2]{0:T(128)S(1)} %pad_add_fusion.place_ref, f32[16,1024]{1,0:T(8,128)S(1)} %get-tuple-element.78.keep_ref, f32[16,1024]{1,0:T(8,128)S(1)} %collective-permute-done.19.got_ref, f32[64,768]{1,0:T(8,128)S(1)} %bitcast.20), custom_call_target="tpu_custom_call" | custom-call | tf_op jit(solution)/shard_map/densities/pallas_call | solution.py:237
  119.5 0.6 pad_maximum_fusion
  (40 shorter events, 1.8 us)
Async XLA Ops:
  0.7 2.2 %copy-start.2 = (bf16[2,512,2048]{2,1,0:T(8,128)(2,1)S(1)}, bf16[2,512,2048]{2,1,0:T(8,128)(2,1)}, u32[]{:S(2)}) copy-start(bf16[2,512,2048]{2,1,0:T(8,128)(2,1)} %a_ref.1) | copy-start | bytes 12582916
  8.7 5.2 %collective-permute-start = (f32[512,1024]{1,0:T(8,128)S(1)}, f32[512,1024]{1,0:T(8,128)S(1)}, u32[]{:S(2)}, u32[]{:S(2)}) collective-permute-start(f32[512,1024]{1,0:T(8,128)S(1)} %other.4.refs_0_), channel_id=1, source_target_pairs={{0,8},{8,0},{1,9},{9,1},{2,10},{10,2},{3,11},{11,3},{4,12},{12,4},... | collective-permute-start | bytes 6291464 | tf_op jit(solution)/shard_map/ppermute | solution.py:39
  23.2 18.6 %collective-permute-start.2 = (f32[512,1024]{1,0:T(8,128)S(1)}, f32[512,1024]{1,0:T(8,128)S(1)}, u32[]{:S(2)}, u32[]{:S(2)}) collective-permute-start(f32[512,1024]{1,0:T(8,128)S(1)} %other.6.refs_0_), channel_id=1, source_target_pairs={{0,8},{8,0},{1,9},{9,1},{2,10},{10,2},{3,11},{11,3},{4,12},{12,4},... | collective-permute-start | bytes 6291464 | tf_op jit(solution)/shard_map/ppermute | solution.py:39
  23.6 20.6 %collective-permute-start.5 = (f32[512,1024]{1,0:T(8,128)S(1)}, f32[512,1024]{1,0:T(8,128)S(1)}, u32[]{:S(2)}, u32[]{:S(2)}) collective-permute-start(f32[512,1024]{1,0:T(8,128)S(1)} %other.5.refs_0_), channel_id=1, source_target_pairs={{0,8},{8,0},{1,9},{9,1},{2,10},{10,2},{3,11},{11,3},{4,12},{12,4},... | collective-permute-start | bytes 6291464 | tf_op jit(solution)/shard_map/ppermute | solution.py:39
  23.8 14.6 %collective-permute-start.8 = (f32[256,1024]{1,0:T(8,128)S(1)}, f32[256,1024]{1,0:T(8,128)S(1)}, u32[]{:S(2)}, u32[]{:S(2)}) collective-permute-start(f32[256,1024]{1,0:T(8,128)S(1)} %get-tuple-element.71), channel_id=1, source_target_pairs={{0,96},{8,14},{1,97},{9,15},{16,112},{24,30},{17,113},{25,31},{2,9... | collective-permute-start | bytes 3145736 | tf_op jit(solution)/shard_map/ppermute | solution.py:35
  26.6 15.2 %collective-permute-start.3 = (f32[256,1024]{1,0:T(8,128)S(1)}, f32[256,1024]{1,0:T(8,128)S(1)}, u32[]{:S(2)}, u32[]{:S(2)}) collective-permute-start(f32[256,1024]{1,0:T(8,128)S(1)} %get-tuple-element.72.refs_0_), channel_id=1, source_target_pairs={{0,32},{8,10},{1,33},{9,11},{16,48},{24,26},{17,49},{25,27},{2,34}... | collective-permute-start | bytes 3145736 | tf_op jit(solution)/shard_map/ppermute | solution.py:35
  32.5 36.7 %collective-permute-start.1 = (f32[512,1024]{1,0:T(8,128)S(1)}, f32[512,1024]{1,0:T(8,128)S(1)}, u32[]{:S(2)}, u32[]{:S(2)}) collective-permute-start(f32[512,1024]{1,0:T(8,128)S(1)} %other.7.refs_0_), channel_id=1, source_target_pairs={{0,8},{8,0},{1,9},{9,1},{2,10},{10,2},{3,11},{11,3},{4,12},{12,4},... | collective-permute-start | bytes 6291464 | tf_op jit(solution)/shard_map/ppermute | solution.py:39
  42.6 14.0 %collective-permute-start.9 = (f32[256,1024]{1,0:T(8,128)S(1)}, f32[256,1024]{1,0:T(8,128)S(1)}, u32[]{:S(2)}, u32[]{:S(2)}) collective-permute-start(f32[256,1024]{1,0:T(8,128)S(1)} %get-tuple-element.69), channel_id=1, source_target_pairs={{0,96},{8,14},{1,97},{9,15},{16,112},{24,30},{17,113},{25,31},{2,9... | collective-permute-start | bytes 3145736 | tf_op jit(solution)/shard_map/ppermute | solution.py:35
  42.7 15.2 %collective-permute-start.4 = (f32[256,1024]{1,0:T(8,128)S(1)}, f32[256,1024]{1,0:T(8,128)S(1)}, u32[]{:S(2)}, u32[]{:S(2)}) collective-permute-start(f32[256,1024]{1,0:T(8,128)S(1)} %get-tuple-element.70), channel_id=1, source_target_pairs={{0,32},{8,10},{1,33},{9,11},{16,48},{24,26},{17,49},{25,27},{2,34}... | collective-permute-start | bytes 3145736 | tf_op jit(solution)/shard_map/ppermute | solution.py:35
  44.7 24.5 %collective-permute-start.7 = (f32[256,1024]{1,0:T(8,128)S(1)}, f32[256,1024]{1,0:T(8,128)S(1)}, u32[]{:S(2)}, u32[]{:S(2)}) collective-permute-start(f32[256,1024]{1,0:T(8,128)S(1)} %get-tuple-element.73), channel_id=1, source_target_pairs={{0,32},{8,10},{1,33},{9,11},{16,48},{24,26},{17,49},{25,27},{2,34}... | collective-permute-start | bytes 3145736 | tf_op jit(solution)/shard_map/ppermute | solution.py:35
  44.7 24.4 %collective-permute-start.6 = (f32[256,1024]{1,0:T(8,128)S(1)}, f32[256,1024]{1,0:T(8,128)S(1)}, u32[]{:S(2)}, u32[]{:S(2)}) collective-permute-start(f32[256,1024]{1,0:T(8,128)S(1)} %get-tuple-element.74), channel_id=1, source_target_pairs={{0,96},{8,14},{1,97},{9,15},{16,112},{24,30},{17,113},{25,31},{2,9... | collective-permute-start | bytes 3145736 | tf_op jit(solution)/shard_map/ppermute | solution.py:35
  69.6 7.9 %collective-permute-start.10 = (f32[64,1024]{1,0:T(8,128)S(1)}, f32[64,1024]{1,0:T(8,128)S(1)}, u32[]{:S(2)}, u32[]{:S(2)}) collective-permute-start(f32[64,1024]{1,0:T(8,128)S(1)} %get-tuple-element.53), channel_id=1, source_target_pairs={{0,2},{8,9},{1,3},{9,24},{16,18},{24,25},{17,19},{25,8},{2,4},{10,... | collective-permute-start | bytes 786440 | tf_op jit(solution)/shard_map/ppermute | solution.py:35
  71.3 7.0 %collective-permute-start.15 = (f32[64,1024]{1,0:T(8,128)S(1)}, f32[64,1024]{1,0:T(8,128)S(1)}, u32[]{:S(2)}, u32[]{:S(2)}) collective-permute-start(f32[64,1024]{1,0:T(8,128)S(1)} %get-tuple-element.58), channel_id=1, source_target_pairs={{0,6},{8,25},{1,7},{9,8},{16,22},{24,9},{17,23},{25,24},{2,0},{10,... | collective-permute-start | bytes 786440 | tf_op jit(solution)/shard_map/ppermute | solution.py:35
  74.0 6.5 %collective-permute-start.12 = (f32[64,1024]{1,0:T(8,128)S(1)}, f32[64,1024]{1,0:T(8,128)S(1)}, u32[]{:S(2)}, u32[]{:S(2)}) collective-permute-start(f32[64,1024]{1,0:T(8,128)S(1)} %get-tuple-element.54), channel_id=1, source_target_pairs={{0,6},{8,25},{1,7},{9,8},{16,22},{24,9},{17,23},{25,24},{2,0},{10,... | collective-permute-start | bytes 786440 | tf_op jit(solution)/shard_map/ppermute | solution.py:35
  77.6 6.8 %collective-permute-start.11 = (f32[64,1024]{1,0:T(8,128)S(1)}, f32[64,1024]{1,0:T(8,128)S(1)}, u32[]{:S(2)}, u32[]{:S(2)}) collective-permute-start(f32[64,1024]{1,0:T(8,128)S(1)} %add.187), channel_id=1, source_target_pairs={{0,2},{8,9},{1,3},{9,24},{16,18},{24,25},{17,19},{25,8},{2,4},{10,... | collective-permute-start | bytes 786440 | tf_op jit(solution)/shard_map/ppermute | solution.py:35
  77.6 9.5 %collective-permute-start.14 = (f32[64,1024]{1,0:T(8,128)S(1)}, f32[64,1024]{1,0:T(8,128)S(1)}, u32[]{:S(2)}, u32[]{:S(2)}) collective-permute-start(f32[64,1024]{1,0:T(8,128)S(1)} %get-tuple-element.56), channel_id=1, source_target_pairs={{0,2},{8,9},{1,3},{9,24},{16,18},{24,25},{17,19},{25,8},{2,4},{10,... | collective-permute-start | bytes 786440 | tf_op jit(solution)/shard_map/ppermute | solution.py:35
  78.3 8.8 %collective-permute-start.16 = (f32[64,1024]{1,0:T(8,128)S(1)}, f32[64,1024]{1,0:T(8,128)S(1)}, u32[]{:S(2)}, u32[]{:S(2)}) collective-permute-start(f32[64,1024]{1,0:T(8,128)S(1)} %add.192), channel_id=1, source_target_pairs={{0,6},{8,25},{1,7},{9,8},{16,22},{24,9},{17,23},{25,24},{2,0},{10,... | collective-permute-start | bytes 786440 | tf_op jit(solution)/shard_map/ppermute | solution.py:35
  84.4 6.2 %collective-permute-start.13 = (f32[32,1024]{1,0:T(8,128)S(1)}, f32[32,1024]{1,0:T(8,128)S(1)}, u32[]{:S(2)}, u32[]{:S(2)}) collective-permute-start(f32[32,1024]{1,0:T(8,128)S(1)} %slice.191), channel_id=1, source_target_pairs={{0,1},{8,40},{1,16},{9,41},{16,17},{24,56},{17,0},{25,57},{2,3},{1... | collective-permute-start | bytes 393224 | tf_op jit(solution)/shard_map/ppermute | solution.py:35
  87.2 7.3 %copy-start = (s32[200]{0:T(256)S(1)}, s32[200]{0:T(256)}, u32[]{:S(2)}) copy-start(s32[200]{0:T(256)} %param.5) | copy-start | bytes 2404
  87.2 7.3 %copy-start.1 = (s32[200]{0:T(256)S(1)}, s32[200]{0:T(256)}, u32[]{:S(2)}) copy-start(s32[200]{0:T(256)} %param.6) | copy-start | bytes 2404
  87.3 5.6 %collective-permute-start.17 = (f32[32,1024]{1,0:T(8,128)S(1)}, f32[32,1024]{1,0:T(8,128)S(1)}, u32[]{:S(2)}, u32[]{:S(2)}) collective-permute-start(f32[32,1024]{1,0:T(8,128)S(1)} %get-tuple-element.75), channel_id=1, source_target_pairs={{0,16},{8,72},{1,17},{9,73},{16,0},{24,88},{17,1},{25,89},{2,18},{... | collective-permute-start | bytes 393224 | tf_op jit(solution)/shard_map/ppermute | solution.py:35
  89.6 4.3 %collective-permute-start.18 = (f32[32,1024]{1,0:T(8,128)S(1)}, f32[32,1024]{1,0:T(8,128)S(1)}, u32[]{:S(2)}, u32[]{:S(2)}) collective-permute-start(f32[32,1024]{1,0:T(8,128)S(1)} %get-tuple-element.76), channel_id=1, source_target_pairs={{0,17},{8,104},{1,0},{9,105},{16,1},{24,120},{17,16},{25,121},{2,1... | collective-permute-start | bytes 393224 | tf_op jit(solution)/shard_map/ppermute | solution.py:35
  94.2 25.3 %copy-start.3 = (s32[200]{0:T(256)S(1)}, s32[200]{0:T(256)}, u32[]{:S(2)}) copy-start(s32[200]{0:T(256)} %param.7) | copy-start | bytes 2404
  96.4 14.2 %all-to-all-start = ((f32[64,1,768]{2,1,0:T(1,128)}), f32[64,1,768]{2,1,0:T(1,128)S(1)}, u32[]{:S(2)}, u32[]{:S(2)}) async-start(f32[64,1,768]{2,1,0:T(1,128)} %copy.11), calls=%async_computation | async-start | bytes 393216 | tf_op jit(solution)/shard_map/all_to_all | solution.py:312
  101.5 16.4 %collective-permute-start.19 = (f32[16,1024]{1,0:T(8,128)S(1)}, f32[16,1024]{1,0:T(8,128)S(1)}, u32[]{:S(2)}, u32[]{:S(2)}) collective-permute-start(f32[16,1024]{1,0:T(8,128)S(1)} %get-tuple-element.77), channel_id=1, source_target_pairs={{0,8},{8,0},{1,9},{9,1},{2,10},{10,2},{3,11},{11,3},{4,12},{12,4},... | collective-permute-start | bytes 196616 | tf_op jit(solution)/shard_map/ppermute | solution.py:39
  110.6 8.9 %collective-permute-start.20 = (f32[200]{0:T(256)S(1)}, f32[200]{0:T(256)S(1)}, u32[]{:S(2)}, u32[]{:S(2)}) collective-permute-start(f32[200]{0:T(256)S(1)} %bitcast.26), channel_id=1, source_target_pairs={{0,8},{8,0},{1,9},{9,1},{2,10},{10,2},{3,11},{11,3},{4,12},{12,4},... | collective-permute-start | bytes 2408 | tf_op jit(solution)/shard_map/ppermute | solution.py:39

commit v4 on v3

--- a/solution.py
+++ b/solution.py
@@ -25,7 +25,7 @@
             for z in range(4):
                 for core in range(2):
                     to = [x, y, z]
-                    axis = (turn + core) % 3
+                    axis = (turn + 1 + core) % 3
                     to[axis] = (to[axis] + step) % 4
                     pairs.append((device_index(x, y, z, core), device_index(*to, core)))
     return pairs
@@ -39,20 +39,32 @@
     return lax.ppermute(array, CORE, [(0, 1), (1, 0)])
 
 
-def prepare_kernel(pos_ref, a_ref, lt_ref, own_ref, other_ref):
+STEPS = 8
+
+
+def prepare_kernel(pos_ref, amps_ref, lt_ref, own_ref, other_ref, a_ref, sems):
     core = pos_ref[3]
-    for block in range(16):
-        cols = slice(block * 128, (block + 1) * 128)
-        re = a_ref[0, :, cols].T
-        im = a_ref[1, :, cols].T
-        lt_ref[cols, 0:512] = re
-        lt_ref[cols, 512:1024] = im
-        lt_ref[cols, 1024:1536] = -re
-    for block in range(8):
-        cols = slice(block * 128, (block + 1) * 128)
-        for ref, which in ((own_ref, core), (other_ref, core ^ 1)):
-            from_cols = pl.ds(pl.multiple_of(block * 256 + which * 128, 128), 128)
-            ref[:, cols] = a_ref[:, :, from_cols].reshape(1024, 128)
+    width = 2048 // STEPS
+    copies = []
+    for step in range(STEPS):
+        cols = slice(step * width, (step + 1) * width)
+        copy = pltpu.make_async_copy(amps_ref.at[:, :, cols], a_ref.at[:, :, cols], sems.at[step])
+        copy.start()
+        copies.append(copy)
+    for step in range(STEPS):
+        copies[step].wait()
+        for block in range(step * width // 128, (step + 1) * width // 128):
+            cols = slice(block * 128, (block + 1) * 128)
+            re = a_ref[0, :, cols].T
+            im = a_ref[1, :, cols].T
+            lt_ref[cols, 0:512] = re
+            lt_ref[cols, 512:1024] = im
+            lt_ref[cols, 1024:1536] = -re
+        for block in range(step * width // 256, (step + 1) * width // 256):
+            cols = slice(block * 128, (block + 1) * 128)
+            for ref, which in ((own_ref, core), (other_ref, core ^ 1)):
+                from_cols = pl.ds(pl.multiple_of(block * 256 + which * 128, 128), 128)
+                ref[:, cols] = a_ref[:, :, from_cols].reshape(1024, 128)
 
 
 def prepare(pos, amps):
@@ -66,85 +78,90 @@
         grid_spec=pltpu.PrefetchScalarGridSpec(
             num_scalar_prefetch=1,
             grid=(1,),
-            in_specs=[pl.BlockSpec((2, 512, 2048), lambda i, p: (0, 0, 0))],
+            in_specs=[pl.BlockSpec(memory_space=pltpu.HBM)],
             out_specs=[
                 pl.BlockSpec((2048, 1536), lambda i, p: (0, 0)),
                 pl.BlockSpec((1024, 1024), lambda i, p: (0, 0)),
                 pl.BlockSpec((1024, 1024), lambda i, p: (0, 0)),
             ],
-        ),
-        compiler_params=pltpu.CompilerParams(vmem_limit_bytes=20 * 2**20),
+            scratch_shapes=[pltpu.VMEM((2, 512, 2048), jnp.bfloat16), pltpu.SemaphoreType.DMA((STEPS,))],
+        ),
+        compiler_params=pltpu.CompilerParams(vmem_limit_bytes=26 * 2**20),
         cost_estimate=pl.CostEstimate(flops=2 * 10**9, bytes_accessed=14 * 2**20, transcendentals=0),
         name="prepare",
-    )(pos, amps)
+    )(pos, pltpu.with_memory_space_constraint(amps, pltpu.HBM))
 
 
 CHUNKS = (((2, 0), (2, 1)), ((1, 1), (3, 0)), ((1, 0), (3, 1)), ((0, 0), (0, 1)))
 
 
 def chunk_kernel(pos_ref, lt_ref, w_ref, *refs, halves, own, waits):
-    *outs, rows_ref, ids_ref = refs[waits:]
+    out_ref, rows_ref, ids_ref = refs[waits:]
     whose = pos_ref[3] if own else pos_ref[3] ^ 1
+    first = whose == 0
+    x0, y0, z0 = pos_ref[0], pos_ref[1], pos_ref[2]
     lane = lax.broadcasted_iota(jnp.int32, (16, 128), 0)
-    at = 0
-    for k1, half in halves:
-        for k2 in (2 * half, 2 * half + 1):
-            for k3 in range(4):
-                ahead = [(k1, k2, k3), (k3, k1, k2)]
-                x, y, z = [
-                    (pos_ref[n] + jnp.where(whose == 0, ahead[0][n], ahead[1][n])) & 3 for n in range(3)
-                ]
-                base = x * 512 + (z >> 1) * 256 + y * 32 + (z & 1) * 16
-                for co in range(2):
-                    row = pl.multiple_of(base + co * 128, 16)
-                    rows_ref[at : at + 16, :] = lt_ref[pl.ds(row, 16), :]
-                    ids_ref[at : at + 16, :] = lane + row
-                    at += 16
+    col = lax.broadcasted_iota(jnp.int32, (1, 256), 1)
+    col = jnp.where(col >= 128, col + 128, col) + whose * 128
+    to = []
+    for x in range(4):
+        kx = (x - x0) & 3
+        pick = (kx >> 1) ^ halves[0][1]
+        k1_there = jnp.where(pick == 0, halves[0][0], halves[1][0])
+        for s in range(4):
+            h, j = divmod(s, 2)
+            k1, half = halves[h]
+            y = jnp.where(first, (y0 + k1) & 3, s)
+            z = jnp.where(first, z0 + 2 * half + j, z0 + k1_there) & 3
+            here = h * 256 + j * 128 + kx * 32
+            there = pick * 256 + (kx & 1) * 128 + ((s - y0) & 3) * 32
+            to.append(pl.multiple_of(jnp.where(first, here, there), 32))
+            base = x * 512 + (z >> 1) * 256 + y * 32 + (z & 1) * 16
+            for co in range(2):
+                at = x * 128 + s * 32 + co * 16
+                row = pl.multiple_of(base + co * 128, 16)
+                rows_ref[at : at + 16, :] = lt_ref[pl.ds(row, 16), :]
+                ids_ref[at : at + 16, :] = lane + row
     for tile in range(4):
         cols = slice(tile * 256, (tile + 1) * 256)
-        real = jnp.dot(rows_ref[:, 0:1024], w_ref[:, cols], preferred_element_type=jnp.float32)
-        imag = jnp.dot(rows_ref[:, 512:1536], w_ref[:, cols], preferred_element_type=jnp.float32)
-        for part in range(2):
-            here = slice(part * 128, (part + 1) * 128)
-            to = slice(tile * 256 + part * 128, tile * 256 + (part + 1) * 128)
-            col = lax.broadcasted_iota(jnp.int32, (CHUNK, 128), 1) + ((tile * 2 + part) * 256 + whose * 128)
-            value = jnp.where(ids_ref[...] >= col, real[:, here], imag[:, here])
-            if own:
-                outs[0][:, to] = value[: CHUNK // 2]
-                outs[1][:, to] = value[CHUNK // 2 :]
+        w = w_ref[:, cols]
+        real = jnp.dot(rows_ref[tile * 128 :, 0:1024], w, preferred_element_type=jnp.float32)
+        imag = jnp.dot(rows_ref[: (tile + 1) * 128, 512:1536], w, preferred_element_type=jnp.float32)
+        for x in range(4):
+            if x > tile:
+                value = real[(x - tile) * 128 : (x - tile + 1) * 128]
+            elif x < tile:
+                value = imag[x * 128 : (x + 1) * 128]
             else:
-                outs[0][:, to] = value
+                ids = ids_ref[x * 128 : (x + 1) * 128, :]
+                lower = jnp.concatenate([ids, ids], 1) >= col + tile * 512
+                value = jnp.where(lower, real[:128], imag[x * 128 :])
+            for s in range(4):
+                out_ref[pl.ds(to[x * 4 + s], 32), cols] = value[s * 32 : (s + 1) * 32]
 
 
 def chunk_part(pos, lt, w, halves, own, waits=()):
     full = pl.BlockSpec((CHUNK, 1024), lambda i, p: (0, 0))
-    half = pl.BlockSpec((CHUNK // 2, 1024), lambda i, p: (0, 0))
-    args = (pos, lt, w, *waits)
-    in_specs = [
-        pl.BlockSpec((2048, 1536), lambda i, p: (0, 0)),
-        pl.BlockSpec((1024, 1024), lambda i, p: (0, 0)),
-        *[pl.BlockSpec(memory_space=pl.ANY) for _ in waits],
-    ]
-    if own:
-        out_shape = [jax.ShapeDtypeStruct((CHUNK // 2, 1024), jnp.float32)] * 2
-    else:
-        out_shape = jax.ShapeDtypeStruct((CHUNK, 1024), jnp.float32)
     return pl.pallas_call(
         functools.partial(chunk_kernel, halves=halves, own=own, waits=len(waits)),
-        out_shape=out_shape,
+        out_shape=jax.ShapeDtypeStruct((CHUNK, 1024), jnp.float32),
         grid_spec=pltpu.PrefetchScalarGridSpec(
             num_scalar_prefetch=1,
             grid=(1,),
-            in_specs=in_specs,
-            out_specs=[half] * 2 if own else full,
+            in_specs=[
+                pl.BlockSpec((2048, 1536), lambda i, p: (0, 0)),
+                pl.BlockSpec((1024, 1024), lambda i, p: (0, 0)),
+                *[pl.BlockSpec(memory_space=pl.ANY) for _ in waits],
+            ],
+            out_specs=full,
             scratch_shapes=[pltpu.VMEM((CHUNK, 1536), jnp.bfloat16), pltpu.VMEM((CHUNK, 128), jnp.int32)],
         ),
         compiler_params=pltpu.CompilerParams(vmem_limit_bytes=12 * 2**20),
         cost_estimate=pl.CostEstimate(
-            flops=4 * CHUNK * 1024 * 1024, bytes_accessed=2**20 * 8, transcendentals=0
+            flops=5 * CHUNK * 512 * 1024, bytes_accessed=2**20 * 8, transcendentals=0
         ),
         name="own" if own else "other",
-    )(*args)
+    )(pos, lt, w, *waits)
 
 
 def parity_sign(values, masks):
@@ -259,21 +276,21 @@
     send1 = send(CHUNKS[0])
     recv1 = swapped(send1)
     far = make(CHUNKS[0], waits=(send1,))
-    far0, far1 = far[0] + recv1[:256], far[1] + recv1[256:]
+    far0, far1 = far[:256] + recv1[:256], far[256:] + recv1[256:]
     via_left = round_ring(far0, 0, 1)
     via_right = round_ring(far1, 0, -1)
     send2 = send(CHUNKS[1], waits=(far0,))
     recv2 = swapped(send2)
     near = make(CHUNKS[1], waits=(send2,))
-    right1, left0 = near[0] + recv2[:256], near[1] + recv2[256:]
+    right1, left0 = near[:256] + recv2[:256], near[256:] + recv2[256:]
     from_left1 = round_ring(right1, 0, 1)
     from_right0 = round_ring(left0, 0, -1)
-    send3 = send(CHUNKS[2], waits=(near[0],))
+    send3 = send(CHUNKS[2], waits=(near,))
     recv3 = swapped(send3)
     near = make(CHUNKS[2], waits=(send3,))
-    from_left0 = round_ring(near[0] + recv3[:256] + via_left, 0, 1)
-    from_right1 = round_ring(near[1] + recv3[256:] + via_right, 0, -1)
-    send4 = send(CHUNKS[3], waits=(near[0],))
+    from_left0 = round_ring(near[:256] + recv3[:256] + via_left, 0, 1)
+    from_right1 = round_ring(near[256:] + recv3[256:] + via_right, 0, -1)
+    send4 = send(CHUNKS[3], waits=(near,))
     recv4 = swapped(send4)
     mine = make(CHUNKS[3], waits=(send4,))
     came = lax.optimization_barrier(((from_left0, from_right0), (from_left1, from_right1)))
@@ -281,7 +298,8 @@
     def first_sum(came, half, at):
         left, right = came[half]
         here = slice(at, at + 64)
-        return (mine[half][here] + recv4[half * 256 + at : half * 256 + at + 64]) + (left[here] + right[here])
+        there = slice(half * 256 + at, half * 256 + at + 64)
+        return (mine[there] + recv4[there]) + (left[here] + right[here])
 
     places = ((1, 0), (1, 64), (0, 192), (1, 128))
     (far0, far1, right1, left0), came = lax.optimization_barrier(

time: 120 us -> 112 us (0.933)
  Pallas kernels: 28.6 us -> 23.8 us
  local copies, waits for them, and re-layouts: 3.79 us -> 1.6 us
  waiting for transfers between devices: 42.4 us -> 40.6 us
    pallas_call x8, Pallas kernels: 23.5 us -> 17.1 us  [chunk_part(): pl.pallas_call(functools.partial(chunk_kernel, halves=halves, own=own, wa...]
    ppermute x15, waiting for transfers between devices: 38.8 us -> 34.9 us  [round_ring(): return lax.ppermute(array, AX, ring_perm(turn, step))]
    ppermute x15, starting transfers between devices: 19.4 us -> 22.7 us  [round_ring(): return lax.ppermute(array, AX, ring_perm(turn, step))]
    ppermute x6, starting transfers between devices: 16 us -> 13.1 us  [swapped(): return lax.ppermute(array, CORE, [(0, 1), (1, 0)])]
    unnamed x9 -> x7, local copies, waits for them, and re-layouts: 2.22 us -> 0.03 us
    pallas_call x1, Pallas kernels: 2.81 us -> 4.44 us  [prepare(): pl.pallas_call(prepare_kernel, out_shape=[jax.ShapeDtypeStruct((2048, 153...]
    all_to_all x1, waiting for transfers between devices: 2.82 us -> 4.04 us  [on_device(): lax.all_to_all(message, SAME_CORE, split_axis=0, concat_axis=0, tiled=True)]
  transfers between devices with their start and end apart: 22 -> 22, of which waited for: 12 -> 11; matrix products, arithmetic and copies ran while one was open for 2% -> 2% of each run, Pallas kernels for 11% -> 13%
where the time goes in v4:
time: 112 us
  starting transfers between devices  41.1 us (37%)
  waiting for transfers between devices  40.6 us (36%)
  Pallas kernels  23.8 us (21%)
  other arithmetic  3.77 us (3%)
  local copies, waits for them, and re-layouts  1.6 us (1%)
    ppermute x15, waiting for transfers between devices, round_ring(): return lax.ppermute(array, AX, ring_perm(turn, step))  34.9 us
    ppermute x15, starting transfers between devices, round_ring(): return lax.ppermute(array, AX, ring_perm(turn, step))  22.7 us
    pallas_call x8, Pallas kernels, chunk_part(): pl.pallas_call(functools.partial(chunk_kernel, halves=halves, own=own, wa...  17.1 us
    ppermute x6, starting transfers between devices, swapped(): return lax.ppermute(array, CORE, [(0, 1), (1, 0)])  13.1 us
    all_to_all x1, starting transfers between devices, on_device(): lax.all_to_all(message, SAME_CORE, split_axis=0, concat_axis=0, tiled=True)  5.24 us
    pallas_call x1, Pallas kernels, prepare(): pl.pallas_call(prepare_kernel, out_shape=[jax.ShapeDtypeStruct((2048, 153...  4.44 us
    all_to_all x1, waiting for transfers between devices, on_device(): lax.all_to_all(message, SAME_CORE, split_axis=0, concat_axis=0, tiled=True)  4.04 us
  transfers between devices with their start and end apart: 22, of which 11 were waited for; matrix products, arithmetic and copies ran while one was open for 2% of the time, Pallas kernels for 13%

profile of v4, /device:TPU:1, one launch (start us, length us, event | category | flops | bytes accessed | tf_op | source)
XLA Modules:
  0.0 111.8 jit_solution(10354421874522036416)
XLA Ops:
  0.7 4.4 %prepare.1 = (bf16[2048,1536]{1,0:T(8,128)(2,1)S(1)}, bf16[1024,1024]{1,0:T(8,128)(2,1)S(1)}, bf16[1024,1024]{1,0:T(8,128)(2,1)S(1)}) custom-call(s32[4]{0:T(128)S(1)} %pad_add_fusion.1.pos_ref, bf16[2,512,2048]{2,1,0:T(8,128)(2,1)} %amps_ref.1), custom_call_target="tpu_custom_call" | custom-call | flops 2000000000 | bytes 14680064 | tf_op jit(solution)/shard_map/prepare/pallas_call | solution.py:71
  5.2 2.1 %other.4.refs_0_ = f32[512,1024]{1,0:T(8,128)S(1)} custom-call(s32[4]{0:T(128)S(1)} %pad_add_fusion.1.pos_ref, bf16[2048,1536]{1,0:T(8,128)(2,1)S(1)} %get-tuple-element.24.lt_ref, bf16[1024,1024]{1,0:T(8,128)(2,1)S(1)} %get-tuple-element.26.w_ref), custom_call_target="tpu_custom_call" | custom-call | flops 1342177280 | bytes 8388608 | tf_op jit(solution)/shard_map/other/pallas_call | solution.py:145
  7.3 1.3 %collective-permute-start = (f32[512,1024]{1,0:T(8,128)S(1)}, f32[512,1024]{1,0:T(8,128)S(1)}, u32[]{:S(2)}, u32[]{:S(2)}) collective-permute-start(f32[512,1024]{1,0:T(8,128)S(1)} %other.4.refs_0_), channel_id=1, source_target_pairs={{0,8},{8,0},{1,9},{9,1},{2,10},{10,2},{3,11},{11,3},{4,12},{12,4},... | collective-permute-start | bytes 6291464 | tf_op jit(solution)/shard_map/ppermute | solution.py:39
  8.6 2.1 %own.4 = f32[512,1024]{1,0:T(8,128)S(1)} custom-call(s32[4]{0:T(128)S(1)} %pad_add_fusion.1.pos_ref, bf16[2048,1536]{1,0:T(8,128)(2,1)S(1)} %get-tuple-element.24.lt_ref, bf16[1024,1024]{1,0:T(8,128)(2,1)S(1)} %get-tuple-element.25.w_ref, f32[512,1024]{1,0:T(8,128)S(1)} %other.4.refs_0_), custom_call_target="tpu_custom_call" | custom-call | flops 1342177280 | bytes 8388608 | tf_op jit(solution)/shard_map/own/pallas_call | solution.py:145
  10.7 1.6 %collective-permute-done = f32[512,1024]{1,0:T(8,128)S(1)} collective-permute-done((f32[512,1024]{1,0:T(8,128)S(1)}, f32[512,1024]{1,0:T(8,128)S(1)}, u32[]{:S(2)}, u32[]{:S(2)}) %collective-permute-start) | collective-permute-done | bytes 2097184 | tf_op jit(solution)/shard_map/ppermute | solution.py:39
  12.4 0.5 slice_add_fusion
  12.9 2.1 %other.5.refs_0_ = f32[512,1024]{1,0:T(8,128)S(1)} custom-call(s32[4]{0:T(128)S(1)} %pad_add_fusion.1.pos_ref, bf16[2048,1536]{1,0:T(8,128)(2,1)S(1)} %get-tuple-element.24.lt_ref, bf16[1024,1024]{1,0:T(8,128)(2,1)S(1)} %get-tuple-element.26.w_ref, f32[256,1024]{1,0:T(8,128)S(1)} %get-tuple-element.56.refs_0_), custom_call_target="tpu_custom_call" | custom-call | flops 1342177280 | bytes 8388608 | tf_op jit(solution)/shard_map/other/pallas_call | solution.py:145
  15.0 0.5 collective-permute-start.5
  15.5 2.1 %own.5.refs_0_ = f32[512,1024]{1,0:T(8,128)S(1)} custom-call(s32[4]{0:T(128)S(1)} %pad_add_fusion.1.pos_ref, bf16[2048,1536]{1,0:T(8,128)(2,1)S(1)} %get-tuple-element.24.lt_ref, bf16[1024,1024]{1,0:T(8,128)(2,1)S(1)} %get-tuple-element.25.w_ref, f32[512,1024]{1,0:T(8,128)S(1)} %other.5.refs_0_), custom_call_target="tpu_custom_call" | custom-call | flops 1342177280 | bytes 8388608 | tf_op jit(solution)/shard_map/own/pallas_call | solution.py:145
  17.6 2.1 %other.6.refs_0_ = f32[512,1024]{1,0:T(8,128)S(1)} custom-call(s32[4]{0:T(128)S(1)} %pad_add_fusion.1.pos_ref, bf16[2048,1536]{1,0:T(8,128)(2,1)S(1)} %get-tuple-element.24.lt_ref, bf16[1024,1024]{1,0:T(8,128)(2,1)S(1)} %get-tuple-element.26.w_ref, f32[512,1024]{1,0:T(8,128)S(1)} %own.5.refs_0_), custom_call_target="tpu_custom_call" | custom-call | flops 1342177280 | bytes 8388608 | tf_op jit(solution)/shard_map/other/pallas_call | solution.py:145
  20.0 1.8 %collective-permute-start.3 = (f32[256,1024]{1,0:T(8,128)S(1)}, f32[256,1024]{1,0:T(8,128)S(1)}, u32[]{:S(2)}, u32[]{:S(2)}) collective-permute-start(f32[256,1024]{1,0:T(8,128)S(1)} %get-tuple-element.56.refs_0_), channel_id=1, source_target_pairs={{0,2},{8,9},{1,3},{9,24},{16,18},{24,25},{17,19},{25,8},{2,4},{10,... | collective-permute-start | bytes 3145736 | tf_op jit(solution)/shard_map/ppermute | solution.py:35
  21.7 2.3 %collective-permute-start.8 = (f32[256,1024]{1,0:T(8,128)S(1)}, f32[256,1024]{1,0:T(8,128)S(1)}, u32[]{:S(2)}, u32[]{:S(2)}) collective-permute-start(f32[256,1024]{1,0:T(8,128)S(1)} %get-tuple-element.55), channel_id=1, source_target_pairs={{0,6},{8,25},{1,7},{9,8},{16,22},{24,9},{17,23},{25,24},{2,0},{10,... | collective-permute-start | bytes 3145736 | tf_op jit(solution)/shard_map/ppermute | solution.py:35
  24.1 2.1 %own.6.refs_0_ = f32[512,1024]{1,0:T(8,128)S(1)} custom-call(s32[4]{0:T(128)S(1)} %pad_add_fusion.1.pos_ref, bf16[2048,1536]{1,0:T(8,128)(2,1)S(1)} %get-tuple-element.24.lt_ref, bf16[1024,1024]{1,0:T(8,128)(2,1)S(1)} %get-tuple-element.25.w_ref, f32[512,1024]{1,0:T(8,128)S(1)} %other.6.refs_0_), custom_call_target="tpu_custom_call" | custom-call | flops 1342177280 | bytes 8388608 | tf_op jit(solution)/shard_map/own/pallas_call | solution.py:145
  26.2 2.1 %other.7.refs_0_ = f32[512,1024]{1,0:T(8,128)S(1)} custom-call(s32[4]{0:T(128)S(1)} %pad_add_fusion.1.pos_ref, bf16[2048,1536]{1,0:T(8,128)(2,1)S(1)} %get-tuple-element.24.lt_ref, bf16[1024,1024]{1,0:T(8,128)(2,1)S(1)} %get-tuple-element.26.w_ref, f32[512,1024]{1,0:T(8,128)S(1)} %own.6.refs_0_), custom_call_target="tpu_custom_call" | custom-call | flops 1342177280 | bytes 8388608 | tf_op jit(solution)/shard_map/other/pallas_call | solution.py:145
  28.5 0.4 slice_add_fusion.2
  28.9 3.4 %collective-permute-start.6 = (f32[256,1024]{1,0:T(8,128)S(1)}, f32[256,1024]{1,0:T(8,128)S(1)}, u32[]{:S(2)}, u32[]{:S(2)}) collective-permute-start(f32[256,1024]{1,0:T(8,128)S(1)} %get-tuple-element.58), channel_id=1, source_target_pairs={{0,6},{8,25},{1,7},{9,8},{16,22},{24,9},{17,23},{25,24},{2,0},{10,... | collective-permute-start | bytes 3145736 | tf_op jit(solution)/shard_map/ppermute | solution.py:35
  32.4 3.7 %collective-permute-done.3 = f32[256,1024]{1,0:T(8,128)S(1)} collective-permute-done((f32[256,1024]{1,0:T(8,128)S(1)}, f32[256,1024]{1,0:T(8,128)S(1)}, u32[]{:S(2)}, u32[]{:S(2)}) %collective-permute-start.3) | collective-permute-done | bytes 1048608 | tf_op jit(solution)/shard_map/ppermute | solution.py:35
  36.1 0.7 fusion
  36.8 1.3 %collective-permute-start.4 = (f32[256,1024]{1,0:T(8,128)S(1)}, f32[256,1024]{1,0:T(8,128)S(1)}, u32[]{:S(2)}, u32[]{:S(2)}) collective-permute-start(f32[256,1024]{1,0:T(8,128)S(1)} %get-tuple-element.54), channel_id=1, source_target_pairs={{0,2},{8,9},{1,3},{9,24},{16,18},{24,25},{17,19},{25,8},{2,4},{10,... | collective-permute-start | bytes 3145736 | tf_op jit(solution)/shard_map/ppermute | solution.py:35
  38.1 2.0 %collective-permute-start.9 = (f32[256,1024]{1,0:T(8,128)S(1)}, f32[256,1024]{1,0:T(8,128)S(1)}, u32[]{:S(2)}, u32[]{:S(2)}) collective-permute-start(f32[256,1024]{1,0:T(8,128)S(1)} %get-tuple-element.53), channel_id=1, source_target_pairs={{0,6},{8,25},{1,7},{9,8},{16,22},{24,9},{17,23},{25,24},{2,0},{10,... | collective-permute-start | bytes 3145736 | tf_op jit(solution)/shard_map/ppermute | solution.py:35
  40.1 2.1 %own.7 = f32[512,1024]{1,0:T(8,128)S(1)} custom-call(s32[4]{0:T(128)S(1)} %pad_add_fusion.1.pos_ref, bf16[2048,1536]{1,0:T(8,128)(2,1)S(1)} %get-tuple-element.24.lt_ref, bf16[1024,1024]{1,0:T(8,128)(2,1)S(1)} %get-tuple-element.25.w_ref, f32[512,1024]{1,0:T(8,128)S(1)} %other.7.refs_0_), custom_call_target="tpu_custom_call" | custom-call | flops 1342177280 | bytes 8388608 | tf_op jit(solution)/shard_map/own/pallas_call | solution.py:145
  42.3 4.8 %collective-permute-done.6 = f32[256,1024]{1,0:T(8,128)S(1)} collective-permute-done((f32[256,1024]{1,0:T(8,128)S(1)}, f32[256,1024]{1,0:T(8,128)S(1)}, u32[]{:S(2)}, u32[]{:S(2)}) %collective-permute-start.6) | collective-permute-done | bytes 1048608 | tf_op jit(solution)/shard_map/ppermute | solution.py:35
  47.1 4.1 %collective-permute-done.7 = f32[256,1024]{1,0:T(8,128)S(1)} collective-permute-done((f32[256,1024]{1,0:T(8,128)S(1)}, f32[256,1024]{1,0:T(8,128)S(1)}, u32[]{:S(2)}, u32[]{:S(2)}) %collective-permute-start.7) | collective-permute-done | bytes 1048608 | tf_op jit(solution)/shard_map/ppermute | solution.py:35
  51.2 11.2 %collective-permute-done.4 = f32[256,1024]{1,0:T(8,128)S(1)} collective-permute-done((f32[256,1024]{1,0:T(8,128)S(1)}, f32[256,1024]{1,0:T(8,128)S(1)}, u32[]{:S(2)}, u32[]{:S(2)}) %collective-permute-start.4) | collective-permute-done | bytes 1048608 | tf_op jit(solution)/shard_map/ppermute | solution.py:35
  62.5 0.4 fusion.5
  62.9 1.3 %collective-permute-start.10 = (f32[64,1024]{1,0:T(8,128)S(1)}, f32[64,1024]{1,0:T(8,128)S(1)}, u32[]{:S(2)}, u32[]{:S(2)}) collective-permute-start(f32[64,1024]{1,0:T(8,128)S(1)} %get-tuple-element.37), channel_id=1, source_target_pairs={{0,1},{8,40},{1,16},{9,41},{16,17},{24,56},{17,0},{25,57},{2,3},{1... | collective-permute-start | bytes 786440 | tf_op jit(solution)/shard_map/ppermute | solution.py:35
  64.2 1.4 %collective-permute-start.15 = (f32[64,1024]{1,0:T(8,128)S(1)}, f32[64,1024]{1,0:T(8,128)S(1)}, u32[]{:S(2)}, u32[]{:S(2)}) collective-permute-start(f32[64,1024]{1,0:T(8,128)S(1)} %get-tuple-element.42), channel_id=1, source_target_pairs={{0,17},{8,104},{1,0},{9,105},{16,1},{24,120},{17,16},{25,121},{2,1... | collective-permute-start | bytes 786440 | tf_op jit(solution)/shard_map/ppermute | solution.py:35
  65.6 0.5 fusion.2
  66.1 1.4 %collective-permute-start.12 = (f32[64,1024]{1,0:T(8,128)S(1)}, f32[64,1024]{1,0:T(8,128)S(1)}, u32[]{:S(2)}, u32[]{:S(2)}) collective-permute-start(f32[64,1024]{1,0:T(8,128)S(1)} %get-tuple-element.38), channel_id=1, source_target_pairs={{0,17},{8,104},{1,0},{9,105},{16,1},{24,120},{17,16},{25,121},{2,1... | collective-permute-start | bytes 786440 | tf_op jit(solution)/shard_map/ppermute | solution.py:35
  67.5 2.2 %collective-permute-done.10 = f32[64,1024]{1,0:T(8,128)S(1)} collective-permute-done((f32[64,1024]{1,0:T(8,128)S(1)}, f32[64,1024]{1,0:T(8,128)S(1)}, u32[]{:S(2)}, u32[]{:S(2)}) %collective-permute-start.10) | collective-permute-done | bytes 262176 | tf_op jit(solution)/shard_map/ppermute | solution.py:35
  69.8 0.9 collective-permute-start.14
  70.8 1.9 %collective-permute-start.16 = (f32[64,1024]{1,0:T(8,128)S(1)}, f32[64,1024]{1,0:T(8,128)S(1)}, u32[]{:S(2)}, u32[]{:S(2)}) collective-permute-start(f32[64,1024]{1,0:T(8,128)S(1)} %add.192), channel_id=1, source_target_pairs={{0,17},{8,104},{1,0},{9,105},{16,1},{24,120},{17,16},{25,121},{2,1... | collective-permute-start | bytes 786440 | tf_op jit(solution)/shard_map/ppermute | solution.py:35
  72.7 3.6 %collective-permute-done.11 = f32[64,1024]{1,0:T(8,128)S(1)} collective-permute-done((f32[64,1024]{1,0:T(8,128)S(1)}, f32[64,1024]{1,0:T(8,128)S(1)}, u32[]{:S(2)}, u32[]{:S(2)}) %collective-permute-start.11) | collective-permute-done | bytes 262176 | tf_op jit(solution)/shard_map/ppermute | solution.py:35
  76.3 1.4 %collective-permute-start.13 = (f32[32,1024]{1,0:T(8,128)S(1)}, f32[32,1024]{1,0:T(8,128)S(1)}, u32[]{:S(2)}, u32[]{:S(2)}) collective-permute-start(f32[32,1024]{1,0:T(8,128)S(1)} %slice.229), channel_id=1, source_target_pairs={{0,32},{8,10},{1,33},{9,11},{16,48},{24,26},{17,49},{25,27},{2,34}... | collective-permute-start | bytes 393224 | tf_op jit(solution)/shard_map/ppermute | solution.py:35
  77.7 1.7 %collective-permute-done.14 = f32[64,1024]{1,0:T(8,128)S(1)} collective-permute-done((f32[64,1024]{1,0:T(8,128)S(1)}, f32[64,1024]{1,0:T(8,128)S(1)}, u32[]{:S(2)}, u32[]{:S(2)}) %collective-permute-start.14) | collective-permute-done | bytes 262176 | tf_op jit(solution)/shard_map/ppermute | solution.py:35
  79.4 2.7 %collective-permute-start.17 = (f32[32,1024]{1,0:T(8,128)S(1)}, f32[32,1024]{1,0:T(8,128)S(1)}, u32[]{:S(2)}, u32[]{:S(2)}) collective-permute-start(f32[32,1024]{1,0:T(8,128)S(1)} %get-tuple-element.59), channel_id=1, source_target_pairs={{0,64},{8,12},{1,65},{9,13},{16,80},{24,28},{17,81},{25,29},{2,66}... | collective-permute-start | bytes 393224 | tf_op jit(solution)/shard_map/ppermute | solution.py:35
  82.1 0.8 collective-permute-start.18
  83.0 1.9 %collective-permute-done.17 = f32[32,1024]{1,0:T(8,128)S(1)} collective-permute-done((f32[32,1024]{1,0:T(8,128)S(1)}, f32[32,1024]{1,0:T(8,128)S(1)}, u32[]{:S(2)}, u32[]{:S(2)}) %collective-permute-start.17) | collective-permute-done | bytes 131104 | tf_op jit(solution)/shard_map/ppermute | solution.py:35
  84.9 1.7 %collective-permute-done.18 = f32[32,1024]{1,0:T(8,128)S(1)} collective-permute-done((f32[32,1024]{1,0:T(8,128)S(1)}, f32[32,1024]{1,0:T(8,128)S(1)}, u32[]{:S(2)}, u32[]{:S(2)}) %collective-permute-start.18) | collective-permute-done | bytes 131104 | tf_op jit(solution)/shard_map/ppermute | solution.py:35
  86.6 0.4 reshape.14
  87.4 0.8 pauli.1
  88.3 0.8 copy.11
  89.2 5.2 %all-to-all-start = ((f32[64,1,768]{2,1,0:T(1,128)}), f32[64,1,768]{2,1,0:T(1,128)S(1)}, u32[]{:S(2)}, u32[]{:S(2)}) async-start(f32[64,1,768]{2,1,0:T(1,128)} %copy.11), calls=%async_computation | async-start | bytes 393216 | tf_op jit(solution)/shard_map/all_to_all | solution.py:330
  94.4 5.0 %collective-permute-start.19 = (f32[16,1024]{1,0:T(8,128)S(1)}, f32[16,1024]{1,0:T(8,128)S(1)}, u32[]{:S(2)}, u32[]{:S(2)}) collective-permute-start(f32[16,1024]{1,0:T(8,128)S(1)} %get-tuple-element.61), channel_id=1, source_target_pairs={{0,8},{8,0},{1,9},{9,1},{2,10},{10,2},{3,11},{11,3},{4,12},{12,4},... | collective-permute-start | bytes 196616 | tf_op jit(solution)/shard_map/ppermute | solution.py:39
  99.4 4.0 %all-to-all-done = f32[64,1,768]{2,1,0:T(1,128)S(1)} async-done(((f32[64,1,768]{2,1,0:T(1,128)}), f32[64,1,768]{2,1,0:T(1,128)S(1)}, u32[]{:S(2)}, u32[]{:S(2)}) %all-to-all-start) | async-done | bytes 196640 | tf_op jit(solution)/shard_map/all_to_all | solution.py:330
  103.5 6.1 %collective-permute-start.20 = (f32[200]{0:T(256)S(1)}, f32[200]{0:T(256)S(1)}, u32[]{:S(2)}, u32[]{:S(2)}) collective-permute-start(f32[200]{0:T(256)S(1)} %bitcast.26), channel_id=1, source_target_pairs={{0,8},{8,0},{1,9},{9,1},{2,10},{10,2},{3,11},{11,3},{4,12},{12,4},... | collective-permute-start | bytes 2408 | tf_op jit(solution)/shard_map/ppermute | solution.py:39
  109.7 1.5 %densities.1 = (f32[16,2048]{1,0:T(8,128)}, f32[16,2048]{1,0:T(8,128)}) custom-call(s32[2]{0:T(128)S(1)} %pad_add_fusion.place_ref, f32[16,1024]{1,0:T(8,128)S(1)} %get-tuple-element.62.keep_ref, f32[16,1024]{1,0:T(8,128)S(1)} %collective-permute-done.19.got_ref, f32[64,768]{1,0:T(8,128)S(1)} %bitcast.20), custom_call_target="tpu_custom_call" | custom-call | tf_op jit(solution)/shard_map/densities/pallas_call | solution.py:254
  111.2 0.6 pad_maximum_fusion
  (38 shorter events, 1.5 us)
Async XLA Ops:
  7.3 5.1 %collective-permute-start = (f32[512,1024]{1,0:T(8,128)S(1)}, f32[512,1024]{1,0:T(8,128)S(1)}, u32[]{:S(2)}, u32[]{:S(2)}) collective-permute-start(f32[512,1024]{1,0:T(8,128)S(1)} %other.4.refs_0_), channel_id=1, source_target_pairs={{0,8},{8,0},{1,9},{9,1},{2,10},{10,2},{3,11},{11,3},{4,12},{12,4},... | collective-permute-start | bytes 6291464 | tf_op jit(solution)/shard_map/ppermute | solution.py:39
  15.0 13.4 %collective-permute-start.5 = (f32[512,1024]{1,0:T(8,128)S(1)}, f32[512,1024]{1,0:T(8,128)S(1)}, u32[]{:S(2)}, u32[]{:S(2)}) collective-permute-start(f32[512,1024]{1,0:T(8,128)S(1)} %other.5.refs_0_), channel_id=1, source_target_pairs={{0,8},{8,0},{1,9},{9,1},{2,10},{10,2},{3,11},{11,3},{4,12},{12,4},... | collective-permute-start | bytes 6291464 | tf_op jit(solution)/shard_map/ppermute | solution.py:39
  19.8 16.3 %collective-permute-start.2 = (f32[512,1024]{1,0:T(8,128)S(1)}, f32[512,1024]{1,0:T(8,128)S(1)}, u32[]{:S(2)}, u32[]{:S(2)}) collective-permute-start(f32[512,1024]{1,0:T(8,128)S(1)} %other.6.refs_0_), channel_id=1, source_target_pairs={{0,8},{8,0},{1,9},{9,1},{2,10},{10,2},{3,11},{11,3},{4,12},{12,4},... | collective-permute-start | bytes 6291464 | tf_op jit(solution)/shard_map/ppermute | solution.py:39
  20.0 16.1 %collective-permute-start.3 = (f32[256,1024]{1,0:T(8,128)S(1)}, f32[256,1024]{1,0:T(8,128)S(1)}, u32[]{:S(2)}, u32[]{:S(2)}) collective-permute-start(f32[256,1024]{1,0:T(8,128)S(1)} %get-tuple-element.56.refs_0_), channel_id=1, source_target_pairs={{0,2},{8,9},{1,3},{9,24},{16,18},{24,25},{17,19},{25,8},{2,4},{10,... | collective-permute-start | bytes 3145736 | tf_op jit(solution)/shard_map/ppermute | solution.py:35
  21.7 14.3 %collective-permute-start.8 = (f32[256,1024]{1,0:T(8,128)S(1)}, f32[256,1024]{1,0:T(8,128)S(1)}, u32[]{:S(2)}, u32[]{:S(2)}) collective-permute-start(f32[256,1024]{1,0:T(8,128)S(1)} %get-tuple-element.55), channel_id=1, source_target_pairs={{0,6},{8,25},{1,7},{9,8},{16,22},{24,9},{17,23},{25,24},{2,0},{10,... | collective-permute-start | bytes 3145736 | tf_op jit(solution)/shard_map/ppermute | solution.py:35
  28.4 34.1 %collective-permute-start.1 = (f32[512,1024]{1,0:T(8,128)S(1)}, f32[512,1024]{1,0:T(8,128)S(1)}, u32[]{:S(2)}, u32[]{:S(2)}) collective-permute-start(f32[512,1024]{1,0:T(8,128)S(1)} %other.7.refs_0_), channel_id=1, source_target_pairs={{0,8},{8,0},{1,9},{9,1},{2,10},{10,2},{3,11},{11,3},{4,12},{12,4},... | collective-permute-start | bytes 6291464 | tf_op jit(solution)/shard_map/ppermute | solution.py:39
  28.9 18.2 %collective-permute-start.6 = (f32[256,1024]{1,0:T(8,128)S(1)}, f32[256,1024]{1,0:T(8,128)S(1)}, u32[]{:S(2)}, u32[]{:S(2)}) collective-permute-start(f32[256,1024]{1,0:T(8,128)S(1)} %get-tuple-element.58), channel_id=1, source_target_pairs={{0,6},{8,25},{1,7},{9,8},{16,22},{24,9},{17,23},{25,24},{2,0},{10,... | collective-permute-start | bytes 3145736 | tf_op jit(solution)/shard_map/ppermute | solution.py:35
  36.1 15.2 %collective-permute-start.7 = (f32[256,1024]{1,0:T(8,128)S(1)}, f32[256,1024]{1,0:T(8,128)S(1)}, u32[]{:S(2)}, u32[]{:S(2)}) collective-permute-start(f32[256,1024]{1,0:T(8,128)S(1)} %get-tuple-element.57), channel_id=1, source_target_pairs={{0,2},{8,9},{1,3},{9,24},{16,18},{24,25},{17,19},{25,8},{2,4},{10,... | collective-permute-start | bytes 3145736 | tf_op jit(solution)/shard_map/ppermute | solution.py:35
  36.8 25.7 %collective-permute-start.4 = (f32[256,1024]{1,0:T(8,128)S(1)}, f32[256,1024]{1,0:T(8,128)S(1)}, u32[]{:S(2)}, u32[]{:S(2)}) collective-permute-start(f32[256,1024]{1,0:T(8,128)S(1)} %get-tuple-element.54), channel_id=1, source_target_pairs={{0,2},{8,9},{1,3},{9,24},{16,18},{24,25},{17,19},{25,8},{2,4},{10,... | collective-permute-start | bytes 3145736 | tf_op jit(solution)/shard_map/ppermute | solution.py:35
  38.1 24.3 %collective-permute-start.9 = (f32[256,1024]{1,0:T(8,128)S(1)}, f32[256,1024]{1,0:T(8,128)S(1)}, u32[]{:S(2)}, u32[]{:S(2)}) collective-permute-start(f32[256,1024]{1,0:T(8,128)S(1)} %get-tuple-element.53), channel_id=1, source_target_pairs={{0,6},{8,25},{1,7},{9,8},{16,22},{24,9},{17,23},{25,24},{2,0},{10,... | collective-permute-start | bytes 3145736 | tf_op jit(solution)/shard_map/ppermute | solution.py:35
  62.9 6.8 %collective-permute-start.10 = (f32[64,1024]{1,0:T(8,128)S(1)}, f32[64,1024]{1,0:T(8,128)S(1)}, u32[]{:S(2)}, u32[]{:S(2)}) collective-permute-start(f32[64,1024]{1,0:T(8,128)S(1)} %get-tuple-element.37), channel_id=1, source_target_pairs={{0,1},{8,40},{1,16},{9,41},{16,17},{24,56},{17,0},{25,57},{2,3},{1... | collective-permute-start | bytes 786440 | tf_op jit(solution)/shard_map/ppermute | solution.py:35
  64.2 6.5 %collective-permute-start.15 = (f32[64,1024]{1,0:T(8,128)S(1)}, f32[64,1024]{1,0:T(8,128)S(1)}, u32[]{:S(2)}, u32[]{:S(2)}) collective-permute-start(f32[64,1024]{1,0:T(8,128)S(1)} %get-tuple-element.42), channel_id=1, source_target_pairs={{0,17},{8,104},{1,0},{9,105},{16,1},{24,120},{17,16},{25,121},{2,1... | collective-permute-start | bytes 786440 | tf_op jit(solution)/shard_map/ppermute | solution.py:35
  66.1 6.6 %collective-permute-start.12 = (f32[64,1024]{1,0:T(8,128)S(1)}, f32[64,1024]{1,0:T(8,128)S(1)}, u32[]{:S(2)}, u32[]{:S(2)}) collective-permute-start(f32[64,1024]{1,0:T(8,128)S(1)} %get-tuple-element.38), channel_id=1, source_target_pairs={{0,17},{8,104},{1,0},{9,105},{16,1},{24,120},{17,16},{25,121},{2,1... | collective-permute-start | bytes 786440 | tf_op jit(solution)/shard_map/ppermute | solution.py:35
  69.7 6.5 %collective-permute-start.11 = (f32[64,1024]{1,0:T(8,128)S(1)}, f32[64,1024]{1,0:T(8,128)S(1)}, u32[]{:S(2)}, u32[]{:S(2)}) collective-permute-start(f32[64,1024]{1,0:T(8,128)S(1)} %add.187), channel_id=1, source_target_pairs={{0,1},{8,40},{1,16},{9,41},{16,17},{24,56},{17,0},{25,57},{2,3},{1... | collective-permute-start | bytes 786440 | tf_op jit(solution)/shard_map/ppermute | solution.py:35
  69.8 9.5 %collective-permute-start.14 = (f32[64,1024]{1,0:T(8,128)S(1)}, f32[64,1024]{1,0:T(8,128)S(1)}, u32[]{:S(2)}, u32[]{:S(2)}) collective-permute-start(f32[64,1024]{1,0:T(8,128)S(1)} %get-tuple-element.40), channel_id=1, source_target_pairs={{0,1},{8,40},{1,16},{9,41},{16,17},{24,56},{17,0},{25,57},{2,3},{1... | collective-permute-start | bytes 786440 | tf_op jit(solution)/shard_map/ppermute | solution.py:35
  70.8 8.5 %collective-permute-start.16 = (f32[64,1024]{1,0:T(8,128)S(1)}, f32[64,1024]{1,0:T(8,128)S(1)}, u32[]{:S(2)}, u32[]{:S(2)}) collective-permute-start(f32[64,1024]{1,0:T(8,128)S(1)} %add.192), channel_id=1, source_target_pairs={{0,17},{8,104},{1,0},{9,105},{16,1},{24,120},{17,16},{25,121},{2,1... | collective-permute-start | bytes 786440 | tf_op jit(solution)/shard_map/ppermute | solution.py:35
  76.3 6.7 %collective-permute-start.13 = (f32[32,1024]{1,0:T(8,128)S(1)}, f32[32,1024]{1,0:T(8,128)S(1)}, u32[]{:S(2)}, u32[]{:S(2)}) collective-permute-start(f32[32,1024]{1,0:T(8,128)S(1)} %slice.229), channel_id=1, source_target_pairs={{0,32},{8,10},{1,33},{9,11},{16,48},{24,26},{17,49},{25,27},{2,34}... | collective-permute-start | bytes 393224 | tf_op jit(solution)/shard_map/ppermute | solution.py:35
  79.4 7.9 %copy-start = (s32[200]{0:T(256)S(1)}, s32[200]{0:T(256)}, u32[]{:S(2)}) copy-start(s32[200]{0:T(256)} %param.5) | copy-start | bytes 2404
  79.4 7.9 %copy-start.1 = (s32[200]{0:T(256)S(1)}, s32[200]{0:T(256)}, u32[]{:S(2)}) copy-start(s32[200]{0:T(256)} %param.6) | copy-start | bytes 2404
  79.4 5.4 %collective-permute-start.17 = (f32[32,1024]{1,0:T(8,128)S(1)}, f32[32,1024]{1,0:T(8,128)S(1)}, u32[]{:S(2)}, u32[]{:S(2)}) collective-permute-start(f32[32,1024]{1,0:T(8,128)S(1)} %get-tuple-element.59), channel_id=1, source_target_pairs={{0,64},{8,12},{1,65},{9,13},{16,80},{24,28},{17,81},{25,29},{2,66}... | collective-permute-start | bytes 393224 | tf_op jit(solution)/shard_map/ppermute | solution.py:35
  82.1 4.4 %collective-permute-start.18 = (f32[32,1024]{1,0:T(8,128)S(1)}, f32[32,1024]{1,0:T(8,128)S(1)}, u32[]{:S(2)}, u32[]{:S(2)}) collective-permute-start(f32[32,1024]{1,0:T(8,128)S(1)} %get-tuple-element.60), channel_id=1, source_target_pairs={{0,96},{8,14},{1,97},{9,15},{16,112},{24,30},{17,113},{25,31},{2,9... | collective-permute-start | bytes 393224 | tf_op jit(solution)/shard_map/ppermute | solution.py:35
  87.0 24.2 %copy-start.2 = (s32[200]{0:T(256)S(1)}, s32[200]{0:T(256)}, u32[]{:S(2)}) copy-start(s32[200]{0:T(256)} %param.7) | copy-start | bytes 2404
  89.2 14.3 %all-to-all-start = ((f32[64,1,768]{2,1,0:T(1,128)}), f32[64,1,768]{2,1,0:T(1,128)S(1)}, u32[]{:S(2)}, u32[]{:S(2)}) async-start(f32[64,1,768]{2,1,0:T(1,128)} %copy.11), calls=%async_computation | async-start | bytes 393216 | tf_op jit(solution)/shard_map/all_to_all | solution.py:330
  94.4 15.2 %collective-permute-start.19 = (f32[16,1024]{1,0:T(8,128)S(1)}, f32[16,1024]{1,0:T(8,128)S(1)}, u32[]{:S(2)}, u32[]{:S(2)}) collective-permute-start(f32[16,1024]{1,0:T(8,128)S(1)} %get-tuple-element.61), channel_id=1, source_target_pairs={{0,8},{8,0},{1,9},{9,1},{2,10},{10,2},{3,11},{11,3},{4,12},{12,4},... | collective-permute-start | bytes 196616 | tf_op jit(solution)/shard_map/ppermute | solution.py:39
  103.5 7.7 %collective-permute-start.20 = (f32[200]{0:T(256)S(1)}, f32[200]{0:T(256)S(1)}, u32[]{:S(2)}, u32[]{:S(2)}) collective-permute-start(f32[200]{0:T(256)S(1)} %bitcast.26), channel_id=1, source_target_pairs={{0,8},{8,0},{1,9},{9,1},{2,10},{10,2},{3,11},{11,3},{4,12},{12,4},... | collective-permute-start | bytes 2408 | tf_op jit(solution)/shard_map/ppermute | solution.py:39

commit v5 on v4

--- a/solution.py
+++ b/solution.py
@@ -92,6 +92,7 @@
     )(pos, pltpu.with_memory_space_constraint(amps, pltpu.HBM))
 
 
+SECOND = ((2, 1), (3, 0))
 CHUNKS = (((2, 0), (2, 1)), ((1, 1), (3, 0)), ((1, 0), (3, 1)), ((0, 0), (0, 1)))
 
 
@@ -106,15 +107,15 @@
     to = []
     for x in range(4):
         kx = (x - x0) & 3
-        pick = (kx >> 1) ^ halves[0][1]
+        pick = (((kx ^ (kx >> 1)) & 1) ^ 1) ^ halves[0][1]
         k1_there = jnp.where(pick == 0, halves[0][0], halves[1][0])
         for s in range(4):
             h, j = divmod(s, 2)
             k1, half = halves[h]
             y = jnp.where(first, (y0 + k1) & 3, s)
-            z = jnp.where(first, z0 + 2 * half + j, z0 + k1_there) & 3
+            z = jnp.where(first, z0 + SECOND[half][j], z0 + k1_there) & 3
             here = h * 256 + j * 128 + kx * 32
-            there = pick * 256 + (kx & 1) * 128 + ((s - y0) & 3) * 32
+            there = pick * 256 + (1 - (kx >> 1)) * 128 + ((s - y0) & 3) * 32
             to.append(pl.multiple_of(jnp.where(first, here, there), 32))
             base = x * 512 + (z >> 1) * 256 + y * 32 + (z & 1) * 16
             for co in range(2):
@@ -293,28 +294,25 @@
     send4 = send(CHUNKS[3], waits=(near,))
     recv4 = swapped(send4)
     mine = make(CHUNKS[3], waits=(send4,))
-    came = lax.optimization_barrier(((from_left0, from_right0), (from_left1, from_right1)))
-
     def first_sum(came, half, at):
-        left, right = came[half]
+        left, right = came
         here = slice(at, at + 64)
         there = slice(half * 256 + at, half * 256 + at + 64)
         return (mine[there] + recv4[there]) + (left[here] + right[here])
 
-    places = ((1, 0), (1, 64), (0, 192), (1, 128))
-    (far0, far1, right1, left0), came = lax.optimization_barrier(
-        (tuple(first_sum(came, *p) for p in places), came)
-    )
+    came = lax.optimization_barrier((from_left0, from_right0))
+    sums = tuple(first_sum(came, 0, at) for at in (0, 64, 128, 192))
+    far0, far1, right0, right1 = lax.optimization_barrier(sums)
     via_left = round_ring(far0, 1, 1)
     via_right = round_ring(far1, 1, -1)
-    from_left1 = round_ring(right1, 1, 1)
-    from_right0 = round_ring(left0, 1, -1)
-    places = ((0, 128), (1, 192), (0, 0), (0, 64))
-    right0, left1, low, high = lax.optimization_barrier(tuple(first_sum(came, *p) for p in places))
-    from_left0 = round_ring(right0 + via_left, 1, 1)
-    from_right1 = round_ring(left1 + via_right, 1, -1)
-    low = low + from_left0 + from_right0
-    high = high + from_left1 + from_right1
+    next_left1 = round_ring(right1, 1, 1)
+    came = lax.optimization_barrier((from_left1, from_right1))
+    left0, left1, low, high = lax.optimization_barrier(tuple(first_sum(came, 1, at) for at in (0, 64, 128, 192)))
+    next_right0 = round_ring(left0, 1, -1)
+    next_left0 = round_ring(right0 + via_left, 1, 1)
+    next_right1 = round_ring(left1 + via_right, 1, -1)
+    low = low + next_left0 + next_right0
+    high = high + next_left1 + next_right1
     rows = [low[:32], low[32:], high[:32], high[32:]]
     arrived = {}
     for k in (2, 1, 3):

time: 112 us -> 114 us (1.018)
  waiting for transfers between devices: 40.6 us -> 48.3 us
  starting transfers between devices: 41.1 us -> 35.7 us
    ppermute x6, starting transfers between devices: 13.1 us -> 6.12 us  [swapped(): return lax.ppermute(array, CORE, [(0, 1), (1, 0)])]
    ppermute x15, waiting for transfers between devices: 34.9 us -> 39.2 us  [round_ring(): return lax.ppermute(array, AX, ring_perm(turn, step))]
    all_to_all x1, starting transfers between devices: 5.24 us -> 8.99 us  [on_device(): lax.all_to_all(message, SAME_CORE, split_axis=0, concat_axis=0, tiled=True)]
    all_to_all x1, waiting for transfers between devices: 4.04 us -> 7.5 us  [on_device(): lax.all_to_all(message, SAME_CORE, split_axis=0, concat_axis=0, tiled=True)]
    ppermute x15, starting transfers between devices: 22.7 us -> 20.6 us  [round_ring(): return lax.ppermute(array, AX, ring_perm(turn, step))]
  transfers between devices with their start and end apart: 22 -> 22, of which waited for: 11 -> 11; matrix products, arithmetic and copies ran while one was open for 2% -> 2% of each run, Pallas kernels for 13% -> 9%
where the time goes in v5:
time: 114 us
  waiting for transfers between devices  48.3 us (42%)
  starting transfers between devices  35.7 us (31%)
  Pallas kernels  23.9 us (21%)
  other arithmetic  3.82 us (3%)
  local copies, waits for them, and re-layouts  1.6 us (1%)
    ppermute x15, waiting for transfers between devices, round_ring(): return lax.ppermute(array, AX, ring_perm(turn, step))  39.2 us
    ppermute x15, starting transfers between devices, round_ring(): return lax.ppermute(array, AX, ring_perm(turn, step))  20.6 us
    pallas_call x8, Pallas kernels, chunk_part(): pl.pallas_call(functools.partial(chunk_kernel, halves=halves, own=own, wa...  17.2 us
    all_to_all x1, starting transfers between devices, on_device(): lax.all_to_all(message, SAME_CORE, split_axis=0, concat_axis=0, tiled=True)  8.99 us
    all_to_all x1, waiting for transfers between devices, on_device(): lax.all_to_all(message, SAME_CORE, split_axis=0, concat_axis=0, tiled=True)  7.5 us
    ppermute x6, starting transfers between devices, swapped(): return lax.ppermute(array, CORE, [(0, 1), (1, 0)])  6.12 us
    pallas_call x1, Pallas kernels, prepare(): pl.pallas_call(prepare_kernel, out_shape=[jax.ShapeDtypeStruct((2048, 153...  4.44 us
  transfers between devices with their start and end apart: 22, of which 11 were waited for; matrix products, arithmetic and copies ran while one was open for 2% of the time, Pallas kernels for 9%

profile of v5, /device:TPU:1, one launch (start us, length us, event | category | flops | bytes accessed | tf_op | source)
XLA Modules:
  0.0 114.2 jit_solution(5995614075237922896)
XLA Ops:
  0.7 4.4 %prepare.1 = (bf16[2048,1536]{1,0:T(8,128)(2,1)S(1)}, bf16[1024,1024]{1,0:T(8,128)(2,1)S(1)}, bf16[1024,1024]{1,0:T(8,128)(2,1)S(1)}) custom-call(s32[4]{0:T(128)S(1)} %pad_add_fusion.1.pos_ref, bf16[2,512,2048]{2,1,0:T(8,128)(2,1)} %amps_ref.1), custom_call_target="tpu_custom_call" | custom-call | flops 2000000000 | bytes 14680064 | tf_op jit(solution)/shard_map/prepare/pallas_call | solution.py:71
  5.2 2.1 %other.4.refs_0_ = f32[512,1024]{1,0:T(8,128)S(1)} custom-call(s32[4]{0:T(128)S(1)} %pad_add_fusion.1.pos_ref, bf16[2048,1536]{1,0:T(8,128)(2,1)S(1)} %get-tuple-element.20.lt_ref, bf16[1024,1024]{1,0:T(8,128)(2,1)S(1)} %get-tuple-element.22.w_ref), custom_call_target="tpu_custom_call" | custom-call | flops 1342177280 | bytes 8388608 | tf_op jit(solution)/shard_map/other/pallas_call | solution.py:146
  7.3 1.3 %collective-permute-start = (f32[512,1024]{1,0:T(8,128)S(1)}, f32[512,1024]{1,0:T(8,128)S(1)}, u32[]{:S(2)}, u32[]{:S(2)}) collective-permute-start(f32[512,1024]{1,0:T(8,128)S(1)} %other.4.refs_0_), channel_id=1, source_target_pairs={{0,8},{8,0},{1,9},{9,1},{2,10},{10,2},{3,11},{11,3},{4,12},{12,4},... | collective-permute-start | bytes 6291464 | tf_op jit(solution)/shard_map/ppermute | solution.py:39
  8.6 2.1 %own.4 = f32[512,1024]{1,0:T(8,128)S(1)} custom-call(s32[4]{0:T(128)S(1)} %pad_add_fusion.1.pos_ref, bf16[2048,1536]{1,0:T(8,128)(2,1)S(1)} %get-tuple-element.20.lt_ref, bf16[1024,1024]{1,0:T(8,128)(2,1)S(1)} %get-tuple-element.21.w_ref, f32[512,1024]{1,0:T(8,128)S(1)} %other.4.refs_0_), custom_call_target="tpu_custom_call" | custom-call | flops 1342177280 | bytes 8388608 | tf_op jit(solution)/shard_map/own/pallas_call | solution.py:146
  10.8 1.6 %collective-permute-done = f32[512,1024]{1,0:T(8,128)S(1)} collective-permute-done((f32[512,1024]{1,0:T(8,128)S(1)}, f32[512,1024]{1,0:T(8,128)S(1)}, u32[]{:S(2)}, u32[]{:S(2)}) %collective-permute-start) | collective-permute-done | bytes 2097184 | tf_op jit(solution)/shard_map/ppermute | solution.py:39
  12.4 0.5 slice_add_fusion.2
  12.9 2.1 %other.5.refs_0_ = f32[512,1024]{1,0:T(8,128)S(1)} custom-call(s32[4]{0:T(128)S(1)} %pad_add_fusion.1.pos_ref, bf16[2048,1536]{1,0:T(8,128)(2,1)S(1)} %get-tuple-element.20.lt_ref, bf16[1024,1024]{1,0:T(8,128)(2,1)S(1)} %get-tuple-element.22.w_ref, f32[256,1024]{1,0:T(8,128)S(1)} %get-tuple-element.50.refs_0_), custom_call_target="tpu_custom_call" | custom-call | flops 1342177280 | bytes 8388608 | tf_op jit(solution)/shard_map/other/pallas_call | solution.py:146
  15.1 2.2 %own.5.refs_0_ = f32[512,1024]{1,0:T(8,128)S(1)} custom-call(s32[4]{0:T(128)S(1)} %pad_add_fusion.1.pos_ref, bf16[2048,1536]{1,0:T(8,128)(2,1)S(1)} %get-tuple-element.20.lt_ref, bf16[1024,1024]{1,0:T(8,128)(2,1)S(1)} %get-tuple-element.21.w_ref, f32[512,1024]{1,0:T(8,128)S(1)} %other.5.refs_0_), custom_call_target="tpu_custom_call" | custom-call | flops 1342177280 | bytes 8388608 | tf_op jit(solution)/shard_map/own/pallas_call | solution.py:146
  17.3 2.1 %other.6.refs_0_ = f32[512,1024]{1,0:T(8,128)S(1)} custom-call(s32[4]{0:T(128)S(1)} %pad_add_fusion.1.pos_ref, bf16[2048,1536]{1,0:T(8,128)(2,1)S(1)} %get-tuple-element.20.lt_ref, bf16[1024,1024]{1,0:T(8,128)(2,1)S(1)} %get-tuple-element.22.w_ref, f32[512,1024]{1,0:T(8,128)S(1)} %own.5.refs_0_), custom_call_target="tpu_custom_call" | custom-call | flops 1342177280 | bytes 8388608 | tf_op jit(solution)/shard_map/other/pallas_call | solution.py:146
  19.4 0.5 collective-permute-start.4
  20.0 3.9 %collective-permute-start.5 = (f32[256,1024]{1,0:T(8,128)S(1)}, f32[256,1024]{1,0:T(8,128)S(1)}, u32[]{:S(2)}, u32[]{:S(2)}) collective-permute-start(f32[256,1024]{1,0:T(8,128)S(1)} %get-tuple-element.49), channel_id=1, source_target_pairs={{0,6},{8,25},{1,7},{9,8},{16,22},{24,9},{17,23},{25,24},{2,0},{10,... | collective-permute-start | bytes 3145736 | tf_op jit(solution)/shard_map/ppermute | solution.py:35
  23.9 2.1 %own.6.refs_0_ = f32[512,1024]{1,0:T(8,128)S(1)} custom-call(s32[4]{0:T(128)S(1)} %pad_add_fusion.1.pos_ref, bf16[2048,1536]{1,0:T(8,128)(2,1)S(1)} %get-tuple-element.20.lt_ref, bf16[1024,1024]{1,0:T(8,128)(2,1)S(1)} %get-tuple-element.21.w_ref, f32[512,1024]{1,0:T(8,128)S(1)} %other.6.refs_0_), custom_call_target="tpu_custom_call" | custom-call | flops 1342177280 | bytes 8388608 | tf_op jit(solution)/shard_map/own/pallas_call | solution.py:146
  26.0 2.1 %other.7.refs_0_ = f32[512,1024]{1,0:T(8,128)S(1)} custom-call(s32[4]{0:T(128)S(1)} %pad_add_fusion.1.pos_ref, bf16[2048,1536]{1,0:T(8,128)(2,1)S(1)} %get-tuple-element.20.lt_ref, bf16[1024,1024]{1,0:T(8,128)(2,1)S(1)} %get-tuple-element.22.w_ref, f32[512,1024]{1,0:T(8,128)S(1)} %own.6.refs_0_), custom_call_target="tpu_custom_call" | custom-call | flops 1342177280 | bytes 8388608 | tf_op jit(solution)/shard_map/other/pallas_call | solution.py:146
  28.3 7.3 %collective-permute-done.5 = f32[256,1024]{1,0:T(8,128)S(1)} collective-permute-done((f32[256,1024]{1,0:T(8,128)S(1)}, f32[256,1024]{1,0:T(8,128)S(1)}, u32[]{:S(2)}, u32[]{:S(2)}) %collective-permute-start.5) | collective-permute-done | bytes 1048608 | tf_op jit(solution)/shard_map/ppermute | solution.py:35
  35.6 3.4 %collective-permute-done.7 = f32[256,1024]{1,0:T(8,128)S(1)} collective-permute-done((f32[256,1024]{1,0:T(8,128)S(1)}, f32[256,1024]{1,0:T(8,128)S(1)}, u32[]{:S(2)}, u32[]{:S(2)}) %collective-permute-start.7) | collective-permute-done | bytes 1048608 | tf_op jit(solution)/shard_map/ppermute | solution.py:35
  39.0 0.7 fusion
  39.8 0.4 slice_add_fusion
  40.3 2.7 %collective-permute-start.9 = (f32[256,1024]{1,0:T(8,128)S(1)}, f32[256,1024]{1,0:T(8,128)S(1)}, u32[]{:S(2)}, u32[]{:S(2)}) collective-permute-start(f32[256,1024]{1,0:T(8,128)S(1)} %get-tuple-element.45), channel_id=1, source_target_pairs={{0,6},{8,25},{1,7},{9,8},{16,22},{24,9},{17,23},{25,24},{2,0},{10,... | collective-permute-start | bytes 3145736 | tf_op jit(solution)/shard_map/ppermute | solution.py:35
  43.1 1.4 %collective-permute-start.3 = (f32[256,1024]{1,0:T(8,128)S(1)}, f32[256,1024]{1,0:T(8,128)S(1)}, u32[]{:S(2)}, u32[]{:S(2)}) collective-permute-start(f32[256,1024]{1,0:T(8,128)S(1)} %get-tuple-element.46), channel_id=1, source_target_pairs={{0,2},{8,9},{1,3},{9,24},{16,18},{24,25},{17,19},{25,8},{2,4},{10,... | collective-permute-start | bytes 3145736 | tf_op jit(solution)/shard_map/ppermute | solution.py:35
  44.5 2.1 %own.7 = f32[512,1024]{1,0:T(8,128)S(1)} custom-call(s32[4]{0:T(128)S(1)} %pad_add_fusion.1.pos_ref, bf16[2048,1536]{1,0:T(8,128)(2,1)S(1)} %get-tuple-element.20.lt_ref, bf16[1024,1024]{1,0:T(8,128)(2,1)S(1)} %get-tuple-element.21.w_ref, f32[512,1024]{1,0:T(8,128)S(1)} %other.7.refs_0_), custom_call_target="tpu_custom_call" | custom-call | flops 1342177280 | bytes 8388608 | tf_op jit(solution)/shard_map/own/pallas_call | solution.py:146
  46.6 8.3 %collective-permute-done.8 = f32[256,1024]{1,0:T(8,128)S(1)} collective-permute-done((f32[256,1024]{1,0:T(8,128)S(1)}, f32[256,1024]{1,0:T(8,128)S(1)}, u32[]{:S(2)}, u32[]{:S(2)}) %collective-permute-start.8) | collective-permute-done | bytes 1048608 | tf_op jit(solution)/shard_map/ppermute | solution.py:35
  55.0 0.4 fusion.2
  55.4 1.3 %collective-permute-start.10 = (f32[64,1024]{1,0:T(8,128)S(1)}, f32[64,1024]{1,0:T(8,128)S(1)}, u32[]{:S(2)}, u32[]{:S(2)}) collective-permute-start(f32[64,1024]{1,0:T(8,128)S(1)} %get-tuple-element.29), channel_id=1, source_target_pairs={{0,1},{8,40},{1,16},{9,41},{16,17},{24,56},{17,0},{25,57},{2,3},{1... | collective-permute-start | bytes 786440 | tf_op jit(solution)/shard_map/ppermute | solution.py:35
  56.7 1.5 %collective-permute-start.15 = (f32[64,1024]{1,0:T(8,128)S(1)}, f32[64,1024]{1,0:T(8,128)S(1)}, u32[]{:S(2)}, u32[]{:S(2)}) collective-permute-start(f32[64,1024]{1,0:T(8,128)S(1)} %get-tuple-element.34), channel_id=1, source_target_pairs={{0,17},{8,104},{1,0},{9,105},{16,1},{24,120},{17,16},{25,121},{2,1... | collective-permute-start | bytes 786440 | tf_op jit(solution)/shard_map/ppermute | solution.py:35
  58.2 10.6 %collective-permute-done.6 = f32[256,1024]{1,0:T(8,128)S(1)} collective-permute-done((f32[256,1024]{1,0:T(8,128)S(1)}, f32[256,1024]{1,0:T(8,128)S(1)}, u32[]{:S(2)}, u32[]{:S(2)}) %collective-permute-start.6) | collective-permute-done | bytes 1048608 | tf_op jit(solution)/shard_map/ppermute | solution.py:35
  68.8 0.4 fusion.6
  69.3 2.5 %collective-permute-start.12 = (f32[64,1024]{1,0:T(8,128)S(1)}, f32[64,1024]{1,0:T(8,128)S(1)}, u32[]{:S(2)}, u32[]{:S(2)}) collective-permute-start(f32[64,1024]{1,0:T(8,128)S(1)} %get-tuple-element.30), channel_id=1, source_target_pairs={{0,17},{8,104},{1,0},{9,105},{16,1},{24,120},{17,16},{25,121},{2,1... | collective-permute-start | bytes 786440 | tf_op jit(solution)/shard_map/ppermute | solution.py:35
  71.9 0.2 collective-permute-start.14
  72.2 2.6 %collective-permute-start.16 = (f32[64,1024]{1,0:T(8,128)S(1)}, f32[64,1024]{1,0:T(8,128)S(1)}, u32[]{:S(2)}, u32[]{:S(2)}) collective-permute-start(f32[64,1024]{1,0:T(8,128)S(1)} %add.192), channel_id=1, source_target_pairs={{0,17},{8,104},{1,0},{9,105},{16,1},{24,120},{17,16},{25,121},{2,1... | collective-permute-start | bytes 786440 | tf_op jit(solution)/shard_map/ppermute | solution.py:35
  74.8 0.3 collective-permute-done.12
  75.1 3.5 %collective-permute-done.11 = f32[64,1024]{1,0:T(8,128)S(1)} collective-permute-done((f32[64,1024]{1,0:T(8,128)S(1)}, f32[64,1024]{1,0:T(8,128)S(1)}, u32[]{:S(2)}, u32[]{:S(2)}) %collective-permute-start.11) | collective-permute-done | bytes 262176 | tf_op jit(solution)/shard_map/ppermute | solution.py:35
  78.7 1.1 collective-permute-start.13
  79.8 1.7 %collective-permute-done.14 = f32[64,1024]{1,0:T(8,128)S(1)} collective-permute-done((f32[64,1024]{1,0:T(8,128)S(1)}, f32[64,1024]{1,0:T(8,128)S(1)}, u32[]{:S(2)}, u32[]{:S(2)}) %collective-permute-start.14) | collective-permute-done | bytes 262176 | tf_op jit(solution)/shard_map/ppermute | solution.py:35
  81.6 2.5 %collective-permute-start.17 = (f32[32,1024]{1,0:T(8,128)S(1)}, f32[32,1024]{1,0:T(8,128)S(1)}, u32[]{:S(2)}, u32[]{:S(2)}) collective-permute-start(f32[32,1024]{1,0:T(8,128)S(1)} %get-tuple-element.51), channel_id=1, source_target_pairs={{0,64},{8,12},{1,65},{9,13},{16,80},{24,28},{17,81},{25,29},{2,66}... | collective-permute-start | bytes 393224 | tf_op jit(solution)/shard_map/ppermute | solution.py:35
  84.1 0.6 collective-permute-start.18
  84.8 2.1 %collective-permute-done.17 = f32[32,1024]{1,0:T(8,128)S(1)} collective-permute-done((f32[32,1024]{1,0:T(8,128)S(1)}, f32[32,1024]{1,0:T(8,128)S(1)}, u32[]{:S(2)}, u32[]{:S(2)}) %collective-permute-start.17) | collective-permute-done | bytes 131104 | tf_op jit(solution)/shard_map/ppermute | solution.py:35
  87.0 1.7 %collective-permute-done.18 = f32[32,1024]{1,0:T(8,128)S(1)} collective-permute-done((f32[32,1024]{1,0:T(8,128)S(1)}, f32[32,1024]{1,0:T(8,128)S(1)}, u32[]{:S(2)}, u32[]{:S(2)}) %collective-permute-start.18) | collective-permute-done | bytes 131104 | tf_op jit(solution)/shard_map/ppermute | solution.py:35
  88.7 0.4 reshape.14
  89.1 0.3 copy.10
  89.5 0.8 pauli.1
  90.3 0.2 maximum_bitcast_fusion
  90.4 0.8 copy.11
  91.3 9.0 %all-to-all-start = ((f32[64,1,768]{2,1,0:T(1,128)}), f32[64,1,768]{2,1,0:T(1,128)S(1)}, u32[]{:S(2)}, u32[]{:S(2)}) async-start(f32[64,1,768]{2,1,0:T(1,128)} %copy.11), calls=%async_computation | async-start | bytes 393216 | tf_op jit(solution)/shard_map/all_to_all | solution.py:328
  100.3 1.5 %collective-permute-start.19 = (f32[16,1024]{1,0:T(8,128)S(1)}, f32[16,1024]{1,0:T(8,128)S(1)}, u32[]{:S(2)}, u32[]{:S(2)}) collective-permute-start(f32[16,1024]{1,0:T(8,128)S(1)} %get-tuple-element.53), channel_id=1, source_target_pairs={{0,8},{8,0},{1,9},{9,1},{2,10},{10,2},{3,11},{11,3},{4,12},{12,4},... | collective-permute-start | bytes 196616 | tf_op jit(solution)/shard_map/ppermute | solution.py:39
  101.8 7.5 %all-to-all-done = f32[64,1,768]{2,1,0:T(1,128)S(1)} async-done(((f32[64,1,768]{2,1,0:T(1,128)}), f32[64,1,768]{2,1,0:T(1,128)S(1)}, u32[]{:S(2)}, u32[]{:S(2)}) %all-to-all-start) | async-done | bytes 196640 | tf_op jit(solution)/shard_map/all_to_all | solution.py:328
  109.4 2.6 %collective-permute-start.20 = (f32[200]{0:T(256)S(1)}, f32[200]{0:T(256)S(1)}, u32[]{:S(2)}, u32[]{:S(2)}) collective-permute-start(f32[200]{0:T(256)S(1)} %bitcast.26), channel_id=1, source_target_pairs={{0,8},{8,0},{1,9},{9,1},{2,10},{10,2},{3,11},{11,3},{4,12},{12,4},... | collective-permute-start | bytes 2408 | tf_op jit(solution)/shard_map/ppermute | solution.py:39
  112.1 1.5 %densities.1 = (f32[16,2048]{1,0:T(8,128)}, f32[16,2048]{1,0:T(8,128)}) custom-call(s32[2]{0:T(128)S(1)} %pad_add_fusion.place_ref, f32[16,1024]{1,0:T(8,128)S(1)} %get-tuple-element.54.keep_ref, f32[16,1024]{1,0:T(8,128)S(1)} %collective-permute-done.19.got_ref, f32[64,768]{1,0:T(8,128)S(1)} %bitcast.20), custom_call_target="tpu_custom_call" | custom-call | tf_op jit(solution)/shard_map/densities/pallas_call | solution.py:255
  113.6 0.6 pad_maximum_fusion
  (38 shorter events, 1.0 us)
Async XLA Ops:
  7.3 5.1 %collective-permute-start = (f32[512,1024]{1,0:T(8,128)S(1)}, f32[512,1024]{1,0:T(8,128)S(1)}, u32[]{:S(2)}, u32[]{:S(2)}) collective-permute-start(f32[512,1024]{1,0:T(8,128)S(1)} %other.4.refs_0_), channel_id=1, source_target_pairs={{0,8},{8,0},{1,9},{9,1},{2,10},{10,2},{3,11},{11,3},{4,12},{12,4},... | collective-permute-start | bytes 6291464 | tf_op jit(solution)/shard_map/ppermute | solution.py:39
  19.4 19.6 %collective-permute-start.4 = (f32[512,1024]{1,0:T(8,128)S(1)}, f32[512,1024]{1,0:T(8,128)S(1)}, u32[]{:S(2)}, u32[]{:S(2)}) collective-permute-start(f32[512,1024]{1,0:T(8,128)S(1)} %other.6.refs_0_), channel_id=1, source_target_pairs={{0,8},{8,0},{1,9},{9,1},{2,10},{10,2},{3,11},{11,3},{4,12},{12,4},... | collective-permute-start | bytes 6291464 | tf_op jit(solution)/shard_map/ppermute | solution.py:39
  19.9 20.0 %collective-permute-start.2 = (f32[512,1024]{1,0:T(8,128)S(1)}, f32[512,1024]{1,0:T(8,128)S(1)}, u32[]{:S(2)}, u32[]{:S(2)}) collective-permute-start(f32[512,1024]{1,0:T(8,128)S(1)} %other.5.refs_0_), channel_id=1, source_target_pairs={{0,8},{8,0},{1,9},{9,1},{2,10},{10,2},{3,11},{11,3},{4,12},{12,4},... | collective-permute-start | bytes 6291464 | tf_op jit(solution)/shard_map/ppermute | solution.py:39
  20.0 15.6 %collective-permute-start.5 = (f32[256,1024]{1,0:T(8,128)S(1)}, f32[256,1024]{1,0:T(8,128)S(1)}, u32[]{:S(2)}, u32[]{:S(2)}) collective-permute-start(f32[256,1024]{1,0:T(8,128)S(1)} %get-tuple-element.49), channel_id=1, source_target_pairs={{0,6},{8,25},{1,7},{9,8},{16,22},{24,9},{17,23},{25,24},{2,0},{10,... | collective-permute-start | bytes 3145736 | tf_op jit(solution)/shard_map/ppermute | solution.py:35
  23.9 15.2 %collective-permute-start.7 = (f32[256,1024]{1,0:T(8,128)S(1)}, f32[256,1024]{1,0:T(8,128)S(1)}, u32[]{:S(2)}, u32[]{:S(2)}) collective-permute-start(f32[256,1024]{1,0:T(8,128)S(1)} %get-tuple-element.50.refs_0_), channel_id=1, source_target_pairs={{0,2},{8,9},{1,3},{9,24},{16,18},{24,25},{17,19},{25,8},{2,4},{10,... | collective-permute-start | bytes 3145736 | tf_op jit(solution)/shard_map/ppermute | solution.py:35
  28.2 26.8 %collective-permute-start.1 = (f32[512,1024]{1,0:T(8,128)S(1)}, f32[512,1024]{1,0:T(8,128)S(1)}, u32[]{:S(2)}, u32[]{:S(2)}) collective-permute-start(f32[512,1024]{1,0:T(8,128)S(1)} %other.7.refs_0_), channel_id=1, source_target_pairs={{0,8},{8,0},{1,9},{9,1},{2,10},{10,2},{3,11},{11,3},{4,12},{12,4},... | collective-permute-start | bytes 6291464 | tf_op jit(solution)/shard_map/ppermute | solution.py:39
  39.8 15.2 %collective-permute-start.8 = (f32[256,1024]{1,0:T(8,128)S(1)}, f32[256,1024]{1,0:T(8,128)S(1)}, u32[]{:S(2)}, u32[]{:S(2)}) collective-permute-start(f32[256,1024]{1,0:T(8,128)S(1)} %get-tuple-element.47), channel_id=1, source_target_pairs={{0,2},{8,9},{1,3},{9,24},{16,18},{24,25},{17,19},{25,8},{2,4},{10,... | collective-permute-start | bytes 3145736 | tf_op jit(solution)/shard_map/ppermute | solution.py:35
  40.3 14.7 %collective-permute-start.9 = (f32[256,1024]{1,0:T(8,128)S(1)}, f32[256,1024]{1,0:T(8,128)S(1)}, u32[]{:S(2)}, u32[]{:S(2)}) collective-permute-start(f32[256,1024]{1,0:T(8,128)S(1)} %get-tuple-element.45), channel_id=1, source_target_pairs={{0,6},{8,25},{1,7},{9,8},{16,22},{24,9},{17,23},{25,24},{2,0},{10,... | collective-permute-start | bytes 3145736 | tf_op jit(solution)/shard_map/ppermute | solution.py:35
  43.0 25.8 %collective-permute-start.6 = (f32[256,1024]{1,0:T(8,128)S(1)}, f32[256,1024]{1,0:T(8,128)S(1)}, u32[]{:S(2)}, u32[]{:S(2)}) collective-permute-start(f32[256,1024]{1,0:T(8,128)S(1)} %get-tuple-element.48), channel_id=1, source_target_pairs={{0,6},{8,25},{1,7},{9,8},{16,22},{24,9},{17,23},{25,24},{2,0},{10,... | collective-permute-start | bytes 3145736 | tf_op jit(solution)/shard_map/ppermute | solution.py:35
  43.1 25.7 %collective-permute-start.3 = (f32[256,1024]{1,0:T(8,128)S(1)}, f32[256,1024]{1,0:T(8,128)S(1)}, u32[]{:S(2)}, u32[]{:S(2)}) collective-permute-start(f32[256,1024]{1,0:T(8,128)S(1)} %get-tuple-element.46), channel_id=1, source_target_pairs={{0,2},{8,9},{1,3},{9,24},{16,18},{24,25},{17,19},{25,8},{2,4},{10,... | collective-permute-start | bytes 3145736 | tf_op jit(solution)/shard_map/ppermute | solution.py:35
  55.4 16.4 %collective-permute-start.10 = (f32[64,1024]{1,0:T(8,128)S(1)}, f32[64,1024]{1,0:T(8,128)S(1)}, u32[]{:S(2)}, u32[]{:S(2)}) collective-permute-start(f32[64,1024]{1,0:T(8,128)S(1)} %get-tuple-element.29), channel_id=1, source_target_pairs={{0,1},{8,40},{1,16},{9,41},{16,17},{24,56},{17,0},{25,57},{2,3},{1... | collective-permute-start | bytes 786440 | tf_op jit(solution)/shard_map/ppermute | solution.py:35
  56.7 15.4 %collective-permute-start.15 = (f32[64,1024]{1,0:T(8,128)S(1)}, f32[64,1024]{1,0:T(8,128)S(1)}, u32[]{:S(2)}, u32[]{:S(2)}) collective-permute-start(f32[64,1024]{1,0:T(8,128)S(1)} %get-tuple-element.34), channel_id=1, source_target_pairs={{0,17},{8,104},{1,0},{9,105},{16,1},{24,120},{17,16},{25,121},{2,1... | collective-permute-start | bytes 786440 | tf_op jit(solution)/shard_map/ppermute | solution.py:35
  69.3 5.9 %collective-permute-start.12 = (f32[64,1024]{1,0:T(8,128)S(1)}, f32[64,1024]{1,0:T(8,128)S(1)}, u32[]{:S(2)}, u32[]{:S(2)}) collective-permute-start(f32[64,1024]{1,0:T(8,128)S(1)} %get-tuple-element.30), channel_id=1, source_target_pairs={{0,17},{8,104},{1,0},{9,105},{16,1},{24,120},{17,16},{25,121},{2,1... | collective-permute-start | bytes 786440 | tf_op jit(solution)/shard_map/ppermute | solution.py:35
  71.9 6.8 %collective-permute-start.11 = (f32[64,1024]{1,0:T(8,128)S(1)}, f32[64,1024]{1,0:T(8,128)S(1)}, u32[]{:S(2)}, u32[]{:S(2)}) collective-permute-start(f32[64,1024]{1,0:T(8,128)S(1)} %add.187), channel_id=1, source_target_pairs={{0,1},{8,40},{1,16},{9,41},{16,17},{24,56},{17,0},{25,57},{2,3},{1... | collective-permute-start | bytes 786440 | tf_op jit(solution)/shard_map/ppermute | solution.py:35
  71.9 9.5 %collective-permute-start.14 = (f32[64,1024]{1,0:T(8,128)S(1)}, f32[64,1024]{1,0:T(8,128)S(1)}, u32[]{:S(2)}, u32[]{:S(2)}) collective-permute-start(f32[64,1024]{1,0:T(8,128)S(1)} %get-tuple-element.32), channel_id=1, source_target_pairs={{0,1},{8,40},{1,16},{9,41},{16,17},{24,56},{17,0},{25,57},{2,3},{1... | collective-permute-start | bytes 786440 | tf_op jit(solution)/shard_map/ppermute | solution.py:35
  72.2 9.3 %collective-permute-start.16 = (f32[64,1024]{1,0:T(8,128)S(1)}, f32[64,1024]{1,0:T(8,128)S(1)}, u32[]{:S(2)}, u32[]{:S(2)}) collective-permute-start(f32[64,1024]{1,0:T(8,128)S(1)} %add.192), channel_id=1, source_target_pairs={{0,17},{8,104},{1,0},{9,105},{16,1},{24,120},{17,16},{25,121},{2,1... | collective-permute-start | bytes 786440 | tf_op jit(solution)/shard_map/ppermute | solution.py:35
  78.7 6.1 %collective-permute-start.13 = (f32[32,1024]{1,0:T(8,128)S(1)}, f32[32,1024]{1,0:T(8,128)S(1)}, u32[]{:S(2)}, u32[]{:S(2)}) collective-permute-start(f32[32,1024]{1,0:T(8,128)S(1)} %slice.229), channel_id=1, source_target_pairs={{0,32},{8,10},{1,33},{9,11},{16,48},{24,26},{17,49},{25,27},{2,34}... | collective-permute-start | bytes 393224 | tf_op jit(solution)/shard_map/ppermute | solution.py:35
  81.5 7.9 %copy-start = (s32[200]{0:T(256)S(1)}, s32[200]{0:T(256)}, u32[]{:S(2)}) copy-start(s32[200]{0:T(256)} %param.5) | copy-start | bytes 2404
  81.5 7.9 %copy-start.1 = (s32[200]{0:T(256)S(1)}, s32[200]{0:T(256)}, u32[]{:S(2)}) copy-start(s32[200]{0:T(256)} %param.6) | copy-start | bytes 2404
  81.6 5.4 %collective-permute-start.17 = (f32[32,1024]{1,0:T(8,128)S(1)}, f32[32,1024]{1,0:T(8,128)S(1)}, u32[]{:S(2)}, u32[]{:S(2)}) collective-permute-start(f32[32,1024]{1,0:T(8,128)S(1)} %get-tuple-element.51), channel_id=1, source_target_pairs={{0,64},{8,12},{1,65},{9,13},{16,80},{24,28},{17,81},{25,29},{2,66}... | collective-permute-start | bytes 393224 | tf_op jit(solution)/shard_map/ppermute | solution.py:35
  84.1 4.6 %collective-permute-start.18 = (f32[32,1024]{1,0:T(8,128)S(1)}, f32[32,1024]{1,0:T(8,128)S(1)}, u32[]{:S(2)}, u32[]{:S(2)}) collective-permute-start(f32[32,1024]{1,0:T(8,128)S(1)} %get-tuple-element.52), channel_id=1, source_target_pairs={{0,96},{8,14},{1,97},{9,15},{16,112},{24,30},{17,113},{25,31},{2,9... | collective-permute-start | bytes 393224 | tf_op jit(solution)/shard_map/ppermute | solution.py:35
  89.1 24.5 %copy-start.2 = (s32[200]{0:T(256)S(1)}, s32[200]{0:T(256)}, u32[]{:S(2)}) copy-start(s32[200]{0:T(256)} %param.7) | copy-start | bytes 2404
  91.3 18.1 %all-to-all-start = ((f32[64,1,768]{2,1,0:T(1,128)}), f32[64,1,768]{2,1,0:T(1,128)S(1)}, u32[]{:S(2)}, u32[]{:S(2)}) async-start(f32[64,1,768]{2,1,0:T(1,128)} %copy.11), calls=%async_computation | async-start | bytes 393216 | tf_op jit(solution)/shard_map/all_to_all | solution.py:328
  100.3 11.8 %collective-permute-start.19 = (f32[16,1024]{1,0:T(8,128)S(1)}, f32[16,1024]{1,0:T(8,128)S(1)}, u32[]{:S(2)}, u32[]{:S(2)}) collective-permute-start(f32[16,1024]{1,0:T(8,128)S(1)} %get-tuple-element.53), channel_id=1, source_target_pairs={{0,8},{8,0},{1,9},{9,1},{2,10},{10,2},{3,11},{11,3},{4,12},{12,4},... | collective-permute-start | bytes 196616 | tf_op jit(solution)/shard_map/ppermute | solution.py:39
  109.4 4.2 %collective-permute-start.20 = (f32[200]{0:T(256)S(1)}, f32[200]{0:T(256)S(1)}, u32[]{:S(2)}, u32[]{:S(2)}) collective-permute-start(f32[200]{0:T(256)S(1)} %bitcast.26), channel_id=1, source_target_pairs={{0,8},{8,0},{1,9},{9,1},{2,10},{10,2},{3,11},{11,3},{4,12},{12,4},... | collective-permute-start | bytes 2408 | tf_op jit(solution)/shard_map/ppermute | solution.py:39

commit v6 on v5

--- a/solution.py
+++ b/solution.py
@@ -228,7 +228,14 @@
     return value
 
 
-def densities_kernel(place_ref, keep_ref, got_ref, col_ref, real_ref, imag_ref):
+def densities_kernel(place_ref, keep_ref, got_ref, col_ref, x_ref, z_ref, phase_ref, real_ref, imag_ref, out_ref):
+    sums = jnp.sum(col_ref[:, 512:], axis=0, keepdims=True)
+    even = parity_sign(x_ref[...], z_ref[...]) > 0
+    sum_real = jnp.where(even, sums, 0.0)
+    sum_imag = jnp.where(even, 0.0, sums)
+    phase_real, phase_imag = phase_parts(phase_ref[...])
+    out_ref[0:1, :] = (phase_real * sum_real - phase_imag * sum_imag)[:, : out_ref.shape[1]]
+    out_ref[1:2, :] = (phase_real * sum_imag + phase_imag * sum_real)[:, : out_ref.shape[1]]
     first, core = place_ref[0], place_ref[1]
     row = lax.broadcasted_iota(jnp.int32, (8, 128), 0)
     lane = lax.broadcasted_iota(jnp.int32, (8, 128), 1)
@@ -249,21 +256,23 @@
                 imag_ref[here, cols] = jnp.where(j > i, mine, jnp.where(j < i, -across, 0.0))
 
 
-def densities(place, keep, got, arrived):
+def densities(place, keep, got, arrived, x, z, phase):
+    terms = pl.BlockSpec((1, 256), lambda i, p: (0, 0))
+    sums = (2, x.shape[1])
     rows = pl.BlockSpec((16, 1024), lambda i, p: (0, 0))
     out = pl.BlockSpec((16, 2048), lambda i, p: (0, 0))
     return pl.pallas_call(
         densities_kernel,
-        out_shape=[jax.ShapeDtypeStruct((16, 2048), jnp.float32)] * 2,
+        out_shape=[jax.ShapeDtypeStruct((16, 2048), jnp.float32)] * 2 + [jax.ShapeDtypeStruct(sums, jnp.float32)],
         grid_spec=pltpu.PrefetchScalarGridSpec(
             num_scalar_prefetch=1,
             grid=(1,),
-            in_specs=[rows, rows, pl.BlockSpec((64, 768), lambda i, p: (0, 0))],
-            out_specs=[out, out],
+            in_specs=[rows, rows, pl.BlockSpec((64, 768), lambda i, p: (0, 0)), terms, terms, terms],
+            out_specs=[out, out, pl.BlockSpec(sums, lambda i, p: (0, 0))],
         ),
         compiler_params=pltpu.CompilerParams(vmem_limit_bytes=4 * 2**20),
         name="densities",
-    )(place, keep, got, arrived)
+    )(place, keep, got, arrived, x, z, phase)
 
 
 def on_device(amplitudes, pauli_x, pauli_z, pauli_phase):
@@ -277,7 +286,8 @@
     send1 = send(CHUNKS[0])
     recv1 = swapped(send1)
     far = make(CHUNKS[0], waits=(send1,))
-    far0, far1 = far[:256] + recv1[:256], far[256:] + recv1[256:]
+    far0, far = lax.optimization_barrier((far[:256] + recv1[:256], far))
+    far1 = far[256:] + recv1[256:]
     via_left = round_ring(far0, 0, 1)
     via_right = round_ring(far1, 0, -1)
     send2 = send(CHUNKS[1], waits=(far0,))
@@ -321,23 +331,14 @@
     first = lax.axis_index(AX) * 16
     first_rows = (first - core * 128).astype(jnp.int32)
     parts = pauli_parts(jnp.stack([first_rows, core.astype(jnp.int32)]), both, pauli_x[None], pauli_z[None])
+    parts = parts + swapped(parts)
     blocks = both.reshape(2, 16, 64, 16).transpose(2, 0, 3, 1).reshape(64, 512)
     message = jnp.concatenate([blocks, jnp.broadcast_to(parts, (64, 256))], 1)
     keep = lax.dynamic_slice_in_dim(both, core * 16, 16, 0)
     got = swapped(lax.dynamic_slice_in_dim(both, (1 - core) * 16, 16, 0))
     arrived = lax.all_to_all(message, SAME_CORE, split_axis=0, concat_axis=0, tiled=True)
-    sums = arrived[:, 512:].sum(0)[:200]
-    sums = sums + swapped(sums)
     place = jnp.stack([first.astype(jnp.int32), core.astype(jnp.int32)])
-    density_real, density_imag = densities(place, keep, got, arrived)
-    even = parity_sign(pauli_x, pauli_z) > 0
-    sum_real = jnp.where(even, sums, 0.0)
-    sum_imag = jnp.where(even, 0.0, sums)
-    phase_real, phase_imag = phase_parts(pauli_phase)
-    expectations = jnp.stack(
-        [phase_real * sum_real - phase_imag * sum_imag, phase_real * sum_imag + phase_imag * sum_real], 0
-    )
-    return density_real, density_imag, expectations
+    return tuple(densities(place, keep, got, arrived, pauli_x[None], pauli_z[None], pauli_phase[None]))
 
 
 def solution(mesh):

time: 114 us -> 113 us (level)
  the two profiles are of different devices: /device:TPU:1 before, /device:TPU:8 now
where the time goes in v6:
time: 113 us; the launch traced here: 111 us
  waiting for transfers between devices  41.9 us (37%)
  starting transfers between devices  40.3 us (36%)
  Pallas kernels  23.7 us (21%)
  other arithmetic  2.98 us (3%)
  local copies, waits for them, and re-layouts  1.61 us (1%)
    ppermute x15, waiting for transfers between devices, round_ring(): return lax.ppermute(array, AX, ring_perm(turn, step))  30.6 us
    ppermute x15, starting transfers between devices, round_ring(): return lax.ppermute(array, AX, ring_perm(turn, step))  26.2 us
    pallas_call x8, Pallas kernels, chunk_part(): pl.pallas_call(functools.partial(chunk_kernel, halves=halves, own=own, wa...  17.1 us
    all_to_all x1, starting transfers between devices, on_device(): lax.all_to_all(message, SAME_CORE, split_axis=0, concat_axis=0, tiled=True)  11 us
    all_to_all x1, waiting for transfers between devices, on_device(): lax.all_to_all(message, SAME_CORE, split_axis=0, concat_axis=0, tiled=True)  8.98 us
    pallas_call x1, Pallas kernels, prepare(): pl.pallas_call(prepare_kernel, out_shape=[jax.ShapeDtypeStruct((2048, 153...  4.26 us
    ppermute x6, starting transfers between devices, swapped(): return lax.ppermute(array, CORE, [(0, 1), (1, 0)])  3 us
  transfers between devices with their start and end apart: 22, of which 13 were waited for; matrix products, arithmetic and copies ran while one was open for 3% of the time, Pallas kernels for 8%

profile of v6, /device:TPU:8, one launch (start us, length us, event | category | flops | bytes accessed | tf_op | source)
XLA Modules:
  0.0 111.3 jit_solution(16685829041921758798)
XLA Ops:
  0.7 4.3 %prepare.1 = (bf16[2048,1536]{1,0:T(8,128)(2,1)S(1)}, bf16[1024,1024]{1,0:T(8,128)(2,1)S(1)}, bf16[1024,1024]{1,0:T(8,128)(2,1)S(1)}) custom-call(s32[4]{0:T(128)S(1)} %pad_add_fusion.1.pos_ref, bf16[2,512,2048]{2,1,0:T(8,128)(2,1)} %amps_ref.1), custom_call_target="tpu_custom_call" | custom-call | flops 2000000000 | bytes 14680064 | tf_op jit(solution)/shard_map/prepare/pallas_call | solution.py:71
  5.0 2.1 %other.4.refs_0_ = f32[512,1024]{1,0:T(8,128)S(1)} custom-call(s32[4]{0:T(128)S(1)} %pad_add_fusion.1.pos_ref, bf16[2048,1536]{1,0:T(8,128)(2,1)S(1)} %get-tuple-element.20.lt_ref, bf16[1024,1024]{1,0:T(8,128)(2,1)S(1)} %get-tuple-element.22.w_ref), custom_call_target="tpu_custom_call" | custom-call | flops 1342177280 | bytes 8388608 | tf_op jit(solution)/shard_map/other/pallas_call | solution.py:146
  7.2 2.1 %own.4 = f32[512,1024]{1,0:T(8,128)S(1)} custom-call(s32[4]{0:T(128)S(1)} %pad_add_fusion.1.pos_ref, bf16[2048,1536]{1,0:T(8,128)(2,1)S(1)} %get-tuple-element.20.lt_ref, bf16[1024,1024]{1,0:T(8,128)(2,1)S(1)} %get-tuple-element.21.w_ref, f32[512,1024]{1,0:T(8,128)S(1)} %other.4.refs_0_), custom_call_target="tpu_custom_call" | custom-call | flops 1342177280 | bytes 8388608 | tf_op jit(solution)/shard_map/own/pallas_call | solution.py:146
  9.4 2.0 %collective-permute-done = f32[512,1024]{1,0:T(8,128)S(1)} collective-permute-done((f32[512,1024]{1,0:T(8,128)S(1)}, f32[512,1024]{1,0:T(8,128)S(1)}, u32[]{:S(2)}, u32[]{:S(2)}) %collective-permute-start) | collective-permute-done | bytes 2097184 | tf_op jit(solution)/shard_map/ppermute | solution.py:39
  11.4 0.2 slice_add_fusion.5.refs_0_
  11.6 2.1 %other.5.refs_0_ = f32[512,1024]{1,0:T(8,128)S(1)} custom-call(s32[4]{0:T(128)S(1)} %pad_add_fusion.1.pos_ref, bf16[2048,1536]{1,0:T(8,128)(2,1)S(1)} %get-tuple-element.20.lt_ref, bf16[1024,1024]{1,0:T(8,128)(2,1)S(1)} %get-tuple-element.22.w_ref, f32[256,1024]{1,0:T(8,128)S(1)} %slice_add_fusion.5.refs_0_), custom_call_target="tpu_custom_call" | custom-call | flops 1342177280 | bytes 8388608 | tf_op jit(solution)/shard_map/other/pallas_call | solution.py:146
  13.7 2.2 %own.5.refs_0_ = f32[512,1024]{1,0:T(8,128)S(1)} custom-call(s32[4]{0:T(128)S(1)} %pad_add_fusion.1.pos_ref, bf16[2048,1536]{1,0:T(8,128)(2,1)S(1)} %get-tuple-element.20.lt_ref, bf16[1024,1024]{1,0:T(8,128)(2,1)S(1)} %get-tuple-element.21.w_ref, f32[512,1024]{1,0:T(8,128)S(1)} %other.5.refs_0_), custom_call_target="tpu_custom_call" | custom-call | flops 1342177280 | bytes 8388608 | tf_op jit(solution)/shard_map/own/pallas_call | solution.py:146
  15.9 2.1 %other.6.refs_0_ = f32[512,1024]{1,0:T(8,128)S(1)} custom-call(s32[4]{0:T(128)S(1)} %pad_add_fusion.1.pos_ref, bf16[2048,1536]{1,0:T(8,128)(2,1)S(1)} %get-tuple-element.20.lt_ref, bf16[1024,1024]{1,0:T(8,128)(2,1)S(1)} %get-tuple-element.22.w_ref, f32[512,1024]{1,0:T(8,128)S(1)} %own.5.refs_0_), custom_call_target="tpu_custom_call" | custom-call | flops 1342177280 | bytes 8388608 | tf_op jit(solution)/shard_map/other/pallas_call | solution.py:146
  18.0 0.2 collective-permute-start.4
  18.2 0.4 collective-permute-start.2
  18.8 0.4 collective-permute-start.5
  19.2 1.7 %collective-permute-start.7 = (f32[256,1024]{1,0:T(8,128)S(1)}, f32[256,1024]{1,0:T(8,128)S(1)}, u32[]{:S(2)}, u32[]{:S(2)}) collective-permute-start(f32[256,1024]{1,0:T(8,128)S(1)} %slice_add_fusion.5.refs_0_), channel_id=1, source_target_pairs={{0,2},{8,9},{1,3},{9,24},{16,18},{24,25},{17,19},{25,8},{2,4},{10,... | collective-permute-start | bytes 3145736 | tf_op jit(solution)/shard_map/ppermute | solution.py:35
  20.9 2.1 %own.6.refs_0_ = f32[512,1024]{1,0:T(8,128)S(1)} custom-call(s32[4]{0:T(128)S(1)} %pad_add_fusion.1.pos_ref, bf16[2048,1536]{1,0:T(8,128)(2,1)S(1)} %get-tuple-element.20.lt_ref, bf16[1024,1024]{1,0:T(8,128)(2,1)S(1)} %get-tuple-element.21.w_ref, f32[512,1024]{1,0:T(8,128)S(1)} %other.6.refs_0_), custom_call_target="tpu_custom_call" | custom-call | flops 1342177280 | bytes 8388608 | tf_op jit(solution)/shard_map/own/pallas_call | solution.py:146
  23.0 2.1 %other.7.refs_0_ = f32[512,1024]{1,0:T(8,128)S(1)} custom-call(s32[4]{0:T(128)S(1)} %pad_add_fusion.1.pos_ref, bf16[2048,1536]{1,0:T(8,128)(2,1)S(1)} %get-tuple-element.20.lt_ref, bf16[1024,1024]{1,0:T(8,128)(2,1)S(1)} %get-tuple-element.22.w_ref, f32[512,1024]{1,0:T(8,128)S(1)} %own.6.refs_0_), custom_call_target="tpu_custom_call" | custom-call | flops 1342177280 | bytes 8388608 | tf_op jit(solution)/shard_map/other/pallas_call | solution.py:146
  25.2 2.0 %collective-permute-start.1 = (f32[512,1024]{1,0:T(8,128)S(1)}, f32[512,1024]{1,0:T(8,128)S(1)}, u32[]{:S(2)}, u32[]{:S(2)}) collective-permute-start(f32[512,1024]{1,0:T(8,128)S(1)} %other.7.refs_0_), channel_id=1, source_target_pairs={{0,8},{8,0},{1,9},{9,1},{2,10},{10,2},{3,11},{11,3},{4,12},{12,4},... | collective-permute-start | bytes 6291464 | tf_op jit(solution)/shard_map/ppermute | solution.py:39
  27.1 6.5 %collective-permute-done.5 = f32[256,1024]{1,0:T(8,128)S(1)} collective-permute-done((f32[256,1024]{1,0:T(8,128)S(1)}, f32[256,1024]{1,0:T(8,128)S(1)}, u32[]{:S(2)}, u32[]{:S(2)}) %collective-permute-start.5) | collective-permute-done | bytes 1048608 | tf_op jit(solution)/shard_map/ppermute | solution.py:35
  33.7 1.4 %collective-permute-done.7 = f32[256,1024]{1,0:T(8,128)S(1)} collective-permute-done((f32[256,1024]{1,0:T(8,128)S(1)}, f32[256,1024]{1,0:T(8,128)S(1)}, u32[]{:S(2)}, u32[]{:S(2)}) %collective-permute-start.7) | collective-permute-done | bytes 1048608 | tf_op jit(solution)/shard_map/ppermute | solution.py:35
  35.1 0.7 fusion
  35.8 0.7 collective-permute-start.8
  36.5 0.4 slice_add_fusion
  36.9 2.7 %collective-permute-start.9 = (f32[256,1024]{1,0:T(8,128)S(1)}, f32[256,1024]{1,0:T(8,128)S(1)}, u32[]{:S(2)}, u32[]{:S(2)}) collective-permute-start(f32[256,1024]{1,0:T(8,128)S(1)} %get-tuple-element.45), channel_id=1, source_target_pairs={{0,6},{8,25},{1,7},{9,8},{16,22},{24,9},{17,23},{25,24},{2,0},{10,... | collective-permute-start | bytes 3145736 | tf_op jit(solution)/shard_map/ppermute | solution.py:35
  39.7 3.2 %collective-permute-start.6 = (f32[256,1024]{1,0:T(8,128)S(1)}, f32[256,1024]{1,0:T(8,128)S(1)}, u32[]{:S(2)}, u32[]{:S(2)}) collective-permute-start(f32[256,1024]{1,0:T(8,128)S(1)} %get-tuple-element.48), channel_id=1, source_target_pairs={{0,6},{8,25},{1,7},{9,8},{16,22},{24,9},{17,23},{25,24},{2,0},{10,... | collective-permute-start | bytes 3145736 | tf_op jit(solution)/shard_map/ppermute | solution.py:35
  42.9 2.1 %own.7 = f32[512,1024]{1,0:T(8,128)S(1)} custom-call(s32[4]{0:T(128)S(1)} %pad_add_fusion.1.pos_ref, bf16[2048,1536]{1,0:T(8,128)(2,1)S(1)} %get-tuple-element.20.lt_ref, bf16[1024,1024]{1,0:T(8,128)(2,1)S(1)} %get-tuple-element.21.w_ref, f32[512,1024]{1,0:T(8,128)S(1)} %other.7.refs_0_), custom_call_target="tpu_custom_call" | custom-call | flops 1342177280 | bytes 8388608 | tf_op jit(solution)/shard_map/own/pallas_call | solution.py:146
  45.0 6.9 %collective-permute-done.8 = f32[256,1024]{1,0:T(8,128)S(1)} collective-permute-done((f32[256,1024]{1,0:T(8,128)S(1)}, f32[256,1024]{1,0:T(8,128)S(1)}, u32[]{:S(2)}, u32[]{:S(2)}) %collective-permute-start.8) | collective-permute-done | bytes 1048608 | tf_op jit(solution)/shard_map/ppermute | solution.py:35
  52.0 0.4 fusion.2
  52.4 2.0 %collective-permute-start.10 = (f32[64,1024]{1,0:T(8,128)S(1)}, f32[64,1024]{1,0:T(8,128)S(1)}, u32[]{:S(2)}, u32[]{:S(2)}) collective-permute-start(f32[64,1024]{1,0:T(8,128)S(1)} %get-tuple-element.31), channel_id=1, source_target_pairs={{0,1},{8,40},{1,16},{9,41},{16,17},{24,56},{17,0},{25,57},{2,3},{1... | collective-permute-start | bytes 786440 | tf_op jit(solution)/shard_map/ppermute | solution.py:35
  54.4 2.2 %collective-permute-start.15 = (f32[64,1024]{1,0:T(8,128)S(1)}, f32[64,1024]{1,0:T(8,128)S(1)}, u32[]{:S(2)}, u32[]{:S(2)}) collective-permute-start(f32[64,1024]{1,0:T(8,128)S(1)} %get-tuple-element.36), channel_id=1, source_target_pairs={{0,17},{8,104},{1,0},{9,105},{16,1},{24,120},{17,16},{25,121},{2,1... | collective-permute-start | bytes 786440 | tf_op jit(solution)/shard_map/ppermute | solution.py:35
  56.6 6.6 %collective-permute-done.6 = f32[256,1024]{1,0:T(8,128)S(1)} collective-permute-done((f32[256,1024]{1,0:T(8,128)S(1)}, f32[256,1024]{1,0:T(8,128)S(1)}, u32[]{:S(2)}, u32[]{:S(2)}) %collective-permute-start.6) | collective-permute-done | bytes 1048608 | tf_op jit(solution)/shard_map/ppermute | solution.py:35
  63.2 0.4 fusion.6
  63.7 4.1 %collective-permute-start.12 = (f32[64,1024]{1,0:T(8,128)S(1)}, f32[64,1024]{1,0:T(8,128)S(1)}, u32[]{:S(2)}, u32[]{:S(2)}) collective-permute-start(f32[64,1024]{1,0:T(8,128)S(1)} %get-tuple-element.32), channel_id=1, source_target_pairs={{0,17},{8,104},{1,0},{9,105},{16,1},{24,120},{17,16},{25,121},{2,1... | collective-permute-start | bytes 786440 | tf_op jit(solution)/shard_map/ppermute | solution.py:35
  68.1 3.3 %collective-permute-start.16 = (f32[64,1024]{1,0:T(8,128)S(1)}, f32[64,1024]{1,0:T(8,128)S(1)}, u32[]{:S(2)}, u32[]{:S(2)}) collective-permute-start(f32[64,1024]{1,0:T(8,128)S(1)} %add.189), channel_id=1, source_target_pairs={{0,17},{8,104},{1,0},{9,105},{16,1},{24,120},{17,16},{25,121},{2,1... | collective-permute-start | bytes 786440 | tf_op jit(solution)/shard_map/ppermute | solution.py:35
  71.3 0.3 collective-permute-done.12
  71.7 3.8 %collective-permute-done.11 = f32[64,1024]{1,0:T(8,128)S(1)} collective-permute-done((f32[64,1024]{1,0:T(8,128)S(1)}, f32[64,1024]{1,0:T(8,128)S(1)}, u32[]{:S(2)}, u32[]{:S(2)}) %collective-permute-start.11) | collective-permute-done | bytes 262176 | tf_op jit(solution)/shard_map/ppermute | solution.py:35
  75.6 1.6 %collective-permute-start.13 = (f32[32,1024]{1,0:T(8,128)S(1)}, f32[32,1024]{1,0:T(8,128)S(1)}, u32[]{:S(2)}, u32[]{:S(2)}) collective-permute-start(f32[32,1024]{1,0:T(8,128)S(1)} %slice.220), channel_id=1, source_target_pairs={{0,32},{8,10},{1,33},{9,11},{16,48},{24,26},{17,49},{25,27},{2,34}... | collective-permute-start | bytes 393224 | tf_op jit(solution)/shard_map/ppermute | solution.py:35
  77.1 1.2 %collective-permute-done.14 = f32[64,1024]{1,0:T(8,128)S(1)} collective-permute-done((f32[64,1024]{1,0:T(8,128)S(1)}, f32[64,1024]{1,0:T(8,128)S(1)}, u32[]{:S(2)}, u32[]{:S(2)}) %collective-permute-start.14) | collective-permute-done | bytes 262176 | tf_op jit(solution)/shard_map/ppermute | solution.py:35
  78.4 3.1 %collective-permute-start.17 = (f32[32,1024]{1,0:T(8,128)S(1)}, f32[32,1024]{1,0:T(8,128)S(1)}, u32[]{:S(2)}, u32[]{:S(2)}) collective-permute-start(f32[32,1024]{1,0:T(8,128)S(1)} %get-tuple-element.49), channel_id=1, source_target_pairs={{0,64},{8,12},{1,65},{9,13},{16,80},{24,28},{17,81},{25,29},{2,66}... | collective-permute-start | bytes 393224 | tf_op jit(solution)/shard_map/ppermute | solution.py:35
  81.5 1.1 %collective-permute-start.18 = (f32[32,1024]{1,0:T(8,128)S(1)}, f32[32,1024]{1,0:T(8,128)S(1)}, u32[]{:S(2)}, u32[]{:S(2)}) collective-permute-start(f32[32,1024]{1,0:T(8,128)S(1)} %get-tuple-element.50), channel_id=1, source_target_pairs={{0,96},{8,14},{1,97},{9,15},{16,112},{24,30},{17,113},{25,31},{2,9... | collective-permute-start | bytes 393224 | tf_op jit(solution)/shard_map/ppermute | solution.py:35
  82.7 2.2 %collective-permute-done.17 = f32[32,1024]{1,0:T(8,128)S(1)} collective-permute-done((f32[32,1024]{1,0:T(8,128)S(1)}, f32[32,1024]{1,0:T(8,128)S(1)}, u32[]{:S(2)}, u32[]{:S(2)}) %collective-permute-start.17) | collective-permute-done | bytes 131104 | tf_op jit(solution)/shard_map/ppermute | solution.py:35
  84.9 1.5 %collective-permute-done.18 = f32[32,1024]{1,0:T(8,128)S(1)} collective-permute-done((f32[32,1024]{1,0:T(8,128)S(1)}, f32[32,1024]{1,0:T(8,128)S(1)}, u32[]{:S(2)}, u32[]{:S(2)}) %collective-permute-start.18) | collective-permute-done | bytes 131104 | tf_op jit(solution)/shard_map/ppermute | solution.py:35
  86.5 0.8 pauli.1
  87.3 0.3 collective-permute-start.20
  87.6 0.4 reshape.14
  88.0 0.3 copy.10
  88.3 0.2 collective-permute-done.20
  88.7 0.8 copy.11
  89.6 11.0 %all-to-all-start = ((f32[64,1,768]{2,1,0:T(1,128)}), f32[64,1,768]{2,1,0:T(1,128)S(1)}, u32[]{:S(2)}, u32[]{:S(2)}) async-start(f32[64,1,768]{2,1,0:T(1,128)} %copy.11), calls=%async_computation | async-start | bytes 393216 | tf_op jit(solution)/shard_map/all_to_all | solution.py:339
  100.8 9.0 %all-to-all-done = f32[64,1,768]{2,1,0:T(1,128)S(1)} async-done(((f32[64,1,768]{2,1,0:T(1,128)}), f32[64,1,768]{2,1,0:T(1,128)S(1)}, u32[]{:S(2)}, u32[]{:S(2)}) %all-to-all-start) | async-done | bytes 196640 | tf_op jit(solution)/shard_map/all_to_all | solution.py:339
  109.8 1.5 %densities.1 = (f32[16,2048]{1,0:T(8,128)}, f32[16,2048]{1,0:T(8,128)}, f32[2,200]{1,0:T(2,128)}) custom-call(s32[2]{0:T(128)S(1)} %pad_add_fusion.place_ref, f32[16,1024]{1,0:T(8,128)S(1)} %get-tuple-element.52.keep_ref, f32[16,1024]{1,0:T(8,128)S(1)} %collective-permute-done.19.got_ref, f32[64,768]{1,0:T(8,128)S(1)} %bitcast.17, s32[1,200]{1,0:T(1,128)S(1)} %bitcast.19, ...), custom_call_target="tpu_custom_call" | custom-call | tf_op jit(solution)/shard_map/densities/pallas_call | solution.py:264
  (37 shorter events, 1.3 us)
Async XLA Ops:
  7.1 4.2 %collective-permute-start = (f32[512,1024]{1,0:T(8,128)S(1)}, f32[512,1024]{1,0:T(8,128)S(1)}, u32[]{:S(2)}, u32[]{:S(2)}) collective-permute-start(f32[512,1024]{1,0:T(8,128)S(1)} %other.4.refs_0_), channel_id=1, source_target_pairs={{0,8},{8,0},{1,9},{9,1},{2,10},{10,2},{3,11},{11,3},{4,12},{12,4},... | collective-permute-start | bytes 6291464 | tf_op jit(solution)/shard_map/ppermute | solution.py:39
  18.0 17.1 %collective-permute-start.4 = (f32[512,1024]{1,0:T(8,128)S(1)}, f32[512,1024]{1,0:T(8,128)S(1)}, u32[]{:S(2)}, u32[]{:S(2)}) collective-permute-start(f32[512,1024]{1,0:T(8,128)S(1)} %other.6.refs_0_), channel_id=1, source_target_pairs={{0,8},{8,0},{1,9},{9,1},{2,10},{10,2},{3,11},{11,3},{4,12},{12,4},... | collective-permute-start | bytes 6291464 | tf_op jit(solution)/shard_map/ppermute | solution.py:39
  18.2 18.2 %collective-permute-start.2 = (f32[512,1024]{1,0:T(8,128)S(1)}, f32[512,1024]{1,0:T(8,128)S(1)}, u32[]{:S(2)}, u32[]{:S(2)}) collective-permute-start(f32[512,1024]{1,0:T(8,128)S(1)} %other.5.refs_0_), channel_id=1, source_target_pairs={{0,8},{8,0},{1,9},{9,1},{2,10},{10,2},{3,11},{11,3},{4,12},{12,4},... | collective-permute-start | bytes 6291464 | tf_op jit(solution)/shard_map/ppermute | solution.py:39
  18.8 14.9 %collective-permute-start.5 = (f32[256,1024]{1,0:T(8,128)S(1)}, f32[256,1024]{1,0:T(8,128)S(1)}, u32[]{:S(2)}, u32[]{:S(2)}) collective-permute-start(f32[256,1024]{1,0:T(8,128)S(1)} %slice_add_fusion.2), channel_id=1, source_target_pairs={{0,6},{8,25},{1,7},{9,8},{16,22},{24,9},{17,23},{25,24},{2,0},{10,... | collective-permute-start | bytes 3145736 | tf_op jit(solution)/shard_map/ppermute | solution.py:35
  19.2 15.9 %collective-permute-start.7 = (f32[256,1024]{1,0:T(8,128)S(1)}, f32[256,1024]{1,0:T(8,128)S(1)}, u32[]{:S(2)}, u32[]{:S(2)}) collective-permute-start(f32[256,1024]{1,0:T(8,128)S(1)} %slice_add_fusion.5.refs_0_), channel_id=1, source_target_pairs={{0,2},{8,9},{1,3},{9,24},{16,18},{24,25},{17,19},{25,8},{2,4},{10,... | collective-permute-start | bytes 3145736 | tf_op jit(solution)/shard_map/ppermute | solution.py:35
  25.2 26.8 %collective-permute-start.1 = (f32[512,1024]{1,0:T(8,128)S(1)}, f32[512,1024]{1,0:T(8,128)S(1)}, u32[]{:S(2)}, u32[]{:S(2)}) collective-permute-start(f32[512,1024]{1,0:T(8,128)S(1)} %other.7.refs_0_), channel_id=1, source_target_pairs={{0,8},{8,0},{1,9},{9,1},{2,10},{10,2},{3,11},{11,3},{4,12},{12,4},... | collective-permute-start | bytes 6291464 | tf_op jit(solution)/shard_map/ppermute | solution.py:39
  35.8 16.1 %collective-permute-start.8 = (f32[256,1024]{1,0:T(8,128)S(1)}, f32[256,1024]{1,0:T(8,128)S(1)}, u32[]{:S(2)}, u32[]{:S(2)}) collective-permute-start(f32[256,1024]{1,0:T(8,128)S(1)} %get-tuple-element.47), channel_id=1, source_target_pairs={{0,2},{8,9},{1,3},{9,24},{16,18},{24,25},{17,19},{25,8},{2,4},{10,... | collective-permute-start | bytes 3145736 | tf_op jit(solution)/shard_map/ppermute | solution.py:35
  36.9 15.1 %collective-permute-start.9 = (f32[256,1024]{1,0:T(8,128)S(1)}, f32[256,1024]{1,0:T(8,128)S(1)}, u32[]{:S(2)}, u32[]{:S(2)}) collective-permute-start(f32[256,1024]{1,0:T(8,128)S(1)} %get-tuple-element.45), channel_id=1, source_target_pairs={{0,6},{8,25},{1,7},{9,8},{16,22},{24,9},{17,23},{25,24},{2,0},{10,... | collective-permute-start | bytes 3145736 | tf_op jit(solution)/shard_map/ppermute | solution.py:35
  39.7 23.6 %collective-permute-start.6 = (f32[256,1024]{1,0:T(8,128)S(1)}, f32[256,1024]{1,0:T(8,128)S(1)}, u32[]{:S(2)}, u32[]{:S(2)}) collective-permute-start(f32[256,1024]{1,0:T(8,128)S(1)} %get-tuple-element.48), channel_id=1, source_target_pairs={{0,6},{8,25},{1,7},{9,8},{16,22},{24,9},{17,23},{25,24},{2,0},{10,... | collective-permute-start | bytes 3145736 | tf_op jit(solution)/shard_map/ppermute | solution.py:35
  42.9 20.3 %collective-permute-start.3 = (f32[256,1024]{1,0:T(8,128)S(1)}, f32[256,1024]{1,0:T(8,128)S(1)}, u32[]{:S(2)}, u32[]{:S(2)}) collective-permute-start(f32[256,1024]{1,0:T(8,128)S(1)} %get-tuple-element.46), channel_id=1, source_target_pairs={{0,2},{8,9},{1,3},{9,24},{16,18},{24,25},{17,19},{25,8},{2,4},{10,... | collective-permute-start | bytes 3145736 | tf_op jit(solution)/shard_map/ppermute | solution.py:35
  52.4 15.3 %collective-permute-start.10 = (f32[64,1024]{1,0:T(8,128)S(1)}, f32[64,1024]{1,0:T(8,128)S(1)}, u32[]{:S(2)}, u32[]{:S(2)}) collective-permute-start(f32[64,1024]{1,0:T(8,128)S(1)} %get-tuple-element.31), channel_id=1, source_target_pairs={{0,1},{8,40},{1,16},{9,41},{16,17},{24,56},{17,0},{25,57},{2,3},{1... | collective-permute-start | bytes 786440 | tf_op jit(solution)/shard_map/ppermute | solution.py:35
  54.4 13.6 %collective-permute-start.15 = (f32[64,1024]{1,0:T(8,128)S(1)}, f32[64,1024]{1,0:T(8,128)S(1)}, u32[]{:S(2)}, u32[]{:S(2)}) collective-permute-start(f32[64,1024]{1,0:T(8,128)S(1)} %get-tuple-element.36), channel_id=1, source_target_pairs={{0,17},{8,104},{1,0},{9,105},{16,1},{24,120},{17,16},{25,121},{2,1... | collective-permute-start | bytes 786440 | tf_op jit(solution)/shard_map/ppermute | solution.py:35
  63.7 8.0 %collective-permute-start.12 = (f32[64,1024]{1,0:T(8,128)S(1)}, f32[64,1024]{1,0:T(8,128)S(1)}, u32[]{:S(2)}, u32[]{:S(2)}) collective-permute-start(f32[64,1024]{1,0:T(8,128)S(1)} %get-tuple-element.32), channel_id=1, source_target_pairs={{0,17},{8,104},{1,0},{9,105},{16,1},{24,120},{17,16},{25,121},{2,1... | collective-permute-start | bytes 786440 | tf_op jit(solution)/shard_map/ppermute | solution.py:35
  67.8 18.7 %copy-start = (s32[200]{0:T(256)S(1)}, s32[200]{0:T(256)}, u32[]{:S(2)}) copy-start(s32[200]{0:T(256)} %param.5) | copy-start | bytes 2404
  67.8 18.7 %copy-start.1 = (s32[200]{0:T(256)S(1)}, s32[200]{0:T(256)}, u32[]{:S(2)}) copy-start(s32[200]{0:T(256)} %param.6) | copy-start | bytes 2404
  67.8 7.7 %collective-permute-start.11 = (f32[64,1024]{1,0:T(8,128)S(1)}, f32[64,1024]{1,0:T(8,128)S(1)}, u32[]{:S(2)}, u32[]{:S(2)}) collective-permute-start(f32[64,1024]{1,0:T(8,128)S(1)} %add.184), channel_id=1, source_target_pairs={{0,1},{8,40},{1,16},{9,41},{16,17},{24,56},{17,0},{25,57},{2,3},{1... | collective-permute-start | bytes 786440 | tf_op jit(solution)/shard_map/ppermute | solution.py:35
  67.9 10.4 %collective-permute-start.14 = (f32[64,1024]{1,0:T(8,128)S(1)}, f32[64,1024]{1,0:T(8,128)S(1)}, u32[]{:S(2)}, u32[]{:S(2)}) collective-permute-start(f32[64,1024]{1,0:T(8,128)S(1)} %get-tuple-element.34), channel_id=1, source_target_pairs={{0,1},{8,40},{1,16},{9,41},{16,17},{24,56},{17,0},{25,57},{2,3},{1... | collective-permute-start | bytes 786440 | tf_op jit(solution)/shard_map/ppermute | solution.py:35
  68.1 10.2 %collective-permute-start.16 = (f32[64,1024]{1,0:T(8,128)S(1)}, f32[64,1024]{1,0:T(8,128)S(1)}, u32[]{:S(2)}, u32[]{:S(2)}) collective-permute-start(f32[64,1024]{1,0:T(8,128)S(1)} %add.189), channel_id=1, source_target_pairs={{0,17},{8,104},{1,0},{9,105},{16,1},{24,120},{17,16},{25,121},{2,1... | collective-permute-start | bytes 786440 | tf_op jit(solution)/shard_map/ppermute | solution.py:35
  75.6 7.1 %collective-permute-start.13 = (f32[32,1024]{1,0:T(8,128)S(1)}, f32[32,1024]{1,0:T(8,128)S(1)}, u32[]{:S(2)}, u32[]{:S(2)}) collective-permute-start(f32[32,1024]{1,0:T(8,128)S(1)} %slice.220), channel_id=1, source_target_pairs={{0,32},{8,10},{1,33},{9,11},{16,48},{24,26},{17,49},{25,27},{2,34}... | collective-permute-start | bytes 393224 | tf_op jit(solution)/shard_map/ppermute | solution.py:35
  78.4 6.6 %collective-permute-start.17 = (f32[32,1024]{1,0:T(8,128)S(1)}, f32[32,1024]{1,0:T(8,128)S(1)}, u32[]{:S(2)}, u32[]{:S(2)}) collective-permute-start(f32[32,1024]{1,0:T(8,128)S(1)} %get-tuple-element.49), channel_id=1, source_target_pairs={{0,64},{8,12},{1,65},{9,13},{16,80},{24,28},{17,81},{25,29},{2,66}... | collective-permute-start | bytes 393224 | tf_op jit(solution)/shard_map/ppermute | solution.py:35
  81.5 5.0 %collective-permute-start.18 = (f32[32,1024]{1,0:T(8,128)S(1)}, f32[32,1024]{1,0:T(8,128)S(1)}, u32[]{:S(2)}, u32[]{:S(2)}) collective-permute-start(f32[32,1024]{1,0:T(8,128)S(1)} %get-tuple-element.50), channel_id=1, source_target_pairs={{0,96},{8,14},{1,97},{9,15},{16,112},{24,30},{17,113},{25,31},{2,9... | collective-permute-start | bytes 393224 | tf_op jit(solution)/shard_map/ppermute | solution.py:35
  87.3 1.2 %collective-permute-start.20 = (f32[1,256]{1,0:T(1,128)S(1)}, f32[1,256]{1,0:T(1,128)S(1)}, u32[]{:S(2)}, u32[]{:S(2)}) collective-permute-start(f32[1,256]{1,0:T(1,128)S(1)} %pauli.1), channel_id=1, source_target_pairs={{0,8},{8,0},{1,9},{9,1},{2,10},{10,2},{3,11},{11,3},{4,12},{12,4},... | collective-permute-start | bytes 3080 | tf_op jit(solution)/shard_map/ppermute | solution.py:39
  87.9 21.9 %copy-start.2 = (s32[200]{0:T(256)S(1)}, s32[200]{0:T(256)}, u32[]{:S(2)}) copy-start(s32[200]{0:T(256)} %param.7) | copy-start | bytes 2404
  89.6 20.2 %all-to-all-start = ((f32[64,1,768]{2,1,0:T(1,128)}), f32[64,1,768]{2,1,0:T(1,128)S(1)}, u32[]{:S(2)}, u32[]{:S(2)}) async-start(f32[64,1,768]{2,1,0:T(1,128)} %copy.11), calls=%async_computation | async-start | bytes 393216 | tf_op jit(solution)/shard_map/all_to_all | solution.py:339
  100.6 9.2 %collective-permute-start.19 = (f32[16,1024]{1,0:T(8,128)S(1)}, f32[16,1024]{1,0:T(8,128)S(1)}, u32[]{:S(2)}, u32[]{:S(2)}) collective-permute-start(f32[16,1024]{1,0:T(8,128)S(1)} %get-tuple-element.51), channel_id=1, source_target_pairs={{0,8},{8,0},{1,9},{9,1},{2,10},{10,2},{3,11},{11,3},{4,12},{12,4},... | collective-permute-start | bytes 196616 | tf_op jit(solution)/shard_map/ppermute | solution.py:39
